TPU v7x, 32 devices: a whole 2x2x4 slice. The times are simulated.
32 devices in a mesh: dp: 4 (over x, y), tp: 8 (over z, core).
Axes of the slice: x: 2, y: 2, z: 4, core: 2. Of those that a mesh axis runs over, the one named last changes fastest.
Arguments:
- hidden: bfloat16 [4, 6144, 1024], P('dp'), parts along dimension 0
- norm_w: bfloat16 [2, 1024], replicated
- w_z: bfloat16 [2, 1024, 2048], P(None, None, 'tp')
- w_x: bfloat16 [2, 1024, 2048], P(None, None, 'tp')
- w_bc: bfloat16 [2, 1024, 256], replicated
- w_dt: bfloat16 [2, 1024, 32], P(None, None, 'tp')
- conv_x: bfloat16 [2, 4, 2048], P(None, None, 'tp')
- conv_bc: bfloat16 [2, 4, 256], replicated
- bias_x: bfloat16 [2, 2048], P(None, 'tp')
- bias_bc: bfloat16 [2, 256], replicated
- dt_bias: float32 [2, 32], P(None, 'tp')
- a_log: float32 [2, 32], P(None, 'tp')
- d_skip: float32 [2, 32], P(None, 'tp')
- gate_w: bfloat16 [2, 2048], P(None, 'tp')
- w_out: bfloat16 [2, 2048, 1024], P(None, 'tp')
Outputs:
- output: bfloat16 [4, 6144, 1024], P('dp'), parts along dimension 0
There are 4 independent parts. A program takes and returns all parts, laid end to end along the dimension named above; an argument that names none is the same for every part.
All inputs are finite; a program needn't handle non-finite values.
Results may differ from a plain program's by a relative error of at most 0.013727.
Values sent between devices are 32-bit elements.
A program may use at most 1 GiB of HBM per device.

v0:
```python
import jax
import jax.numpy as jnp
from jax import lax
from jax.sharding import PartitionSpec as P

EPSILON = 1e-5
CONV_WIDTH = 4
BLOCK_LEN = 256
FULL_PRECISION = lax.Precision.HIGHEST


def causal_conv(seq_in, kernel, conv_bias):
    n_steps = seq_in.shape[1]
    padded = jnp.pad(seq_in, ((0, 0), (CONV_WIDTH - 1, 0), (0, 0)))
    conv_sum = conv_bias.astype(jnp.float32)
    for tap_index in range(CONV_WIDTH):
        conv_sum = conv_sum + padded[:, tap_index:tap_index + n_steps, :].astype(jnp.float32) * kernel[tap_index].astype(jnp.float32)
    return conv_sum


def ssd_blocks(x_heads, dt_val, a_vals, b_in, c_in):
    n_batch, n_steps, n_heads, head_width = x_heads.shape
    n_state = b_in.shape[-1]
    n_blocks = n_steps // BLOCK_LEN
    x_blocks = x_heads.reshape(n_batch, n_blocks, BLOCK_LEN, n_heads, head_width)
    dt_blocks = dt_val.reshape(n_batch, n_blocks, BLOCK_LEN, n_heads)
    b_blocks = b_in.reshape(n_batch, n_blocks, BLOCK_LEN, n_state)
    c_blocks = c_in.reshape(n_batch, n_blocks, BLOCK_LEN, n_state)
    a_cum = jnp.cumsum(a_vals.reshape(n_batch, n_blocks, BLOCK_LEN, n_heads), axis=2)
    a_cum_t = jnp.swapaxes(a_cum, 2, 3)
    seg_sum = a_cum_t[..., :, None] - a_cum_t[..., None, :]
    step_ids = jnp.arange(BLOCK_LEN)
    lower_tri = step_ids[:, None] >= step_ids[None, :]
    c_dot_b = jnp.einsum('bcin,bcjn->bcij', c_blocks, b_blocks, precision=FULL_PRECISION)
    mix_mat = jnp.where(lower_tri, jnp.exp(jnp.minimum(seg_sum, 0.0)), 0.0) * c_dot_b[:, :, None]
    x_dt = x_blocks * dt_blocks[..., None]
    y_in = jnp.einsum('bchij,bcjhp->bcihp', mix_mat, x_dt, precision=FULL_PRECISION)
    a_last = a_cum[:, :, -1, :]
    tail_decay = jnp.exp(a_last[:, :, None, :] - a_cum)
    block_states = jnp.einsum('bcjn,bcjhp->bchpn', b_blocks, x_dt * tail_decay[..., None], precision=FULL_PRECISION)
    block_ends = jnp.swapaxes(jnp.cumsum(a_last, axis=1), 1, 2)
    block_starts = block_ends - jnp.swapaxes(a_last, 1, 2)
    block_ids = jnp.arange(n_blocks)
    earlier = block_ids[:, None] > block_ids[None, :]
    carry_mat = jnp.where(earlier, jnp.exp(jnp.minimum(block_starts[..., :, None] - block_ends[..., None, :], 0.0)), 0.0)
    s_in = jnp.einsum('bhck,bkhpn->bchpn', carry_mat, block_states, precision=FULL_PRECISION)
    y_st = jnp.einsum('bcin,bchpn->bcihp', c_blocks, s_in, precision=FULL_PRECISION) * jnp.exp(a_cum)[..., None]
    return (y_in + y_st).reshape(n_batch, n_steps, n_heads, head_width)


def mixer_layer(current, norm_w, w_z, w_x, w_bc, w_dt, conv_x, conv_bc, bias_x, bias_bc, dt_bias, a_log, d_skip, gate_w, w_out, inner_width):
    n_batch = current.shape[0]
    n_steps = current.shape[1]
    n_heads = dt_bias.shape[0]
    local_width = w_x.shape[-1]
    state_dim = w_bc.shape[-1] // 2
    residual = current.astype(jnp.float32)
    normed = (residual * lax.rsqrt(jnp.mean(residual * residual, axis=-1, keepdims=True) + EPSILON) * norm_w.astype(jnp.float32)).astype(jnp.bfloat16)
    gate_z = jnp.einsum('btd,de->bte', normed, w_z, preferred_element_type=jnp.float32).astype(jnp.bfloat16)
    x_pre = jnp.einsum('btd,de->bte', normed, w_x, preferred_element_type=jnp.float32).astype(jnp.bfloat16)
    bc_pre = jnp.einsum('btd,de->bte', normed, w_bc, preferred_element_type=jnp.float32).astype(jnp.bfloat16)
    dt_pre = jnp.einsum('btd,de->bte', normed, w_dt, preferred_element_type=jnp.float32).astype(jnp.bfloat16)
    x_act = jax.nn.silu(causal_conv(x_pre, conv_x, bias_x))
    bc_act = jax.nn.silu(causal_conv(bc_pre, conv_bc, bias_bc))
    dt_val = jax.nn.softplus(dt_pre.astype(jnp.float32) + dt_bias)
    a_vals = -dt_val * jnp.exp(a_log)
    x_heads = x_act.reshape(n_batch, n_steps, n_heads, local_width // n_heads)
    y_heads = ssd_blocks(x_heads, dt_val, a_vals, bc_act[..., :state_dim], bc_act[..., state_dim:]) + d_skip[:, None] * x_heads
    gated_v = y_heads.reshape(n_batch, n_steps, local_width) * jax.nn.silu(gate_z.astype(jnp.float32))
    part_sq = jnp.sum(gated_v * gated_v, axis=-1, keepdims=True)
    total_sq = lax.psum(part_sq, 'tp')
    normed_y = (gated_v * lax.rsqrt(total_sq / inner_width + EPSILON) * gate_w.astype(jnp.float32)).astype(jnp.bfloat16)
    part_out = jnp.einsum('bte,ed->btd', normed_y, w_out, preferred_element_type=jnp.float32)
    full_out = lax.psum(part_out, 'tp')
    return (residual + full_out).astype(jnp.bfloat16)


def solution(mesh):
    tp_size = mesh.shape['tp']
    rep_spec = P()
    col_spec = P(None, None, 'tp')
    vec_spec = P(None, 'tp')
    in_specs = (P('dp'), rep_spec, col_spec, col_spec, rep_spec, col_spec, col_spec, rep_spec, vec_spec, rep_spec, vec_spec, vec_spec, vec_spec, vec_spec, P(None, 'tp', None))

    def device_forward(hidden, norm_w, w_z, w_x, w_bc, w_dt, conv_x, conv_bc, bias_x, bias_bc, dt_bias, a_log, d_skip, gate_w, w_out):
        inner_width = w_x.shape[-1] * tp_size
        current = hidden
        for layer_idx in range(norm_w.shape[0]):
            current = mixer_layer(current, norm_w[layer_idx], w_z[layer_idx], w_x[layer_idx], w_bc[layer_idx], w_dt[layer_idx], conv_x[layer_idx], conv_bc[layer_idx], bias_x[layer_idx], bias_bc[layer_idx], dt_bias[layer_idx], a_log[layer_idx], d_skip[layer_idx], gate_w[layer_idx], w_out[layer_idx], inner_width)
        return current

    return jax.shard_map(device_forward, mesh=mesh, in_specs=in_specs, out_specs=P('dp'), check_vma=False)
```

profile of v0, /device:TPU:0, one launch (start us, length us, event | category | flops | bytes accessed | tf_op | source)
XLA Modules:
  0.0 1443.3 jit_solution(12512921526593057363)
XLA Ops:
  6.5 0.6 iota_compare_fusion
  7.2 0.8 slice_convert_fusion
  8.0 7.1 fusion
  15.6 7.9 fusion.21
  23.6 3.4 negate_multiply_fusion.1
  27.0 1.3 copy-done.1
  28.5 2.3 reduce-window.14
  32.1 0.7 mul.532
  37.0 0.7 copy.56
  37.6 0.6 copy.57
  38.6 8.0 convolution_convert_fusion.4
  46.6 4.4 divide_multiply_fusion.2
  51.1 2.1 fusion.124
  53.2 1.2 slice-done.2
  54.7 3.7 convolution_convert_fusion.5
  58.5 5.9 divide_multiply_fusion.3
  64.4 6.6 copy.40
  70.9 5.4 copy.108
  76.3 5.5 broadcast_multiply_fusion.2
  81.8 11.0 fusion.48
  92.8 6.1 fusion.125
  98.9 4.6 fusion.68
  103.5 31.3 %fusion.14 = f32[24,4,64,256]{3,2,1,0:T(8,128)S(1)} fusion(f32[24,256,256]{2,1,0:T(8,128)S(1)} %fusion.125, f32[24,4,256]{2,1,0:T(4,128)S(1)} %copy.45, pred[256,256]{1,0:T(8,128)(4,1)S(1)} %copy-done.10, f32[24,256,4,64]{1,0,3,2:T(8,128)} %get-tuple-element.12), kind=kOutput, calls=%fused_computation.20 | convolution fusion | flops 4857004032 | bytes 19038208 | tf_op jit(solution)/shard_map/bchij,bcjhp->bcihp/dot_general | solution.py:37
  134.8 7.5 bitcast_add_fusion.1
  142.3 11.9 copy.97
  154.2 12.7 reshape.666
  166.9 15.6 %multiply_reduce_fusion.1 = (f32[6144]{0:T(1024)S(1)}, f32[6144,256]{1,0:T(8,128)}) fusion(bf16[6144,1024]{1,0:T(8,128)(2,1)} %copy-done.1, bf16[2,1024,256]{2,1,0:T(8,128)(2,1)S(1)} %copy-done.45, f32[6144,256]{1,0:T(8,128)} %reshape.666, f32[1,6144,256]{2,1,0:T(8,128)} %divide_multiply_fusion.3, f32[256]{0:T(256)S(1)} %copy-done.38), kind=kOutput, calls=%fused_computation.85 | convolution fusion | flops 3238520832 | bytes 32007168 | tf_op jit(solution)/shard_map/btd,de->bte/dot_general | solution.py:59
  182.6 30.3 %psum.28 = f32[1,6144,1]{1,2,0:T(1,128)S(1)} all-reduce(f32[1,6144,1]{1,2,0:T(1,128)S(1)} %bitcast.330), channel_id=1, replica_groups=mesh['dp'=4,'tp'=8] {'tp'}, use_global_device_ids=true, to_apply=%region_5.6 | all-reduce | flops 6144 | bytes 49152 | tf_op jit(solution)/shard_map/psum | solution.py:71
  212.9 12.0 convolution_bitcast_fusion.1
  225.7 0.7 mul.600
  226.4 487.2 %all-reduce.7.cloned.1.call-done = f32[1,6144,1024]{2,1,0:T(8,128)} async-done(((f32[1,6144,1024]{2,1,0:T(8,128)}), f32[1,6144,1024]{2,1,0:T(8,128)}) %all-reduce.7.cloned.1.call-update) | async-done | bytes 25165840 | tf_op jit(solution)/shard_map/psum | solution.py:74
  713.6 13.1 fusion.4
  726.7 3.3 fusion.20
  730.1 1.1 copy-done
  731.2 3.4 negate_multiply_fusion
  734.6 1.4 copy-done.2
  736.1 2.3 reduce-window.16
  738.6 0.7 copy.105
  739.3 0.7 copy.66
  740.2 8.2 convolution_convert_fusion.1
  748.7 4.9 convolution_convert_fusion.2
  753.8 0.7 reshape.628
  754.6 0.9 reduce_window_sum.75
  755.5 0.7 copy.67
  756.2 1.0 broadcast.247.clone
  758.3 5.5 divide_multiply_fusion
  763.9 2.1 fusion.123
  766.0 0.9 copy-done.5
  766.9 5.7 divide_multiply_fusion.1
  772.6 6.6 copy.62
  779.1 5.4 copy.111
  784.5 5.5 broadcast_multiply_fusion
  790.0 10.9 fusion.46
  801.0 6.1 fusion.126
  807.1 4.6 fusion.71
  811.6 31.1 %fusion.8 = f32[24,4,64,256]{3,2,1,0:T(8,128)S(1)} fusion(f32[24,256,256]{2,1,0:T(8,128)S(1)} %fusion.126, f32[24,4,256]{2,1,0:T(4,128)S(1)} %copy-done.9, pred[256,256]{1,0:T(8,128)(4,1)S(1)} %copy-done.11, f32[24,256,4,64]{1,0,3,2:T(8,128)} %get-tuple-element.6), kind=kOutput, calls=%fused_computation.14 | convolution fusion | flops 4857004032 | bytes 19038208 | tf_op jit(solution)/shard_map/bchij,bcjhp->bcihp/dot_general | solution.py:37
  842.8 7.5 bitcast_add_fusion
  850.3 11.9 copy.99
  862.2 12.8 reshape.667
  875.0 15.6 %multiply_reduce_fusion = (f32[6144]{0:T(1024)S(1)}, f32[6144,256]{1,0:T(8,128)}) fusion(bf16[6144,1024]{1,0:T(8,128)(2,1)} %copy-done.2, bf16[2,1024,256]{2,1,0:T(8,128)(2,1)S(1)} %copy-done.46, f32[6144,256]{1,0:T(8,128)} %reshape.667, f32[1,6144,256]{2,1,0:T(8,128)} %divide_multiply_fusion.1, f32[256]{0:T(256)S(1)} %copy-done.37), kind=kOutput, calls=%fused_computation.81 | convolution fusion | flops 3238520832 | bytes 32007168 | tf_op jit(solution)/shard_map/btd,de->bte/dot_general | solution.py:59
  890.6 27.8 %psum.30 = f32[1,6144,1]{1,2,0:T(1,128)S(1)} all-reduce(f32[1,6144,1]{1,2,0:T(1,128)S(1)} %bitcast.331), channel_id=1, replica_groups=mesh['dp'=4,'tp'=8] {'tp'}, use_global_device_ids=true, to_apply=%region_12.13 | all-reduce | flops 6144 | bytes 49152 | tf_op jit(solution)/shard_map/psum | solution.py:71
  918.4 12.0 convolution_bitcast_fusion
  930.5 488.5 %all-reduce.9.cloned.1.call-done = f32[1,6144,1024]{2,1,0:T(8,128)} async-done(((f32[1,6144,1024]{2,1,0:T(8,128)}), f32[1,6144,1024]{2,1,0:T(8,128)}) %all-reduce.9.cloned.1.call-update) | async-done | bytes 25165840 | tf_op jit(solution)/shard_map/psum | solution.py:74
  1419.0 17.2 %fusion.7 = bf16[1,6144,1024]{2,1,0:T(8,128)(2,1)} fusion(f32[1,6144,1024]{2,1,0:T(8,128)} %all-reduce.9.cloned.1.call-done, bf16[1,6144,1024]{2,1,0:T(8,128)(2,1)} %copy-done), kind=kLoop, calls=%fused_computation.13 | loop fusion | flops 18874368 | bytes 50331648 | tf_op jit(solution)/shard_map/convert_element_type | solution.py:75
  (171 shorter events, 9.7 us)
Async XLA Ops:
  6.5 707.1 %all-reduce.7.cloned.1.call-start = ((), (), s32[]{:S(2)}) async-start(), calls=%async_computation | async-start | bytes 50331648 | tf_op jit(solution)/shard_map/psum | solution.py:74
  8.0 7.2 copy-start.40
  8.0 7.2 copy-start.41
  15.6 7.9 copy-start.12
  23.5 4.8 copy-start.1
  23.6 7.8 copy-start.39
  23.6 9.2 copy-start.33
  23.6 9.7 copy-start.34
  23.6 10.3 copy-start.35
  23.6 10.9 copy-start.14
  23.6 11.5 copy-start.15
  23.6 15.0 %copy-start.42 = (bf16[2,1024,256]{2,1,0:T(8,128)(2,1)S(1)}, bf16[2,1024,256]{2,1,0:T(8,128)(2,1)}, u32[]{:S(2)}) copy-start(bf16[2,1024,256]{2,1,0:T(8,128)(2,1)} %param.19) | copy-start | bytes 3145732
  46.6 6.6 slice-start
  46.6 6.6 slice-start.1
  51.0 3.3 slice-start.2
  51.1 3.6 copy-start.43
  54.7 3.8 copy-start.27
  54.7 3.8 copy-start.28
  54.7 3.8 copy-start.29
  54.7 3.8 copy-start.30
  54.7 3.8 copy-start.32
  76.3 5.5 copy-start.4
  92.8 6.1 copy-start.18
  92.8 6.1 copy-start.19
  98.9 4.6 copy-start.10
  154.2 12.7 copy-start.38
  154.2 12.7 copy-start.45
  166.9 46.0 %copy-start.6 = (bf16[2,256,1024]{2,1,0:T(8,128)(2,1)S(1)}, bf16[2,256,1024]{2,1,0:T(8,128)(2,1)}, u32[]{:S(2)}) copy-start(bf16[2,256,1024]{2,1,0:T(8,128)(2,1)} %param.29) | copy-start | bytes 3145732
  225.0 0.7 copy-start.36
  225.0 1194.0 %all-reduce.9.cloned.1.call-start = ((), (), s32[]{:S(2)}) async-start(), calls=%async_computation.1 | async-start | bytes 50331648 | tf_op jit(solution)/shard_map/psum | solution.py:74
  726.7 4.5 copy-start
  726.7 4.4 copy-start.13
  726.7 4.4 copy-start.17
  731.2 4.8 copy-start.2
  740.0 8.4 slice-start.3
  740.2 8.3 slice-start.4
  740.2 8.3 slice-start.5
  740.2 8.5 copy-start.44
  748.7 4.9 copy-start.8
  748.7 9.6 copy-start.24
  748.7 9.6 copy-start.25
  748.7 9.6 copy-start.26
  763.8 3.0 copy-start.5
  763.8 3.0 copy-start.20
  763.8 3.0 copy-start.21
  763.9 3.0 copy-start.22
  763.9 3.0 copy-start.23
  763.9 3.0 copy-start.31
  784.5 5.5 copy-start.3
  807.0 4.6 copy-start.9
  807.0 4.6 copy-start.11
  862.2 12.8 copy-start.37
  862.2 12.8 copy-start.46
  875.0 43.5 %copy-start.7 = (bf16[2,256,1024]{2,1,0:T(8,128)(2,1)S(1)}, bf16[2,256,1024]{2,1,0:T(8,128)(2,1)}, u32[]{:S(2)}) copy-start(bf16[2,256,1024]{2,1,0:T(8,128)(2,1)} %param.29) | copy-start | bytes 3145732
  875.0 43.5 %copy-start.16 = (f32[1,256]{1,0:T(1,128)S(1)}, f32[1,256]{1,0:T(1,128)}, u32[]{:S(2)}) copy-start(f32[1,256]{1,0:T(1,128)} %get-tuple-element.37) | copy-start | bytes 3076
Sparse Core Ops, SparseCore 0:
  225.1 488.4 all-reduce.6
  930.6 488.3 all-reduce.8
where the time goes:
time: 1450 us; the launch traced here: 1440 us
  waiting for transfers between devices  976 us (67%)
  matrix products  208 us (14%)
  local copies, waits for them, and re-layouts  95.3 us (7%)
  other arithmetic  92 us (6%)
  blocking collectives  58.1 us (4%)
  between operations  14.6 us (1%)
    psum x2, waiting for transfers between devices, mixer_layer(): full_out = lax.psum(part_out, 'tp')  976 us
    dot_general x2, matrix products, ssd_blocks(): jnp.einsum('bchij,bcjhp->bcihp', mix_mat, x_dt, precision=FULL_PRECISION)  62.4 us
    psum x2, blocking collectives, mixer_layer(): total_sq = lax.psum(part_sq, 'tp')  58.1 us
    reshape x4, local copies, waits for them, and re-layouts, ssd_blocks(): return (y_in + y_st).reshape(n_batch, n_steps, n_heads, head_width)  49.3 us
    dot_general x2, matrix products, mixer_layer(): jnp.einsum('btd,de->bte', normed, w_z, preferred_element_type=jnp.float32)  31.3 us
  transfers between devices with their start and end apart: 2, of which 2 were waited for; matrix products, arithmetic and copies ran while one was open for 0% of the time, Pallas kernels for 0%

commit v1 on v0

v1 whole, which is shorter than its diff:
```python
import functools
import jax
import jax.numpy as jnp
from jax import lax
from jax.experimental import pallas as pl
from jax.experimental.pallas import tpu as pltpu

EPS = 1e-5
LOG2E = 1.4426950408889634
HI = lax.Precision.HIGHEST
F32 = jnp.float32
BF16 = jnp.bfloat16
BLK = 128


def silu(v):
    half = 0.5 * v
    return half + half * jnp.tanh(half)


def split3(v):
    a = v.astype(BF16)
    r = v - a.astype(F32)
    b = r.astype(BF16)
    c = (r - b.astype(F32)).astype(BF16)
    return a, b, c


def rms(u, nw):
    return (u * lax.rsqrt(jnp.mean(u * u, axis=-1, keepdims=True) + EPS) * nw).astype(BF16)


def dot(a, b, prec=None):
    return jnp.dot(a, b, preferred_element_type=F32, precision=prec)


def dott(a, b, prec=None):
    return lax.dot_general(a, b, (((1,), (1,)), ((), ())), preferred_element_type=F32, precision=prec)


def load_cols(wf_ref, wb_ref, n_dp, n_tp, rows, cols):
    for d in range(n_dp):
        for t in range(n_tp):
            wb_ref[d * rows:(d + 1) * rows, t * cols:(t + 1) * cols] = wf_ref[d * n_tp + t].astype(BF16)


def p1_body(off_ref, u_ref, halo_ref, nw_ref, wf_ref, sm_ref, wbc_ref, cbc_ref, bbc_ref, e3_ref,
            y_ref, c_ref, ac_ref, send_ref, wxb, wdt, cst, st, xpad, qpad, aoff, *, geom):
    n_dp, n_tp, hd, width, heads = geom
    i = pl.program_id(0)
    nst = 128
    pc = width // n_tp
    hp = heads // n_tp

    @pl.when(i == 0)
    def _():
        load_cols(wf_ref, wxb, n_dp, n_tp, wxb.shape[0] // n_dp, pc)
        kc = wxb.shape[0] // pc
        for t in range(n_tp):
            for k in range(hp):
                for c in range(kc):
                    wdt[hp * t + k:hp * t + k + 1, c * pc:(c + 1) * pc] = sm_ref[t, 16 + kc * k + c:17 + kc * k + c, :].astype(BF16)
            cst[hp * t:hp * (t + 1), :] = sm_ref[t, 8:8 + hp, :]
            cst[heads + hp * t:heads + hp * (t + 1), :] = sm_ref[t, 12:12 + hp, :]
        st[...] = jnp.zeros_like(st)
        aoff[...] = jnp.zeros_like(aoff)
        hh = rms(halo_ref[...], nw_ref[...])
        xpad[0:8, :] = dot(hh, wxb[...]).astype(BF16).astype(F32)
        qpad[0:8, :] = dot(hh, wbc_ref[...]).astype(BF16).astype(F32)

    @pl.when(i > 0)
    def _():
        xpad[0:8, :] = xpad[BLK:BLK + 8, :]
        qpad[0:8, :] = qpad[BLK:BLK + 8, :]

    h = rms(u_ref[...].astype(F32), nw_ref[...])
    xpad[8:8 + BLK, :] = dot(h, wxb[...]).astype(BF16).astype(F32)
    qpad[8:8 + BLK, :] = dot(h, wbc_ref[...]).astype(BF16).astype(F32)
    rT = dott(wdt[...], h).astype(BF16).astype(F32)

    acc = bbc_ref[...]
    for j in range(4):
        acc = acc + qpad[5 + j:5 + j + BLK, :] * cbc_ref[j:j + 1, :]
    bc = silu(acc)
    bmat, cmat = bc[:, :nst], bc[:, nst:]
    c_ref[...] = cmat

    pre = rT + cst[0:heads, 0:BLK]
    dtT = jnp.maximum(pre, 0.0) + jnp.log1p(jnp.exp(-jnp.abs(pre)))
    aT = dtT * cst[heads:2 * heads, 0:BLK]
    ri = lax.broadcasted_iota(jnp.int32, (BLK, BLK), 0)
    ci = lax.broadcasted_iota(jnp.int32, (BLK, BLK), 1)
    upper = jnp.where(ri <= ci, 1.0, 0.0).astype(F32)
    acT = dot(aT, upper, HI)
    alast = acT[:, BLK - 1:BLK]
    ac = acT.T
    wT = dtT * jnp.exp2(alast - acT)
    w3 = jnp.concatenate(split3(wT), axis=0)
    e3 = jnp.concatenate(split3(jnp.exp2(acT)), axis=0)
    d3 = jnp.concatenate(split3(jnp.broadcast_to(jnp.exp2(alast), (heads, BLK))), axis=0)
    ac_ref[...] = acT + aoff[:, 0:1]
    aoff[...] = aoff[...] + alast

    cbm = jnp.where(ri >= ci, dott(cmat, bmat, HI), 0.0)
    bT = bmat.T

    lane = lax.broadcasted_iota(jnp.int32, (BLK, 128), 1)
    low = lane < hd
    w3t, e3t, d3t = w3.T, e3.T, d3.T
    for t in range(n_tp):
        for pp in range(pc // 128):
            lo = t * pc + pp * 128
            sl = slice(lo, lo + 128)
            csl = slice(pp * 128, (pp + 1) * 128)
            acc = sm_ref[t, 4:5, csl]
            for j in range(4):
                acc = acc + xpad[5 + j:5 + j + BLK, sl] * sm_ref[t, j:j + 1, csl]
            x = silu(acc)
            ms = []
            for hh in range(2):
                h_id = lo // hd + hh
                col = jnp.broadcast_to(ac[:, h_id:h_id + 1], (BLK, BLK))
                dec = jnp.exp2(jnp.minimum(col - acT[h_id:h_id + 1, :], 0.0))
                ms.append(dec * cbm * dtT[h_id:h_id + 1, :])
            m = jnp.concatenate(ms, axis=1)
            xx = jnp.concatenate([jnp.where(low, x, 0.0), jnp.where(low, 0.0, x)], axis=0)
            y = dot(m, xx, HI)
            eexp = dot(e3t, e3_ref[:, sl])
            wexp = dot(w3t, e3_ref[:, sl])
            dexp = dot(d3t, e3_ref[:, sl])
            s = st[:, sl]
            y = y + dot(cmat, s, HI) * eexp
            st[:, sl] = s * dexp + dot(bT, x * wexp, HI)
            y_ref[:, sl] = y + sm_ref[t, 6:7, csl] * x

    @pl.when(i == pl.num_programs(0) - 1)
    def _():
        send_ref[...] = st[...]


def p1(u, off, halo, nw, wf, wbc, cbc, bbc, e3, n, n_dp, n_tp, interpret=False):
    d_model = u.shape[1]
    width = 256 * n_tp
    heads = width // 64
    rows = d_model // n_dp
    geom = (n_dp, n_tp, 64, width, heads)
    nb = n // BLK
    full = lambda shp: pl.BlockSpec(shp, lambda i, o: (0,) * len(shp), pipeline_mode=pl.Buffered(1))
    gs = pltpu.PrefetchScalarGridSpec(
        num_scalar_prefetch=1, grid=(nb,),
        in_specs=[
            pl.BlockSpec((BLK, d_model), lambda i, o: (o[0] + i, 0)),
            full((8, d_model)), full((1, d_model)),
            full((n_dp * n_tp, rows, 256)),
            pl.BlockSpec((n_tp, 32, 256), lambda i, o: (0, rows // 32, 0), pipeline_mode=pl.Buffered(1)),
            full((d_model, 256)), full((4, 256)), full((1, 256)), full((3 * heads, width)),
        ],
        out_specs=[
            pl.BlockSpec((BLK, width), lambda i, o: (i, 0)),
            pl.BlockSpec((BLK, 128), lambda i, o: (i, 0)),
            pl.BlockSpec((heads, BLK), lambda i, o: (0, i)),
            pl.BlockSpec((128, width), lambda i, o: (0, 0)),
        ],
        scratch_shapes=[
            pltpu.VMEM((d_model, width), BF16), pltpu.VMEM((heads, d_model), BF16), pltpu.VMEM((2 * heads, 256), F32),
            pltpu.VMEM((128, width), F32), pltpu.VMEM((BLK + 8, width), F32), pltpu.VMEM((BLK + 8, 256), F32),
            pltpu.VMEM((heads, 128), F32),
        ])
    return pl.pallas_call(
        functools.partial(p1_body, geom=geom), grid_spec=gs, name="p1",
        out_shape=[jax.ShapeDtypeStruct((n, width), F32), jax.ShapeDtypeStruct((n, 128), F32),
                   jax.ShapeDtypeStruct((heads, n), F32), jax.ShapeDtypeStruct((128, width), F32)],
        compiler_params=pltpu.CompilerParams(dimension_semantics=("arbitrary",), vmem_limit_bytes=60 << 20),
        cost_estimate=pl.CostEstimate(flops=n * 70_000_000, bytes_accessed=n * 12000, transcendentals=0),
        interpret=interpret,
    )(off, u, halo, nw, wf, wf, wbc, cbc, bbc, e3)


def p2_body(off_ref, u_ref, nw_ref, wz_ref, wo_ref, sm_ref, y_ref, c_ref, ac_ref, s_ref, e3_ref,
            o_ref, f_ref, wzb, wob, s3, *, geom):
    n_dp, n_tp, hd, width, heads = geom
    pc = width // n_tp
    rows_z = wzb.shape[0] // n_dp

    @pl.when(pl.program_id(0) == 0)
    def _():
        load_cols(wz_ref, wzb, n_dp, n_tp, rows_z, pc)
        load_wo(wo_ref, wob, n_dp, n_tp)
        a, b, c = split3(s_ref[...])
        s3[0, 0:128, :] = a
        s3[0, 128:256, :] = a
        s3[1, 0:128, :] = b
        s3[1, 128:256, :] = b
        s3[2, 0:128, :] = c
        s3[2, 128:256, :] = a

    u = u_ref[...].astype(F32)
    h = rms(u, nw_ref[...])
    c1, c2, c3 = split3(c_ref[...])
    cc12 = jnp.concatenate([c1, c2], axis=1)
    cc13 = jnp.concatenate([c1, c3], axis=1)
    eT = jnp.concatenate(split3(jnp.exp2(ac_ref[...])), axis=0).T
    vs, ss = [], 0.0
    for t in range(n_tp):
        sl = slice(t * pc, (t + 1) * pc)
        z = dot(h, wzb[:, sl]).astype(BF16).astype(F32)
        cor = dot(cc12, s3[0, :, sl]) + dot(cc12, s3[1, :, sl]) + dot(cc13, s3[2, :, sl])
        v = (y_ref[:, sl] + cor * dot(eT, e3_ref[:, sl])) * silu(z)
        ss = ss + jnp.sum(v * v, axis=-1, keepdims=True)
        vs.append(v)
    sc = lax.rsqrt(ss / width + EPS)
    acc = u
    g = jnp.concatenate([(vs[t] * sc * sm_ref[t, 5:6, :]).astype(BF16) for t in range(n_tp)], axis=1)
    un = (u + dot(g, wob[...])).astype(BF16)
    o_ref[...] = un
    f_ref[...] = un.astype(F32)


def load_wo(wf_ref, wb_ref, n_dp, n_tp):
    rows = wb_ref.shape[0] // n_tp
    cols = wb_ref.shape[1] // n_dp
    for d in range(n_dp):
        for t in range(n_tp):
            wb_ref[t * rows:(t + 1) * rows, d * cols:(d + 1) * cols] = wf_ref[d * n_tp + t].astype(BF16)


def p2(u, off, nw, wz, wo, wsm, y, c, ac, s, e3, n, n_dp, n_tp, out_rows=None, interpret=False):
    d_model = u.shape[1]
    width = 256 * n_tp
    heads = width // 64
    rows = d_model // n_dp
    geom = (n_dp, n_tp, 64, width, heads)
    nb = n // BLK
    full = lambda shp: pl.BlockSpec(shp, lambda i, o: (0,) * len(shp), pipeline_mode=pl.Buffered(1))
    gs = pltpu.PrefetchScalarGridSpec(
        num_scalar_prefetch=1, grid=(nb,),
        in_specs=[
            pl.BlockSpec((BLK, d_model), lambda i, o: (o[0] + i, 0)),
            full((1, d_model)),
            full((n_dp * n_tp, rows, 256)), full((n_dp * n_tp, 256, d_model // n_dp)),
            pl.BlockSpec((n_tp, 32, 256), lambda i, o: (0, rows // 32, 0), pipeline_mode=pl.Buffered(1)),
            pl.BlockSpec((BLK, width), lambda i, o: (i, 0)),
            pl.BlockSpec((BLK, 128), lambda i, o: (i, 0)),
            pl.BlockSpec((heads, BLK), lambda i, o: (0, i)),
            full((128, width)), full((3 * heads, width)),
        ],
        out_specs=[pl.BlockSpec((BLK, d_model), lambda i, o: (o[1] + i, 0)), pl.BlockSpec((BLK, d_model), lambda i, o: (i, 0))],
        scratch_shapes=[pltpu.VMEM((d_model, width), BF16), pltpu.VMEM((width, d_model), BF16),
                        pltpu.VMEM((3, 256, width), BF16)])
    return pl.pallas_call(
        functools.partial(p2_body, geom=geom), grid_spec=gs, name="p2",
        out_shape=[jax.ShapeDtypeStruct((out_rows or n, d_model), BF16), jax.ShapeDtypeStruct((n, d_model), F32)],
        compiler_params=pltpu.CompilerParams(dimension_semantics=("arbitrary",), vmem_limit_bytes=60 << 20),
        cost_estimate=pl.CostEstimate(flops=n * 30_000_000, bytes_accessed=n * 12000, transcendentals=0),
        interpret=interpret,
    )(off, u, nw, wz, wo, wsm, y, c, ac, s, e3)


def fin_body(off_ref, buf_ref, f_ref, o_ref):
    o_ref[...] = f_ref[...].astype(BF16)


def finish(buf, f, off):
    n, d_model = f.shape
    rows = 512
    gs = pltpu.PrefetchScalarGridSpec(
        num_scalar_prefetch=1, grid=(n // rows,),
        in_specs=[pl.BlockSpec(memory_space=pl.ANY), pl.BlockSpec((rows, d_model), lambda i, o: (i, 0))],
        out_specs=pl.BlockSpec((rows, d_model), lambda i, o: (o[0] + i, 0)))
    return pl.pallas_call(
        fin_body, grid_spec=gs, name="finish", out_shape=jax.ShapeDtypeStruct(buf.shape, BF16),
        input_output_aliases={1: 0},
        compiler_params=pltpu.CompilerParams(dimension_semantics=("arbitrary",)),
        cost_estimate=pl.CostEstimate(flops=n * d_model, bytes_accessed=n * d_model * 6, transcendentals=0),
    )(off, buf, f)


from jax.sharding import PartitionSpec as P


def small_rows(conv, bias, gate, skip, dtb, al, wdt):
    f = lambda v: v.astype(F32)
    hp = skip.shape[0]
    return jnp.concatenate([
        f(conv), f(bias)[None], f(gate)[None], jnp.repeat(skip, 256 // hp)[None], jnp.zeros((1, 256), F32),
        jnp.broadcast_to(dtb[:, None], (hp, 256)), jnp.broadcast_to((-jnp.exp(al) * LOG2E)[:, None], (hp, 256)),
        f(wdt).T.reshape(-1, 256)], axis=0)


def solution(mesh):
    n_tp, n_dp = mesh.shape['tp'], mesh.shape['dp']
    rep, col, vec = P(), P(None, None, 'tp'), P(None, 'tp')
    in_specs = (P('dp'), rep, col, col, rep, col, col, rep, vec, rep, vec, vec, vec, vec, P(None, 'tp', None))

    def device_forward(hidden, norm_w, w_z, w_x, w_bc, w_dt, conv_x, conv_bc, bias_x, bias_bc, dt_bias, a_log, d_skip, gate_w, w_out):
        u = hidden[0]
        steps, d_model = u.shape
        heads = dt_bias.shape[1] * n_tp
        n = steps // 2
        dp, tp = lax.axis_index('dp'), lax.axis_index('tp')
        core = tp % 2
        rows, ocols = d_model // n_dp, d_model // n_dp
        gather = lambda v: lax.all_gather(v, ('dp', 'tp'))
        one = jnp.repeat(jnp.eye(heads, dtype=BF16), 64, axis=1)
        e3 = jnp.concatenate([one, one, one], axis=0)
        up = [(2 * k, 2 * k + 1) for k in range(n_tp // 2)]
        swap = [(k, k ^ 1) for k in range(n_tp)]
        wxs, wzs, wos = [], [], []
        for l in range(2):
            sm = small_rows(conv_x[l], bias_x[l], gate_w[l], d_skip[l], dt_bias[l], a_log[l], w_dt[l])
            qx = lax.dynamic_slice(w_x[l], (dp * rows, 0), (rows, 256)).astype(F32)
            wxs.append(gather(jnp.concatenate([qx, sm], axis=0)))
            wzs.append(gather(lax.dynamic_slice(w_z[l], (dp * rows, 0), (rows, 256)).astype(F32)))
            wos.append(gather(lax.dynamic_slice(w_out[l], (0, dp * ocols), (256, ocols)).astype(F32)))
        cur, nb = u, n // BLK
        off = jnp.stack([core * nb, 0 * core])
        zero = jnp.zeros((2,), jnp.int32)
        start = lax.dynamic_slice(u, (core * (n - 8), 0), (8, d_model)).astype(F32)
        halo = jnp.where(core == 1, start, 0.0)
        for l in range(2):
            nw = norm_w[l].astype(F32)[None]
            y, c, ac, s_end = p1(cur, off, halo, nw, wxs[l], w_bc[l], conv_bc[l].astype(F32), bias_bc[l].astype(F32)[None], e3, n, n_dp, n_tp)
            s = lax.ppermute(s_end, 'tp', up)
            off2 = off if l == 0 else jnp.stack([0 * core, core * nb])
            o, f = p2(cur, off2, nw, wzs[l], wos[l], wxs[l], y, c, ac, s, e3, n, n_dp, n_tp, out_rows=n if l == 0 else steps)
            cur, off = o, zero
            if l == 0:
                halo = lax.ppermute(f[n - 8:], 'tp', up)
        other = lax.ppermute(f, 'tp', swap)
        return finish(o, other, jnp.reshape((1 - core) * (n // 512), (1,)))[None]

    return jax.shard_map(device_forward, mesh=mesh, in_specs=in_specs, out_specs=P('dp'), check_vma=False)
```

time: 1450 us -> 600 us (0.41)
  waiting for transfers between devices: 976 us -> 108 us
  Pallas kernels: 0 us -> 441 us
  matrix products: 208 us -> 0 us
  other arithmetic: 92 us -> 11.9 us
  local copies, waits for them, and re-layouts: 95.3 us -> 16.9 us
  blocking collectives: 58.1 us -> 0 us
    psum x2 -> x0, waiting for transfers between devices: 976 us -> none  [mixer_layer(): full_out = lax.psum(part_out, 'tp')]
    pallas_call x0 -> x5, Pallas kernels: none -> 441 us  [the longest x2 304 us: p1(): pl.pallas_call(functools.partial(p1_body, geom=geom), grid_spec=gs, name=...]
    dot_general x20 -> x0, matrix products: 208 us -> none  [the longest x2 62.4 us: ssd_blocks(): jnp.einsum('bchij,bcjhp->bcihp', mix_mat, x_dt, precision=FULL_PRECISION)]
    all_gather x0 -> x6, waiting for transfers between devices: none -> 89.3 us  [device_forward(): gather = lambda v: lax.all_gather(v, ('dp', 'tp'))]
    psum x2 -> x0, blocking collectives: 58.1 us -> none  [mixer_layer(): total_sq = lax.psum(part_sq, 'tp')]
    reshape x7 -> x3, local copies, waits for them, and re-layouts: 49.5 us -> 0.3 us  [the longest x1 0.27 us: device_forward(): one = jnp.repeat(jnp.eye(heads, dtype=BF16), 64, axis=1)]
    mul x8 -> x1, other arithmetic: 33.7 us -> 0.76 us  [small_rows(): -jnp.exp(al) * LOG2E]
    reduce_sum x2 -> x0, other arithmetic: 20.2 us -> none  [mixer_layer(): jnp.mean(residual * residual, axis=-1, keepdims=True) + EPSILON]
  transfers between devices with their start and end apart: 2 -> 10, of which waited for: 2 -> 5; matrix products, arithmetic and copies ran while one was open for 0% -> 3% of each run, Pallas kernels for 0% -> 61%
where the time goes in v1:
time: 600 us; the launch traced here: 599 us
  Pallas kernels  441 us (74%)
  waiting for transfers between devices  108 us (18%)
  local copies, waits for them, and re-layouts  16.9 us (3%)
  between operations  13.6 us (2%)
  other arithmetic  11.9 us (2%)
  starting transfers between devices  7.46 us (1%)
    pallas_call x2, Pallas kernels, p1(): pl.pallas_call(functools.partial(p1_body, geom=geom), grid_spec=gs, name=...  304 us
    pallas_call x2, Pallas kernels, p2(): pl.pallas_call(functools.partial(p2_body, geom=geom), grid_spec=gs, name=...  129 us
    all_gather x6, waiting for transfers between devices, device_forward(): gather = lambda v: lax.all_gather(v, ('dp', 'tp'))  89.3 us
    ppermute x1, waiting for transfers between devices, device_forward(): other = lax.ppermute(f, 'tp', swap)  18.8 us
  transfers between devices with their start and end apart: 10, of which 5 were waited for; matrix products, arithmetic and copies ran while one was open for 3% of the time, Pallas kernels for 61%

profile of v1, /device:TPU:0, one launch (start us, length us, event | category | flops | bytes accessed | tf_op | source)
XLA Modules:
  0.0 599.4 jit_solution(1991152641438406898)
XLA Ops:
  6.5 1.4 fusion.1
  7.9 0.7 convert_bitcast_fusion
  8.6 0.7 bitcast_convert_fusion.3
  9.3 0.8 slice_bitcast_fusion.2
  10.1 0.8 multiply_bitcast_fusion
  10.9 0.8 slice_bitcast_fusion.3
  11.6 0.1 broadcast_in_dim.54
  11.7 0.1 broadcast_in_dim_reshape.6
  11.8 0.8 slice_convert_fusion.3
  12.6 0.1 broadcast_in_dim.56
  12.6 0.1 broadcast_in_dim.57
  12.7 2.6 concatenate.9
  15.3 0.0 all-gather.17.cloned.1.call-update
  15.3 0.0 all-gather.11.cloned.1.call-start
  15.3 2.1 fusion.2
  17.4 0.7 dynamic-slice_convert_fusion.2
  18.1 0.0 all-gather.11.cloned.1.call-update
  18.1 0.0 all-gather.9.cloned.1.call-start
  18.2 1.3 fusion.3
  19.5 0.7 dynamic-slice_convert_fusion.3
  20.2 0.0 all-gather.9.cloned.1.call-update
  20.2 0.0 all-gather.19.cloned.1.call-start
  20.3 0.1 broadcast_in_dim.60
  20.4 0.1 broadcast_in_dim_reshape.7
  20.5 0.1 broadcast_in_dim.62
  20.5 0.1 broadcast_in_dim.63
  20.6 2.6 concatenate.11
  23.2 0.0 all-gather.19.cloned.1.call-update
  23.2 0.0 all-gather.13.cloned.1.call-start
  23.2 0.7 dynamic-slice_convert_fusion.1
  24.0 0.0 all-gather.13.cloned.1.call-update
  24.0 0.0 all-gather.15.cloned.1.call-start
  24.1 0.2 broadcast_in_dim.59
  24.3 0.3 reshape.76
  24.6 1.4 slice_convert_fusion
  26.0 1.1 slice_bitcast_fusion
  27.1 0.6 bitcast_convert_fusion.2
  27.7 0.5 slice_convert_fusion.2
  28.3 0.6 pad_add_fusion.1.off_ref
  28.9 1.3 select_bitcast_fusion.halo_ref
  30.2 69.5 %all-gather.17.cloned.1.call-done = f32[9216,256]{1,0:T(8,128)} async-done(((f32[288,256]{1,0:T(8,128)}), f32[9216,256]{1,0:T(8,128)}) %all-gather.17.cloned.1.call-update) | async-done | bytes 9437200 | tf_op jit(solution)/shard_map/all_gather | solution.py:303
  99.6 152.2 %p1.2 = (f32[3072,2048]{1,0:T(8,128)}, f32[3072,128]{1,0:T(8,128)}, f32[32,3072]{1,0:T(8,128)}, f32[128,2048]{1,0:T(8,128)}) custom-call(s32[2]{0:T(128)} %pad_add_fusion.1.off_ref, bf16[6144,1024]{1,0:T(8,128)(2,1)} %bitcast.52, f32[8,1024]{1,0:T(8,128)} %select_bitcast_fusion.halo_ref, f32[1,1024]{1,0:T(1,128)} %get-tuple-element.44.nw_ref, ...), custom_call_target="tpu_custom_call" | custom-call | flops 215040000000 | bytes 36864000 | tf_op jit(solution)/shard_map/p1/pallas_call | solution.py:169
  251.8 2.4 collective-permute-start
  254.2 0.0 all-gather.11.cloned.1.call-done.wo_ref
  254.2 4.1 all-gather.9.cloned.1.call-done.wz_ref
  258.3 1.0 copy-done.5
  259.4 64.3 %p2.2 = (bf16[3072,1024]{1,0:T(8,128)(2,1)}, f32[3072,1024]{1,0:T(8,128)}) custom-call(s32[2]{0:T(128)} %pad_add_fusion.1.off_ref, bf16[6144,1024]{1,0:T(8,128)(2,1)} %bitcast.53, f32[1,1024]{1,0:T(1,128)} %get-tuple-element.44.nw_ref, f32[32,256,256]{2,1,0:T(8,128)} %all-gather.9.cloned.1.call-done.wz_ref, ...), custom_call_target="tpu_custom_call" | custom-call | flops 92160000000 | bytes 36864000 | tf_op jit(solution)/shard_map/p2/pallas_call | solution.py:250
  323.6 0.8 slice.112
  324.4 2.1 collective-permute-start.1
  326.6 1.7 dynamic-slice_convert_fusion
  328.2 0.0 all-gather.15.cloned.1.call-update
  328.2 12.9 %all-gather.19.cloned.1.call-done = f32[9216,256]{1,0:T(8,128)} async-done(((f32[288,256]{1,0:T(8,128)}), f32[9216,256]{1,0:T(8,128)}) %all-gather.19.cloned.1.call-update) | async-done | bytes 9437200 | tf_op jit(solution)/shard_map/all_gather | solution.py:303
  341.2 0.0 collective-permute-done.1.halo_ref
  341.2 0.5 broadcast_3_off_ref.2.off_ref
  341.7 0.1 copy-done.6
  341.8 152.2 %p1.3 = (f32[3072,2048]{1,0:T(8,128)}, f32[3072,128]{1,0:T(8,128)}, f32[32,3072]{1,0:T(8,128)}, f32[128,2048]{1,0:T(8,128)}) custom-call(s32[2]{0:T(128)} %broadcast_3_off_ref.2.off_ref, bf16[3072,1024]{1,0:T(8,128)(2,1)} %get-tuple-element.21.u_ref, f32[8,1024]{1,0:T(8,128)} %copy-done.6, f32[1,1024]{1,0:T(1,128)} %get-tuple-element.43.nw_ref, ...), custom_call_target="tpu_custom_call" | custom-call | flops 215040000000 | bytes 36864000 | tf_op jit(solution)/shard_map/p1/pallas_call | solution.py:169
  493.9 2.4 collective-permute-start.2
  496.4 0.6 pad_add_fusion.off_ref
  497.0 2.8 all-gather.15.cloned.1.call-done.wo_ref
  499.9 1.0 copy-done.4
  500.8 64.3 %p2.3 = (bf16[6144,1024]{1,0:T(8,128)(2,1)}, f32[3072,1024]{1,0:T(8,128)}) custom-call(s32[2]{0:T(128)} %pad_add_fusion.off_ref, bf16[3072,1024]{1,0:T(8,128)(2,1)} %get-tuple-element.21.u_ref, f32[1,1024]{1,0:T(1,128)} %get-tuple-element.43.nw_ref, f32[32,256,256]{2,1,0:T(8,128)} %all-gather.13.cloned.1.call-done.wz_ref, ...), custom_call_target="tpu_custom_call" | custom-call | flops 92160000000 | bytes 36864000 | tf_op jit(solution)/shard_map/p2/pallas_call | solution.py:250
  565.1 0.3 collective-permute-start.3
  565.4 18.8 %collective-permute-done.3.f_ref = f32[3072,1024]{1,0:T(8,128)} collective-permute-done((f32[3072,1024]{1,0:T(8,128)}, f32[3072,1024]{1,0:T(8,128)}, u32[]{:S(2)}, u32[]{:S(2)}) %collective-permute-start.3) | collective-permute-done | bytes 12582944 | tf_op jit(solution)/shard_map/ppermute | solution.py:329
  584.2 8.4 %finish.1 = bf16[6144,1024]{1,0:T(8,128)(2,1)} custom-call(s32[1]{0:T(128)} %bitcast.off_ref, bf16[6144,1024]{1,0:T(8,128)(2,1)} %get-tuple-element.27.buf_ref, f32[3072,1024]{1,0:T(8,128)} %collective-permute-done.3.f_ref), custom_call_target="tpu_custom_call", output_to_operand_aliasing={{}: (1, {})} | custom-call | flops 3145728 | bytes 18874368 | tf_op jit(solution)/shard_map/finish/pallas_call | solution.py:270
  (24 shorter events, 0.1 us)
Async XLA Ops:
  6.5 19.5 %copy-start = (bf16[2,1024,256]{2,1,0:T(8,128)(2,1)S(1)}, bf16[2,1024,256]{2,1,0:T(8,128)(2,1)}, u32[]{:S(2)}) copy-start(bf16[2,1024,256]{2,1,0:T(8,128)(2,1)} %param.19) | copy-start | bytes 3145732
  6.5 20.6 %copy-start.2 = (bf16[2,4,256]{2,1,0:T(4,128)(2,1)S(1)}, bf16[2,4,256]{2,1,0:T(4,128)(2,1)}, u32[]{:S(2)}) copy-start(bf16[2,4,256]{2,1,0:T(4,128)(2,1)} %param.22) | copy-start | bytes 12292
  6.5 21.2 %copy-start.3 = (bf16[2,256]{1,0:T(2,128)(2,1)S(1)}, bf16[2,256]{1,0:T(2,128)(2,1)}, u32[]{:S(2)}) copy-start(bf16[2,256]{1,0:T(2,128)(2,1)} %param.24) | copy-start | bytes 3076
  6.5 93.1 %all-gather.17.cloned.1.call-start = ((), (), s32[]{:S(2)}) async-start(), calls=%async_computation.4 | async-start | bytes 9732096 | tf_op jit(solution)/shard_map/all_gather | solution.py:303
  15.3 239.0 %all-gather.11.cloned.1.call-start = ((), (), s32[]{:S(2)}) async-start(), calls=%async_computation.1 | async-start | bytes 8650752 | tf_op jit(solution)/shard_map/all_gather | solution.py:303
  18.1 240.2 %all-gather.9.cloned.1.call-start = ((), (), s32[]{:S(2)}) async-start(), calls=%async_computation | async-start | bytes 8650752 | tf_op jit(solution)/shard_map/all_gather | solution.py:303
  20.2 320.9 %all-gather.19.cloned.1.call-start = ((), (), s32[]{:S(2)}) async-start(), calls=%async_computation.5 | async-start | bytes 9732096 | tf_op jit(solution)/shard_map/all_gather | solution.py:303
  23.2 473.8 %all-gather.13.cloned.1.call-start = ((), (), s32[]{:S(2)}) async-start(), calls=%async_computation.2 | async-start | bytes 8650752 | tf_op jit(solution)/shard_map/all_gather | solution.py:303
  24.0 475.8 %all-gather.15.cloned.1.call-start = ((), (), s32[]{:S(2)}) async-start(), calls=%async_computation.3 | async-start | bytes 8650752 | tf_op jit(solution)/shard_map/all_gather | solution.py:303
  24.6 75.0 %copy-start.1 = (bf16[96,2048]{1,0:T(8,128)(2,1)}, bf16[96,2048]{1,0:T(8,128)(2,1)S(1)}, u32[]{:S(2)}) copy-start(bf16[96,2048]{1,0:T(8,128)(2,1)S(1)} %constant_dynamic-update-slice_fusion.e3_ref) | copy-start | bytes 1179652
  251.8 6.5 %collective-permute-start = (f32[128,2048]{1,0:T(8,128)}, f32[128,2048]{1,0:T(8,128)S(1)}, u32[]{:S(2)}, u32[]{:S(2)}) collective-permute-start(f32[128,2048]{1,0:T(8,128)} %get-tuple-element.20), channel_id=1, source_target_pairs={{0,1},{2,3},{4,5},{6,7},{8,9},{10,11},{12,13},{14,15},{16,17},{18,... | collective-permute-start | bytes 3145736 | tf_op jit(solution)/shard_map/ppermute | solution.py:323
  258.3 1.0 copy-start.5
  324.4 16.8 %collective-permute-start.1 = (f32[8,1024]{1,0:T(8,128)S(1)}, f32[8,1024]{1,0:T(8,128)S(1)}, u32[]{:S(2)}, u32[]{:S(2)}) collective-permute-start(f32[8,1024]{1,0:T(8,128)S(1)} %slice.112), channel_id=1, source_target_pairs={{0,1},{2,3},{4,5},{6,7},{8,9},{10,11},{12,13},{14,15},{16,17},{18,... | collective-permute-start | bytes 98312 | tf_op jit(solution)/shard_map/ppermute | solution.py:328
  341.2 0.6 copy-start.6
  493.9 5.9 collective-permute-start.2
  499.9 1.0 copy-start.4
  565.1 19.1 %collective-permute-start.3 = (f32[3072,1024]{1,0:T(8,128)}, f32[3072,1024]{1,0:T(8,128)}, u32[]{:S(2)}, u32[]{:S(2)}) collective-permute-start(f32[3072,1024]{1,0:T(8,128)} %get-tuple-element.28), channel_id=1, source_target_pairs={{0,1},{1,0},{2,3},{3,2},{4,5},{5,4},{6,7},{7,6},{8,9},{9,8},{10,11... | collective-permute-start | bytes 37748744 | tf_op jit(solution)/shard_map/ppermute | solution.py:329
Sparse Core Ops, SparseCore 0:
  15.4 84.1 all-gather.16
  102.6 75.8 all-gather.10
  181.5 76.7 all-gather.8
  261.2 79.8 all-gather.18
  344.0 75.8 all-gather.12
  422.7 77.0 all-gather.14

commit v2 on v1

v2 whole, which is shorter than its diff:
```python
import functools
import jax
import jax.numpy as jnp
from jax import lax
from jax.experimental import pallas as pl
from jax.experimental.pallas import tpu as pltpu

EPS = 1e-5
LOG2E = 1.4426950408889634
HI = lax.Precision.HIGHEST
F32 = jnp.float32
BF16 = jnp.bfloat16
BLK = 128
BLK2 = 256


def silu(v):
    half = 0.5 * v
    return half + half * jnp.tanh(half)


def split3(v):
    a = v.astype(BF16)
    r = v - a.astype(F32)
    b = r.astype(BF16)
    c = (r - b.astype(F32)).astype(BF16)
    return a, b, c


def rms(u, nw):
    return (u * lax.rsqrt(jnp.mean(u * u, axis=-1, keepdims=True) + EPS) * nw).astype(BF16)


def dot(a, b, prec=None):
    return jnp.dot(a, b, preferred_element_type=F32, precision=prec)


def dott(a, b, prec=None):
    return lax.dot_general(a, b, (((1,), (1,)), ((), ())), preferred_element_type=F32, precision=prec)


def load_cols(wf_ref, wb_ref, n_dp, n_tp, rows, cols):
    for d in range(n_dp):
        for t in range(n_tp):
            wb_ref[d * rows:(d + 1) * rows, t * cols:(t + 1) * cols] = wf_ref[d * n_tp + t].astype(BF16)


def time_of(r):
    return 8 * (r % 8) + r // 8


def roll8(v):
    c = v.shape[1]
    return pltpu.roll(v.reshape(3, 8, c), 1, 1).reshape(24, c)


def conv_block(cur, prev, taps, bias, first):
    now = roll8(cur[40:])
    sh = jnp.where(first, prev, now)
    out = bias + cur * taps[3]
    for k in range(1, 4):
        out = out + jnp.concatenate([sh[8 * (3 - k):], cur[:64 - 8 * k]], axis=0) * taps[3 - k]
    return out, now


def unmix(v, buf):
    n, c = v.shape
    for j in range(c // 128):
        buf[n * j:n * (j + 1), :] = v[:, 128 * j:128 * (j + 1)]
    cols = [jnp.concatenate([buf[pl.ds(n * j + b + k, 8, stride=8), :] for b in range(0, n, 64) for k in range(8)], axis=0)
            for j in range(c // 128)]
    return jnp.concatenate(cols, axis=1)


EARLY = (2, 4, 6)


def head_row(h, heads):
    return (h % 2) * (heads // 2) + h // 2


def expand_mat(heads):
    order = sorted(range(heads), key=lambda h: head_row(h, heads))
    one = jnp.repeat(jnp.eye(heads, dtype=BF16)[jnp.array(order)], 64, axis=1)
    return jnp.concatenate([one, one, one], axis=0)


def kcat6(parts):
    a, b, c = parts
    return jnp.concatenate([a, b, c, a], axis=1), jnp.concatenate([b, a], axis=1)


def kcat6r(parts):
    a, b, c = parts
    return jnp.concatenate([a, a, a, b], axis=0), jnp.concatenate([b, c], axis=0)


def block_diag(x, lo, hi):
    z = jnp.zeros((x.shape[0], 128), BF16)
    l, r = x[:, :128], x[:, 128:]
    return jnp.concatenate([
        jnp.concatenate([l * lo, z], axis=1), jnp.concatenate([l * hi, z], axis=1),
        jnp.concatenate([z, r * lo], axis=1), jnp.concatenate([z, r * hi], axis=1)], axis=0)


def p1_body(off_ref, u_ref, halo_ref, nw_ref, wf_ref, sm_ref, wbc_ref, cbc_ref, bbc_ref, e3_ref,
            y_ref, c_ref, ac_ref, send_ref, wxb, wdt, cst, st, xcar, qcar, aoff, ubuf, *, geom, mixed):
    n_dp, n_tp, hd, width, heads = geom
    i = pl.program_id(0)
    nst = 128
    pc = width // n_tp
    hp = heads // n_tp
    sub = BLK // 2

    @pl.when(i == 0)
    def _():
        load_cols(wf_ref, wxb, n_dp, n_tp, wxb.shape[0] // n_dp, pc)
        kc = wxb.shape[0] // pc
        for t in range(n_tp):
            for k in range(hp):
                r = head_row(hp * t + k, heads)
                for c in range(kc):
                    wdt[r:r + 1, c * pc:(c + 1) * pc] = sm_ref[t, 16 + kc * k + c:17 + kc * k + c, :].astype(BF16)
                cst[r:r + 1, :] = sm_ref[t, 8 + k:9 + k, :]
                cst[heads + r:heads + r + 1, :] = sm_ref[t, 12 + k:13 + k, :]
        st[...] = jnp.zeros_like(st)
        aoff[...] = jnp.zeros_like(aoff)
        hh = rms(halo_ref[...], nw_ref[...])
        xcar[...] = roll8(dot(hh, wxb[...]).astype(BF16).astype(F32))
        qcar[...] = roll8(dot(hh, wbc_ref[...]).astype(BF16).astype(F32))

    if mixed:
        u = u_ref[...].astype(F32)
    else:
        u = unmix(u_ref[...].astype(F32), ubuf)
    h = rms(u, nw_ref[...])
    first = lax.broadcasted_iota(jnp.int32, (24, 256), 0) % 8 == 0

    def conv(cur, prev, taps, bias):
        a, now = conv_block(cur[:sub], prev, taps, bias, first)
        b, now = conv_block(cur[sub:], now, taps, bias, first)
        return silu(jnp.concatenate([a, b], axis=0)), now

    q0 = dot(h, wbc_ref[...])
    rT = dott(wdt[...], h).astype(BF16).astype(F32)
    x0s = {}

    def proj(t):
        if t < n_tp:
            x0s[t] = dot(h, wxb[:, t * pc:(t + 1) * pc])

    for t in range(EARLY[0]):
        proj(t)

    bc, qcar[...] = conv(q0.astype(BF16).astype(F32), qcar[...],
                         [cbc_ref[j:j + 1, :] for j in range(4)], bbc_ref[...])
    bmat, cmat = bc[:, :nst], bc[:, nst:]
    c_ref[...] = cmat

    pre = rT + cst[0:heads, 0:BLK]
    dtT = jnp.maximum(pre, 0.0) + jnp.log1p(jnp.exp(-jnp.abs(pre)))
    aT = dtT * cst[heads:2 * heads, 0:BLK]
    ri = lax.broadcasted_iota(jnp.int32, (BLK, BLK), 0)
    ci = lax.broadcasted_iota(jnp.int32, (BLK, BLK), 1)
    tr, tc = ri // sub * sub + time_of(ri % sub), ci // sub * sub + time_of(ci % sub)
    upper = jnp.where(tr <= tc, 1.0, 0.0).astype(F32)
    acT = dot(aT, upper, HI)
    mid, alast = acT[:, sub - 1:sub], acT[:, BLK - 1:BLK]
    lowh = lax.broadcasted_iota(jnp.int32, (heads, BLK), 1) < sub
    wT = dtT * jnp.exp2(jnp.where(lowh, mid, alast) - acT)
    w3t = jnp.concatenate(split3(wT), axis=0).T
    a3t = jnp.concatenate(split3(acT), axis=0).T
    ac_ref[...] = acT + aoff[:, 0:1]
    aoff[...] = aoff[...] + alast
    low16 = lax.broadcasted_iota(jnp.int32, (heads // 2, BLK), 1) < sub

    def pair_rows(v):
        ev, od = v[:heads // 2], v[heads // 2:]
        return (jnp.where(low16, ev, pltpu.roll(od, sub, 1)), jnp.where(low16, pltpu.roll(ev, sub, 1), od))

    ac_rows, dt_rows = pair_rows(acT), pair_rows(dtT)

    for t in range(EARLY[0], EARLY[1]):
        proj(t)
    cb = dott(cmat, bmat, HI)
    for t in range(EARLY[1], EARLY[2]):
        proj(t)
    rs = lax.broadcasted_iota(jnp.int32, (sub, BLK), 0)
    cs = lax.broadcasted_iota(jnp.int32, (sub, BLK), 1)
    tri = time_of(rs) >= time_of(cs % sub)
    ca, cb_ = cb[:sub], cb[sub:]
    cbd = (jnp.where(tri, jnp.where(cs < sub, ca, pltpu.roll(ca, sub, 1)), 0.0),
           jnp.where(tri, jnp.where(cs < sub, pltpu.roll(cb_, sub, 1), cb_), 0.0))
    bT = bmat.T
    la = jnp.concatenate([bT[:, :sub], cb_[:, :sub]], axis=0)
    la1, la2 = kcat6(split3(la))
    lb1, lb2 = kcat6(split3(pltpu.roll(bT, sub, 1)[:, :sub]))
    c1, c2, c3 = split3(cmat)
    cc12 = jnp.concatenate([c1, c2], axis=1)
    cc13 = jnp.concatenate([c1, c3], axis=1)

    lane = lax.broadcasted_iota(jnp.int32, (sub, 128), 1)
    lo = jnp.where(lane < hd, 1.0, 0.0).astype(BF16)
    hi = jnp.where(lane < hd, 0.0, 1.0).astype(BF16)
    def pre(t):
        sl = slice(t * pc, (t + 1) * pc)
        s1, s2, s3 = split3(st[:, sl])
        inter = (dot(cc12, jnp.concatenate([s1, s1], axis=0)) + dot(cc12, jnp.concatenate([s2, s2], axis=0))
                 + dot(cc13, jnp.concatenate([s3, s1], axis=0)))
        proj(t + EARLY[2])
        return x0s.pop(t), dot(a3t, e3_ref[:, sl]), dot(w3t, e3_ref[:, sl]), inter

    def mid_(t, x0, acx, wx, inter):
        sl = slice(t * pc, (t + 1) * pc)
        x, xcar[:, sl] = conv(x0.astype(BF16).astype(F32), xcar[:, sl],
                              [sm_ref[t, j:j + 1, :] for j in range(4)], sm_ref[t, 4:5, :])
        xw = split3(x * wx)
        r = kcat6r([v[:sub] for v in xw]) + kcat6r([v[sub:] for v in xw])
        ms, xs = [], []
        for k in range(2):
            rows = slice(k * sub, (k + 1) * sub)
            m = []
            for p in range(pc // 128):
                g = t * (pc // 128) + p
                seg = acx[rows, p * 128:(p + 1) * 128] - ac_rows[k][g:g + 1, :]
                m.append(jnp.exp2(jnp.minimum(seg, 0.0)) * cbd[k] * dt_rows[k][g:g + 1, :])
            ms.append(split3(jnp.concatenate(m, axis=1)))
            xs.append([block_diag(v, lo, hi) for v in split3(x[rows])])
        return x, acx, inter, r, ms, xs

    def fin(t, x, acx, inter, r, ms, xs):
        sl = slice(t * pc, (t + 1) * pc)
        ra1, ra2, rb1, rb2 = r
        ra = dot(la1, ra1) + dot(la2, ra2)
        rb = dot(lb1, rb1) + dot(lb2, rb2)
        am, al = acx[sub - 1:sub], acx[BLK - 1:BLK]
        skip = sm_ref[t, 6:7, :]
        for k in range(2):
            rows = slice(k * sub, (k + 1) * sub)
            (m1, m2, m3), (x1, x2, x3) = ms[k], xs[k]
            r1 = dot(jnp.concatenate([m1, m2, m3], axis=0), x1)
            r2 = dot(jnp.concatenate([m1, m2], axis=0), x2)
            y = r1[:sub] + r1[sub:2 * sub] + r1[2 * sub:] + r2[:sub] + r2[sub:] + dot(m1, x3)
            y = y + inter[rows] * jnp.exp2(acx[rows])
            if k == 1:
                y = y + ra[nst:] * jnp.exp2(acx[rows] - am)
            y_ref[rows, sl] = y + skip * x[rows]
        st[:, sl] = st[:, sl] * jnp.exp2(al) + ra[:nst] * jnp.exp2(al - am) + rb

    m = mid_(0, *pre(0))
    for t in range(n_tp):
        if t + 1 < n_tp:
            p = pre(t + 1)
        fin(t, *m)
        if t + 1 < n_tp:
            m = mid_(t + 1, *p)

    @pl.when(i == pl.num_programs(0) - 1)
    def _():
        send_ref[...] = st[...]


def p1(u, off, halo, nw, wf, wbc, cbc, bbc, e3, n, n_dp, n_tp, mixed, interpret=False):
    d_model = u.shape[1]
    width = 256 * n_tp
    heads = width // 64
    rows = d_model // n_dp
    geom = (n_dp, n_tp, 64, width, heads)
    nb = n // BLK
    full = lambda shp: pl.BlockSpec(shp, lambda i, o: (0,) * len(shp), pipeline_mode=pl.Buffered(1))
    gs = pltpu.PrefetchScalarGridSpec(
        num_scalar_prefetch=1, grid=(nb,),
        in_specs=[
            pl.BlockSpec((BLK, d_model), lambda i, o: (o[0] + i, 0)),
            full((24, d_model)), full((1, d_model)),
            full((n_dp * n_tp, rows, 256)),
            pl.BlockSpec((n_tp, 32, 256), lambda i, o: (0, rows // 32, 0), pipeline_mode=pl.Buffered(1)),
            full((d_model, 256)), full((4, 256)), full((1, 256)), full((3 * heads, width)),
        ],
        out_specs=[
            pl.BlockSpec((BLK, width), lambda i, o: (i, 0)),
            pl.BlockSpec((BLK, 128), lambda i, o: (i, 0)),
            pl.BlockSpec((heads, BLK), lambda i, o: (0, i)),
            pl.BlockSpec((128, width), lambda i, o: (0, 0)),
        ],
        scratch_shapes=[
            pltpu.VMEM((d_model, width), BF16), pltpu.VMEM((heads, d_model), BF16), pltpu.VMEM((2 * heads, 256), F32),
            pltpu.VMEM((128, width), F32), pltpu.VMEM((24, width), F32), pltpu.VMEM((24, 256), F32),
            pltpu.VMEM((heads, 128), F32), pltpu.VMEM((d_model // 128 * BLK, 128), F32),
        ])
    return pl.pallas_call(
        functools.partial(p1_body, geom=geom, mixed=mixed), grid_spec=gs, name="p1",
        out_shape=[jax.ShapeDtypeStruct((n, width), F32), jax.ShapeDtypeStruct((n, 128), F32),
                   jax.ShapeDtypeStruct((heads, n), F32), jax.ShapeDtypeStruct((128, width), F32)],
        compiler_params=pltpu.CompilerParams(dimension_semantics=("arbitrary",), vmem_limit_bytes=60 << 20),
        cost_estimate=pl.CostEstimate(flops=n * 70_000_000, bytes_accessed=n * 12000, transcendentals=0),
        interpret=interpret,
    )(off, u, halo, nw, wf, wf, wbc, cbc, bbc, e3)


def p2_body(off_ref, u_ref, nw_ref, wz_ref, wo_ref, sm_ref, y_ref, c_ref, ac_ref, s_ref, e3_ref,
            o_ref, f_ref, wzb, wob, s3, ubuf, *, geom, mix_in, mix_out):
    n_dp, n_tp, hd, width, heads = geom
    pc = width // n_tp
    rows_z = wzb.shape[0] // n_dp

    @pl.when(pl.program_id(0) == 0)
    def _():
        load_cols(wz_ref, wzb, n_dp, n_tp, rows_z, pc)
        load_wo(wo_ref, wob, n_dp, n_tp)
        a, b, c = split3(s_ref[...])
        s3[0, 0:128, :] = a
        s3[0, 128:256, :] = a
        s3[1, 0:128, :] = b
        s3[1, 128:256, :] = b
        s3[2, 0:128, :] = c
        s3[2, 128:256, :] = a

    if mix_in:
        u = u_ref[...].astype(F32)
    else:
        u = unmix(u_ref[...].astype(F32), ubuf)
    h = rms(u, nw_ref[...])
    c1, c2, c3 = split3(c_ref[...])
    cc12 = jnp.concatenate([c1, c2], axis=1)
    cc13 = jnp.concatenate([c1, c3], axis=1)
    eT = jnp.concatenate(split3(jnp.exp2(ac_ref[...])), axis=0).T
    vs, ss = [], 0.0
    for t in range(n_tp):
        sl = slice(t * pc, (t + 1) * pc)
        z = dot(h, wzb[:, sl]).astype(BF16).astype(F32)
        cor = dot(cc12, s3[0, :, sl]) + dot(cc12, s3[1, :, sl]) + dot(cc13, s3[2, :, sl])
        v = (y_ref[:, sl] + cor * dot(eT, e3_ref[:, sl])) * silu(z)
        ss = ss + jnp.sum(v * v, axis=-1, keepdims=True)
        vs.append(v)
    sc = lax.rsqrt(ss / width + EPS)
    acc = u
    g = jnp.concatenate([(vs[t] * sc * sm_ref[t, 5:6, :]).astype(BF16) for t in range(n_tp)], axis=1)
    un = (u + dot(g, wob[...])).astype(BF16)
    f_ref[...] = un.astype(F32)
    if mix_out:
        o_ref[...] = un
    else:
        o_ref[...] = unmix(un.astype(F32), ubuf).astype(BF16)


def load_wo(wf_ref, wb_ref, n_dp, n_tp):
    rows = wb_ref.shape[0] // n_tp
    cols = wb_ref.shape[1] // n_dp
    for d in range(n_dp):
        for t in range(n_tp):
            wb_ref[t * rows:(t + 1) * rows, d * cols:(d + 1) * cols] = wf_ref[d * n_tp + t].astype(BF16)


def p2(u, off, nw, wz, wo, wsm, y, c, ac, s, e3, n, n_dp, n_tp, mix_in, mix_out, out_rows=None, interpret=False):
    d_model = u.shape[1]
    width = 256 * n_tp
    heads = width // 64
    rows = d_model // n_dp
    geom = (n_dp, n_tp, 64, width, heads)
    nb = n // BLK2
    full = lambda shp: pl.BlockSpec(shp, lambda i, o: (0,) * len(shp), pipeline_mode=pl.Buffered(1))
    gs = pltpu.PrefetchScalarGridSpec(
        num_scalar_prefetch=1, grid=(nb,),
        in_specs=[
            pl.BlockSpec((BLK2, d_model), lambda i, o: (o[0] + i, 0)),
            full((1, d_model)),
            full((n_dp * n_tp, rows, 256)), full((n_dp * n_tp, 256, d_model // n_dp)),
            pl.BlockSpec((n_tp, 32, 256), lambda i, o: (0, rows // 32, 0), pipeline_mode=pl.Buffered(1)),
            pl.BlockSpec((BLK2, width), lambda i, o: (i, 0)),
            pl.BlockSpec((BLK2, 128), lambda i, o: (i, 0)),
            pl.BlockSpec((heads, BLK2), lambda i, o: (0, i)),
            full((128, width)), full((3 * heads, width)),
        ],
        out_specs=[pl.BlockSpec((BLK2, d_model), lambda i, o: (o[1] + i, 0)), pl.BlockSpec((BLK2, d_model), lambda i, o: (i, 0))],
        scratch_shapes=[pltpu.VMEM((d_model, width), BF16), pltpu.VMEM((width, d_model), BF16),
                        pltpu.VMEM((3, 256, width), BF16), pltpu.VMEM((d_model // 128 * BLK2, 128), F32)])
    return pl.pallas_call(
        functools.partial(p2_body, geom=geom, mix_in=mix_in, mix_out=mix_out), grid_spec=gs, name="p2",
        out_shape=[jax.ShapeDtypeStruct((out_rows or n, d_model), BF16), jax.ShapeDtypeStruct((n, d_model), F32)],
        compiler_params=pltpu.CompilerParams(dimension_semantics=("arbitrary",), vmem_limit_bytes=60 << 20),
        cost_estimate=pl.CostEstimate(flops=n * 30_000_000, bytes_accessed=n * 12000, transcendentals=0),
        interpret=interpret,
    )(off, u, nw, wz, wo, wsm, y, c, ac, s, e3)


def fin_body(off_ref, buf_ref, f_ref, o_ref, ubuf):
    o_ref[...] = unmix(f_ref[...], ubuf).astype(BF16)


def finish(buf, f, off):
    n, d_model = f.shape
    rows = 512
    gs = pltpu.PrefetchScalarGridSpec(
        num_scalar_prefetch=1, grid=(n // rows,),
        in_specs=[pl.BlockSpec(memory_space=pl.ANY), pl.BlockSpec((rows, d_model), lambda i, o: (i, 0))],
        out_specs=pl.BlockSpec((rows, d_model), lambda i, o: (o[0] + i, 0)),
        scratch_shapes=[pltpu.VMEM((d_model // 128 * rows, 128), F32)])
    return pl.pallas_call(
        fin_body, grid_spec=gs, name="finish", out_shape=jax.ShapeDtypeStruct(buf.shape, BF16),
        input_output_aliases={1: 0},
        compiler_params=pltpu.CompilerParams(dimension_semantics=("arbitrary",)),
        cost_estimate=pl.CostEstimate(flops=n * d_model, bytes_accessed=n * d_model * 6, transcendentals=0),
    )(off, buf, f)


from jax.sharding import PartitionSpec as P


def small_rows(conv, bias, gate, skip, dtb, al, wdt):
    f = lambda v: v.astype(F32)
    hp = skip.shape[0]
    return jnp.concatenate([
        f(conv), f(bias)[None], f(gate)[None], jnp.repeat(skip, 256 // hp)[None], jnp.zeros((1, 256), F32),
        jnp.broadcast_to(dtb[:, None], (hp, 256)), jnp.broadcast_to((-jnp.exp(al) * LOG2E)[:, None], (hp, 256)),
        f(wdt).T.reshape(-1, 256)], axis=0)


def solution(mesh):
    n_tp, n_dp = mesh.shape['tp'], mesh.shape['dp']
    rep, col, vec = P(), P(None, None, 'tp'), P(None, 'tp')
    in_specs = (P('dp'), rep, col, col, rep, col, col, rep, vec, rep, vec, vec, vec, vec, P(None, 'tp', None))

    def device_forward(hidden, norm_w, w_z, w_x, w_bc, w_dt, conv_x, conv_bc, bias_x, bias_bc, dt_bias, a_log, d_skip, gate_w, w_out):
        u = hidden[0]
        steps, d_model = u.shape
        heads = dt_bias.shape[1] * n_tp
        n = steps // 2
        dp, tp = lax.axis_index('dp'), lax.axis_index('tp')
        core = tp % 2
        rows, ocols = d_model // n_dp, d_model // n_dp
        gather = lambda v: lax.all_gather(v, ('dp', 'tp'))
        e3 = expand_mat(heads)
        up = [(2 * k, 2 * k + 1) for k in range(n_tp // 2)]
        swap = [(k, k ^ 1) for k in range(n_tp)]
        wxs, wzs, wos = [], [], []
        for l in range(2):
            sm = small_rows(conv_x[l], bias_x[l], gate_w[l], d_skip[l], dt_bias[l], a_log[l], w_dt[l])
            qx = lax.dynamic_slice(w_x[l], (dp * rows, 0), (rows, 256)).astype(F32)
            wxs.append(gather(jnp.concatenate([qx, sm], axis=0)))
            wzs.append(gather(lax.dynamic_slice(w_z[l], (dp * rows, 0), (rows, 256)).astype(F32)))
            wos.append(gather(lax.dynamic_slice(w_out[l], (0, dp * ocols), (256, ocols)).astype(F32)))
        cur = u
        off = jnp.stack([core * (n // BLK), 0 * core])
        zero = jnp.zeros((2,), jnp.int32)
        tail = u[n - 64:n].astype(F32).reshape(8, 8, d_model).transpose(1, 0, 2).reshape(64, d_model)[40:]
        halo = jnp.where(core == 1, tail, 0.0)
        for l in range(2):
            nw = norm_w[l].astype(F32)[None]
            y, c, ac, s_end = p1(cur, off, halo, nw, wxs[l], w_bc[l], conv_bc[l].astype(F32), bias_bc[l].astype(F32)[None], e3, n, n_dp, n_tp, l > 0)
            s = lax.ppermute(s_end, 'tp', up)
            off2 = jnp.stack([core, 0 * core] if l == 0 else [0 * core, core]) * (n // BLK2)
            o, f = p2(cur, off2, nw, wzs[l], wos[l], wxs[l], y, c, ac, s, e3, n, n_dp, n_tp, l > 0, l == 0, out_rows=n if l == 0 else steps)
            cur, off = o, zero
            if l == 0:
                halo = lax.ppermute(f[n - 24:], 'tp', up)
        other = lax.ppermute(f, 'tp', swap)
        return finish(o, other, jnp.reshape((1 - core) * (n // 512), (1,)))[None]

    return jax.shard_map(device_forward, mesh=mesh, in_specs=in_specs, out_specs=P('dp'), check_vma=False)
```

time: 600 us -> 595 us (level)
  Pallas kernels: 441 us -> 331 us
  waiting for transfers between devices: 108 us -> 211 us
    pallas_call x4, Pallas kernels: 433 us -> 322 us  [the longest x2 203 us: p1(): pl.pallas_call(functools.partial(p1_body, geom=geom, mixed=mixed), grid_s...]
    all_gather x6, waiting for transfers between devices: 89.3 us -> 192 us  [device_forward(): gather = lambda v: lax.all_gather(v, ('dp', 'tp'))]
  transfers between devices with their start and end apart: 10 -> 10, of which waited for: 5 -> 5; matrix products, arithmetic and copies ran while one was open for 3% -> 3% of each run, Pallas kernels for 61% -> 44%
where the time goes in v2:
time: 595 us; the launch traced here: 594 us
  Pallas kernels  331 us (56%)
  waiting for transfers between devices  211 us (35%)
  local copies, waits for them, and re-layouts  18.7 us (3%)
  between operations  13.7 us (2%)
  other arithmetic  11.8 us (2%)
  starting transfers between devices  7.54 us (1%)
    pallas_call x2, Pallas kernels, p1(): pl.pallas_call(functools.partial(p1_body, geom=geom, mixed=mixed), grid_s...  203 us
    all_gather x6, waiting for transfers between devices, device_forward(): gather = lambda v: lax.all_gather(v, ('dp', 'tp'))  192 us
    pallas_call x2, Pallas kernels, p2(): pl.pallas_call(functools.partial(p2_body, geom=geom, mix_in=mix_in, mix_o...  119 us
    ppermute x1, waiting for transfers between devices, device_forward(): other = lax.ppermute(f, 'tp', swap)  18.9 us
  transfers between devices with their start and end apart: 10, of which 5 were waited for; matrix products, arithmetic and copies ran while one was open for 3% of the time, Pallas kernels for 44%

profile of v2, /device:TPU:0, one launch (start us, length us, event | category | flops | bytes accessed | tf_op | source)
XLA Modules:
  0.0 594.2 jit_solution(7809329165656635607)
XLA Ops:
  6.5 0.0 all-gather.17.cloned.1.call-start
  6.6 1.4 fusion.2
  7.9 0.7 convert_bitcast_fusion
  8.7 0.7 bitcast_convert_fusion.3
  9.4 0.8 slice_bitcast_fusion.3
  10.1 0.8 multiply_bitcast_fusion
  10.9 0.8 slice_bitcast_fusion.4
  11.7 0.1 broadcast_in_dim.26
  11.7 0.1 broadcast_in_dim_reshape.6
  11.8 0.8 slice_convert_fusion.3
  12.6 0.1 broadcast_in_dim.28
  12.7 0.1 broadcast_in_dim.56
  12.8 2.6 concatenate.9
  15.3 0.0 all-gather.17.cloned.1.call-update
  15.3 0.0 all-gather.11.cloned.1.call-start
  15.4 2.1 fusion.3
  17.4 0.7 dynamic-slice_convert_fusion.2
  18.2 0.0 all-gather.11.cloned.1.call-update
  18.2 0.0 all-gather.9.cloned.1.call-start
  18.2 1.3 fusion.4
  19.5 0.7 dynamic-slice_convert_fusion.3
  20.3 0.0 all-gather.19.cloned.1.call-start
  20.3 0.1 broadcast_in_dim.60
  20.4 0.1 broadcast_in_dim_reshape.7
  20.5 0.1 broadcast_in_dim.62
  20.6 0.1 broadcast_in_dim.63
  20.6 2.5 concatenate.11
  23.2 0.0 all-gather.13.cloned.1.call-start
  23.3 0.7 dynamic-slice_convert_fusion.1
  24.0 0.0 all-gather.15.cloned.1.call-start
  24.1 0.9 slice_bitcast_fusion.2
  25.0 0.1 copy.21
  25.1 0.7 pad_clamp_fusion
  25.8 0.6 gather_fusion
  26.4 0.2 broadcast_in_dim.59
  26.6 0.3 reshape.77
  26.9 0.6 slice_convert_fusion
  27.6 1.1 slice_bitcast_fusion
  28.7 0.6 bitcast_convert_fusion.2
  29.3 0.6 slice_convert_fusion.2
  29.9 0.6 select_bitcast_fusion.halo_ref
  30.5 0.7 pad_add_fusion.off_ref
  31.2 68.6 %all-gather.17.cloned.1.call-done = f32[9216,256]{1,0:T(8,128)} async-done(((f32[288,256]{1,0:T(8,128)}), f32[9216,256]{1,0:T(8,128)}) %all-gather.17.cloned.1.call-update) | async-done | bytes 9437200 | tf_op jit(solution)/shard_map/all_gather | solution.py:432
  99.7 102.6 %p1.2 = (f32[3072,2048]{1,0:T(8,128)}, f32[3072,128]{1,0:T(8,128)}, f32[32,3072]{1,0:T(8,128)}, f32[128,2048]{1,0:T(8,128)}) custom-call(s32[2]{0:T(128)} %pad_add_fusion.off_ref, bf16[6144,1024]{1,0:T(8,128)(2,1)} %bitcast.59, f32[24,1024]{1,0:T(8,128)} %select_bitcast_fusion.halo_ref, f32[1,1024]{1,0:T(1,128)} %get-tuple-element.44.nw_ref, ...), custom_call_target="tpu_custom_call" | custom-call | flops 215040000000 | bytes 36864000 | tf_op jit(solution)/shard_map/p1/pallas_call | solution.py:291
  202.3 2.4 collective-permute-start
  204.8 0.6 fusion.1.off_ref
  205.4 52.3 %all-gather.9.cloned.1.call-done.wz_ref = f32[32,256,256]{2,1,0:T(8,128)} async-done(((f32[1,256,256]{2,1,0:T(8,128)}), f32[32,256,256]{2,1,0:T(8,128)}) %all-gather.9.cloned.1.call-update) | async-done | bytes 8388624 | tf_op jit(solution)/shard_map/all_gather | solution.py:432
  257.7 1.0 copy-done.6
  258.7 59.6 %p2.2 = (bf16[3072,1024]{1,0:T(8,128)(2,1)}, f32[3072,1024]{1,0:T(8,128)}) custom-call(s32[2]{0:T(128)} %fusion.1.off_ref, bf16[6144,1024]{1,0:T(8,128)(2,1)} %bitcast.60, f32[1,1024]{1,0:T(1,128)} %get-tuple-element.44.nw_ref, f32[32,256,256]{2,1,0:T(8,128)} %all-gather.9.cloned.1.call-done.wz_ref, f32[32,256,256]{2,1,0:T(8,128)} %all-gather.11.cloned.1.call-done.wo_ref, ...), custom_call_target="tpu_custom_call" | custom-call | flops 92160000000 | bytes 36864000 | tf_op jit(solution)/shard_map/p2/pallas_call | solution.py:378
  318.3 0.9 slice.126
  319.2 2.1 collective-permute-start.1
  321.4 1.7 dynamic-slice_convert_fusion
  323.0 18.0 %all-gather.19.cloned.1.call-done = f32[9216,256]{1,0:T(8,128)} async-done(((f32[288,256]{1,0:T(8,128)}), f32[9216,256]{1,0:T(8,128)}) %all-gather.19.cloned.1.call-update) | async-done | bytes 9437200 | tf_op jit(solution)/shard_map/all_gather | solution.py:432
  341.0 0.5 broadcast_5_off_ref.2.off_ref
  341.5 0.1 copy-done.7
  341.6 100.7 %p1.3 = (f32[3072,2048]{1,0:T(8,128)}, f32[3072,128]{1,0:T(8,128)}, f32[32,3072]{1,0:T(8,128)}, f32[128,2048]{1,0:T(8,128)}) custom-call(s32[2]{0:T(128)} %broadcast_5_off_ref.2.off_ref, bf16[3072,1024]{1,0:T(8,128)(2,1)} %get-tuple-element.21.u_ref, f32[24,1024]{1,0:T(8,128)} %copy-done.7, f32[1,1024]{1,0:T(1,128)} %get-tuple-element.43.nw_ref, ...), custom_call_target="tpu_custom_call" | custom-call | flops 215040000000 | bytes 36864000 | tf_op jit(solution)/shard_map/p1/pallas_call | solution.py:291
  442.3 2.4 collective-permute-start.2
  444.8 0.6 add_multiply_fusion.off_ref
  445.4 53.3 %all-gather.15.cloned.1.call-done.wo_ref = f32[32,256,256]{2,1,0:T(8,128)} async-done(((f32[1,256,256]{2,1,0:T(8,128)}), f32[32,256,256]{2,1,0:T(8,128)}) %all-gather.15.cloned.1.call-update) | async-done | bytes 8388624 | tf_op jit(solution)/shard_map/all_gather | solution.py:432
  498.6 1.0 copy-done.5
  499.6 59.1 %p2.3 = (bf16[6144,1024]{1,0:T(8,128)(2,1)}, f32[3072,1024]{1,0:T(8,128)}) custom-call(s32[2]{0:T(128)} %add_multiply_fusion.off_ref, bf16[3072,1024]{1,0:T(8,128)(2,1)} %get-tuple-element.21.u_ref, f32[1,1024]{1,0:T(1,128)} %get-tuple-element.43.nw_ref, f32[32,256,256]{2,1,0:T(8,128)} %all-gather.13.cloned.1.call-done.wz_ref, ...), custom_call_target="tpu_custom_call" | custom-call | flops 92160000000 | bytes 36864000 | tf_op jit(solution)/shard_map/p2/pallas_call | solution.py:378
  558.7 0.3 collective-permute-start.3
  559.0 18.9 %collective-permute-done.3.f_ref = f32[3072,1024]{1,0:T(8,128)} collective-permute-done((f32[3072,1024]{1,0:T(8,128)}, f32[3072,1024]{1,0:T(8,128)}, u32[]{:S(2)}, u32[]{:S(2)}) %collective-permute-start.3) | collective-permute-done | bytes 12582944 | tf_op jit(solution)/shard_map/ppermute | solution.py:457
  577.8 9.5 %finish.1 = bf16[6144,1024]{1,0:T(8,128)(2,1)} custom-call(s32[1]{0:T(128)} %bitcast.off_ref, bf16[6144,1024]{1,0:T(8,128)(2,1)} %get-tuple-element.27.buf_ref, f32[3072,1024]{1,0:T(8,128)} %collective-permute-done.3.f_ref), custom_call_target="tpu_custom_call", output_to_operand_aliasing={{}: (1, {})} | custom-call | flops 3145728 | bytes 18874368 | tf_op jit(solution)/shard_map/finish/pallas_call | solution.py:399
  (31 shorter events, 0.2 us)
Async XLA Ops:
  6.5 20.4 %copy-start.2 = (bf16[2,1024]{1,0:T(2,128)(2,1)S(1)}, bf16[2,1024]{1,0:T(2,128)(2,1)}, u32[]{:S(2)}) copy-start(bf16[2,1024]{1,0:T(2,128)(2,1)} %param.17) | copy-start | bytes 12292
  6.5 21.0 %copy-start = (bf16[2,1024,256]{2,1,0:T(8,128)(2,1)S(1)}, bf16[2,1024,256]{2,1,0:T(8,128)(2,1)}, u32[]{:S(2)}) copy-start(bf16[2,1024,256]{2,1,0:T(8,128)(2,1)} %param.20) | copy-start | bytes 3145732
  6.5 22.1 %copy-start.3 = (bf16[2,4,256]{2,1,0:T(4,128)(2,1)S(1)}, bf16[2,4,256]{2,1,0:T(4,128)(2,1)}, u32[]{:S(2)}) copy-start(bf16[2,4,256]{2,1,0:T(4,128)(2,1)} %param.23) | copy-start | bytes 12292
  6.5 22.8 %copy-start.4 = (bf16[2,256]{1,0:T(2,128)(2,1)S(1)}, bf16[2,256]{1,0:T(2,128)(2,1)}, u32[]{:S(2)}) copy-start(bf16[2,256]{1,0:T(2,128)(2,1)} %param.25) | copy-start | bytes 3076
  6.5 93.2 %all-gather.17.cloned.1.call-start = ((), (), s32[]{:S(2)}) async-start(), calls=%async_computation.4 | async-start | bytes 9732096 | tf_op jit(solution)/shard_map/all_gather | solution.py:432
  15.3 190.0 %all-gather.11.cloned.1.call-start = ((), (), s32[]{:S(2)}) async-start(), calls=%async_computation.1 | async-start | bytes 8650752 | tf_op jit(solution)/shard_map/all_gather | solution.py:432
  18.2 239.5 %all-gather.9.cloned.1.call-start = ((), (), s32[]{:S(2)}) async-start(), calls=%async_computation | async-start | bytes 8650752 | tf_op jit(solution)/shard_map/all_gather | solution.py:432
  20.3 320.7 %all-gather.19.cloned.1.call-start = ((), (), s32[]{:S(2)}) async-start(), calls=%async_computation.5 | async-start | bytes 9732096 | tf_op jit(solution)/shard_map/all_gather | solution.py:432
  23.2 422.2 %all-gather.13.cloned.1.call-start = ((), (), s32[]{:S(2)}) async-start(), calls=%async_computation.2 | async-start | bytes 8650752 | tf_op jit(solution)/shard_map/all_gather | solution.py:432
  24.0 474.6 %all-gather.15.cloned.1.call-start = ((), (), s32[]{:S(2)}) async-start(), calls=%async_computation.3 | async-start | bytes 8650752 | tf_op jit(solution)/shard_map/all_gather | solution.py:432
  26.9 72.8 %copy-start.1 = (bf16[96,2048]{1,0:T(8,128)(2,1)}, bf16[96,2048]{1,0:T(8,128)(2,1)S(1)}, u32[]{:S(2)}) copy-start(bf16[96,2048]{1,0:T(8,128)(2,1)S(1)} %constant_dynamic-update-slice_fusion.e3_ref) | copy-start | bytes 1179652
  202.3 55.3 %collective-permute-start = (f32[128,2048]{1,0:T(8,128)}, f32[128,2048]{1,0:T(8,128)S(1)}, u32[]{:S(2)}, u32[]{:S(2)}) collective-permute-start(f32[128,2048]{1,0:T(8,128)} %get-tuple-element.20), channel_id=1, source_target_pairs={{0,1},{2,3},{4,5},{6,7},{8,9},{10,11},{12,13},{14,15},{16,17},{18,... | collective-permute-start | bytes 3145736 | tf_op jit(solution)/shard_map/ppermute | solution.py:451
  257.7 1.0 copy-start.6
  319.2 21.8 %collective-permute-start.1 = (f32[24,1024]{1,0:T(8,128)S(1)}, f32[24,1024]{1,0:T(8,128)S(1)}, u32[]{:S(2)}, u32[]{:S(2)}) collective-permute-start(f32[24,1024]{1,0:T(8,128)S(1)} %slice.126), channel_id=1, source_target_pairs={{0,1},{2,3},{4,5},{6,7},{8,9},{10,11},{12,13},{14,15},{16,17},{18,... | collective-permute-start | bytes 294920 | tf_op jit(solution)/shard_map/ppermute | solution.py:456
  341.0 0.6 copy-start.7
  442.3 56.3 %collective-permute-start.2 = (f32[128,2048]{1,0:T(8,128)}, f32[128,2048]{1,0:T(8,128)S(1)}, u32[]{:S(2)}, u32[]{:S(2)}) collective-permute-start(f32[128,2048]{1,0:T(8,128)} %get-tuple-element.26), channel_id=1, source_target_pairs={{0,1},{2,3},{4,5},{6,7},{8,9},{10,11},{12,13},{14,15},{16,17},{18,... | collective-permute-start | bytes 3145736 | tf_op jit(solution)/shard_map/ppermute | solution.py:451
  498.6 1.0 copy-start.5
  558.7 19.2 %collective-permute-start.3 = (f32[3072,1024]{1,0:T(8,128)}, f32[3072,1024]{1,0:T(8,128)}, u32[]{:S(2)}, u32[]{:S(2)}) collective-permute-start(f32[3072,1024]{1,0:T(8,128)} %get-tuple-element.28), channel_id=1, source_target_pairs={{0,1},{1,0},{2,3},{3,2},{4,5},{5,4},{6,7},{7,6},{8,9},{9,8},{10,11... | collective-permute-start | bytes 37748744 | tf_op jit(solution)/shard_map/ppermute | solution.py:457
Sparse Core Ops, SparseCore 0:
  15.4 84.2 all-gather.16
  102.7 75.8 all-gather.10
  181.7 75.9 all-gather.8
  260.6 80.3 all-gather.18
  343.8 75.8 all-gather.12
  422.6 76.0 all-gather.14

commit v3 on v2

--- a/solution.py
+++ b/solution.py
@@ -404,6 +404,106 @@
     )(off, buf, f)
 
 
+class Gather:
+    N_SEM = 17
+
+    def __init__(self, a, g, send, recv, base):
+        self.a, self.g, self.send, self.recv, self.base = a, g, send, recv, base
+        dp, tp = lax.axis_index('dp'), lax.axis_index('tp')
+        x, y, z, c = dp // 2, dp % 2, tp // 2, tp % 2
+        self.dp, self.tp, self.z, self.c = dp, tp, z, c
+        self.plane = [(1 - x) * 2 + y, x * 2 + 1 - y, (1 - x) * 2 + 1 - y]
+        self.partner = (dp, 2 * z + 1 - c)
+
+    def slot(self, dz):
+        return 2 * ((self.z + 4 - dz) % 4) + self.c
+
+    def rdma(self, k, src, dst, dev):
+        return pltpu.make_async_remote_copy(src_ref=src, dst_ref=dst, send_sem=self.send.at[self.base + k],
+                                            recv_sem=self.recv.at[self.base + k], device_id=dev,
+                                            device_id_type=pl.DeviceIdType.MESH)
+
+    def local(self):
+        return pltpu.make_async_copy(self.a, self.g.at[:, self.tp], self.send.at[self.base])
+
+    def own(self):
+        return self.rdma(1, self.a, self.g.at[:, self.tp], self.partner)
+
+    def line(self, dz):
+        return self.rdma(1 + dz, self.a.at[self.dp], self.g.at[self.dp, self.tp], (self.dp, 2 * ((self.z + dz) % 4) + self.c))
+
+    def cross(self, dz, n):
+        s = self.slot(dz)
+        return self.rdma(2 + 3 * dz + n, self.g.at[self.dp, s], self.g.at[self.dp, s], (self.plane[n], self.tp))
+
+    def over(self, dz):
+        s = self.slot(dz)
+        return self.rdma(13 + dz, self.g.at[:, s], self.g.at[:, s], self.partner)
+
+    def peers(self):
+        return [(self.dp, 2 * ((self.z + dz) % 4) + self.c) for dz in (1, 2, 3)] + [(p, self.tp) for p in self.plane] + [self.partner]
+
+    def step0(self):
+        for dz in (1, 3, 2):
+            self.line(dz).start()
+        self.own().start()
+        self.local().start()
+
+    def step1(self, dz):
+        self.line(dz).wait_recv()
+        for n in range(3):
+            self.cross(dz, n).start()
+
+    def step2(self, dz):
+        for n in range(3):
+            self.cross(dz, n).wait_recv()
+        self.over(dz).start()
+
+    def step3(self):
+        self.local().wait()
+        self.own().wait()
+        for dz in (1, 2, 3):
+            self.line(dz).wait_send()
+            for n in range(3):
+                self.cross(dz, n).wait_send()
+            self.over(dz).wait()
+
+
+def entry_barrier(peers):
+    sem = pltpu.get_barrier_semaphore()
+    for p in peers:
+        pl.semaphore_signal(sem, inc=1, device_id=p, device_id_type=pl.DeviceIdType.MESH)
+    pl.semaphore_wait(sem, len(peers))
+
+
+def gather_body(*refs, n):
+    ins, outs, (send, recv) = refs[:n], refs[n:2 * n], refs[2 * n:]
+    gs = [Gather(a, g, send, recv, Gather.N_SEM * k) for k, (a, g) in enumerate(zip(ins, outs))]
+    entry_barrier(gs[0].peers())
+    for g in gs:
+        g.step0()
+    for g in gs:
+        for dz in (1, 3, 2):
+            g.step1(dz)
+    for g in gs:
+        for dz in (1, 3, 2):
+            g.step2(dz)
+    for g in gs:
+        g.step3()
+
+
+def gather_all(shards, n_tp, cid):
+    n = len(shards)
+    return pl.pallas_call(
+        functools.partial(gather_body, n=n), name="gather",
+        out_shape=[jax.ShapeDtypeStruct((s.shape[0], n_tp) + s.shape[1:], F32) for s in shards],
+        in_specs=[pl.BlockSpec(memory_space=pl.ANY)] * n, out_specs=[pl.BlockSpec(memory_space=pl.ANY)] * n,
+        scratch_shapes=[pltpu.SemaphoreType.DMA((Gather.N_SEM * n,)), pltpu.SemaphoreType.DMA((Gather.N_SEM * n,))],
+        compiler_params=pltpu.CompilerParams(collective_id=cid, has_side_effects=True),
+        cost_estimate=pl.CostEstimate(flops=10 ** 10, bytes_accessed=n * 16 * 10 ** 6, transcendentals=0),
+    )(*shards)
+
+
 from jax.sharding import PartitionSpec as P
 
 
@@ -433,13 +533,22 @@
         e3 = expand_mat(heads)
         up = [(2 * k, 2 * k + 1) for k in range(n_tp // 2)]
         swap = [(k, k ^ 1) for k in range(n_tp)]
-        wxs, wzs, wos = [], [], []
-        for l in range(2):
-            sm = small_rows(conv_x[l], bias_x[l], gate_w[l], d_skip[l], dt_bias[l], a_log[l], w_dt[l])
-            qx = lax.dynamic_slice(w_x[l], (dp * rows, 0), (rows, 256)).astype(F32)
-            wxs.append(gather(jnp.concatenate([qx, sm], axis=0)))
-            wzs.append(gather(lax.dynamic_slice(w_z[l], (dp * rows, 0), (rows, 256)).astype(F32)))
-            wos.append(gather(lax.dynamic_slice(w_out[l], (0, dp * ocols), (256, ocols)).astype(F32)))
+        def cut(w):
+            return w.reshape(n_dp, rows, 256).astype(F32)
+
+        def cut_o(w):
+            return w.reshape(256, n_dp, ocols).transpose(1, 0, 2).astype(F32)
+
+        sm = [small_rows(conv_x[l], bias_x[l], gate_w[l], d_skip[l], dt_bias[l], a_log[l], w_dt[l]) for l in range(2)]
+        sx = [jnp.concatenate([cut(w_x[l]), jnp.broadcast_to(sm[l], (n_dp,) + sm[l].shape)], axis=1) for l in range(2)]
+        wxs, wzs, wos = [None, None], [None, None], [None, None]
+        wxs[0], wzs[0], wos[0] = gather_all([sx[0], cut(w_z[0]), cut_o(w_out[0])], n_tp, 1)
+        part = lambda v: lax.dynamic_index_in_dim(v, dp, 0, keepdims=False)
+        wxs[1] = gather(part(sx[1]))
+        wzs[1] = gather(part(cut(w_z[1])))
+        wos[1] = gather(part(cut_o(w_out[1])))
+        flat = lambda v: v.reshape((n_dp * n_tp,) + v.shape[2:])
+        wxs[0], wzs[0], wos[0] = flat(wxs[0]), flat(wzs[0]), flat(wos[0])
         cur = u
         off = jnp.stack([core * (n // BLK), 0 * core])
         zero = jnp.zeros((2,), jnp.int32)

time: 595 us -> 558 us (0.938)
  waiting for transfers between devices: 211 us -> 21.7 us
  Pallas kernels: 331 us -> 487 us
    all_gather x6 -> x3, waiting for transfers between devices: 192 us -> 0.02 us  [device_forward(): gather = lambda v: lax.all_gather(v, ('dp', 'tp'))]
    pallas_call x0 -> x1, Pallas kernels: none -> 156 us  [gather_all(): pl.pallas_call(functools.partial(gather_body, n=n), name='gather', out_sh...]
  transfers between devices with their start and end apart: 10 -> 7, of which waited for: 5 -> 3; matrix products, arithmetic and copies ran while one was open for 3% -> 3% of each run, Pallas kernels for 44% -> 75%
where the time goes in v3:
time: 558 us
  Pallas kernels  487 us (87%)
  waiting for transfers between devices  21.7 us (4%)
  local copies, waits for them, and re-layouts  15.1 us (3%)
  between operations  13.4 us (2%)
  other arithmetic  13.3 us (2%)
  starting transfers between devices  7.04 us (1%)
    pallas_call x2, Pallas kernels, p1(): pl.pallas_call(functools.partial(p1_body, geom=geom, mixed=mixed), grid_s...  203 us
    pallas_call x1, Pallas kernels, gather_all(): pl.pallas_call(functools.partial(gather_body, n=n), name='gather', out_sh...  156 us
    pallas_call x2, Pallas kernels, p2(): pl.pallas_call(functools.partial(p2_body, geom=geom, mix_in=mix_in, mix_o...  119 us
    ppermute x1, waiting for transfers between devices, device_forward(): other = lax.ppermute(f, 'tp', swap)  18.8 us
  transfers between devices with their start and end apart: 7, of which 3 were waited for; matrix products, arithmetic and copies ran while one was open for 3% of the time, Pallas kernels for 75%

profile of v3, /device:TPU:0, one launch (start us, length us, event | category | flops | bytes accessed | tf_op | source)
XLA Modules:
  0.0 557.7 jit_solution(17561956802311629388)
XLA Ops:
  6.5 0.7 convert_bitcast_fusion
  7.3 0.7 bitcast_convert_fusion.1
  8.0 0.8 slice_bitcast_fusion.3
  8.7 0.8 multiply_bitcast_fusion
  9.5 0.8 slice_bitcast_fusion.4
  10.2 1.3 fusion.3
  11.5 0.1 broadcast_in_dim.67
  11.6 0.1 broadcast_in_dim_reshape.7
  11.7 0.1 convert.27
  11.8 0.8 slice_convert_fusion.4
  12.6 0.1 broadcast_in_dim.69
  12.6 0.1 broadcast_in_dim.70
  12.8 0.8 fusion
  13.5 0.0 all-gather.7.cloned.1.call-update
  13.5 0.0 all-gather.9.cloned.1.call-start
  13.6 1.3 slice_convert_fusion
  14.9 0.5 reshape.102
  15.4 0.2 constant_dynamic-slice_fusion
  15.7 0.7 copy.29
  16.4 0.0 all-gather.9.cloned.1.call-update
  16.4 0.0 all-gather.5.cloned.1.call-start
  16.5 0.9 slice_bitcast_fusion.2
  17.4 0.1 copy.31
  17.5 0.1 broadcast_in_dim.30
  17.6 0.1 broadcast_in_dim_reshape.6
  17.7 0.1 convert.20
  17.8 0.2 copy.28
  18.0 1.2 copy.25
  19.2 2.1 fusion.4
  21.3 1.0 convert.23.refs_1_
  22.3 0.6 gather_fusion
  22.9 0.2 broadcast_in_dim.66
  23.1 0.3 reshape.92
  23.5 0.7 slice_convert_fusion.1
  24.1 1.1 slice_bitcast_fusion
  25.2 0.6 bitcast_convert_fusion
  25.8 0.6 slice_convert_fusion.3
  26.4 0.6 select_bitcast_fusion.halo_ref
  27.0 0.6 pad_add_fusion.off_ref
  27.6 0.1 broadcast_in_dim.61
  27.7 0.1 broadcast_in_dim.62
  27.8 1.1 pad_maximum_fusion.refs_0_
  28.9 155.8 %gather.7 = (f32[4,8,288,256]{3,2,1,0:T(8,128)}, f32[4,8,256,256]{3,2,1,0:T(8,128)}, f32[4,8,256,256]{3,2,1,0:T(8,128)}) custom-call(f32[4,288,256]{2,1,0:T(8,128)} %pad_maximum_fusion.refs_0_, f32[4,256,256]{2,1,0:T(8,128)} %convert.23.refs_1_, f32[4,256,256]{2,1,0:T(8,128)} %bitcast.69), custom_call_target="tpu_custom_call" | custom-call | flops 10000000000 | bytes 48000000 | tf_op jit(solution)/shard_map/gather/pallas_call | solution.py:497
  184.7 102.6 %p1.2 = (f32[3072,2048]{1,0:T(8,128)}, f32[3072,128]{1,0:T(8,128)}, f32[32,3072]{1,0:T(8,128)}, f32[128,2048]{1,0:T(8,128)}) custom-call(s32[2]{0:T(128)} %pad_add_fusion.off_ref, bf16[6144,1024]{1,0:T(8,128)(2,1)} %bitcast.72, f32[24,1024]{1,0:T(8,128)} %select_bitcast_fusion.halo_ref, f32[1,1024]{1,0:T(1,128)} %get-tuple-element.50.nw_ref, ...), custom_call_target="tpu_custom_call" | custom-call | flops 215040000000 | bytes 36864000 | tf_op jit(solution)/shard_map/p1/pallas_call | solution.py:291
  287.4 2.5 collective-permute-start
  289.8 0.6 fusion.2.off_ref
  290.4 1.4 collective-permute-done.s_ref
  291.9 1.0 copy-done.7
  292.9 59.6 %p2.2 = (bf16[3072,1024]{1,0:T(8,128)(2,1)}, f32[3072,1024]{1,0:T(8,128)}) custom-call(s32[2]{0:T(128)} %fusion.2.off_ref, bf16[6144,1024]{1,0:T(8,128)(2,1)} %bitcast.73, f32[1,1024]{1,0:T(1,128)} %get-tuple-element.50.nw_ref, f32[32,256,256]{2,1,0:T(8,128)} %bitcast.78, f32[32,256,256]{2,1,0:T(8,128)} %bitcast.79, f32[32,288,256]{2,1,0:T(8,128)} %bitcast.77, ...), custom_call_target="tpu_custom_call" | custom-call | flops 92160000000 | bytes 36864000 | tf_op jit(solution)/shard_map/p2/pallas_call | solution.py:378
  352.5 0.9 slice.126
  353.4 2.3 collective-permute-start.1
  355.6 1.7 dynamic-slice_convert_fusion
  357.3 0.0 all-gather.7.cloned.1.call-done.wf_ref.sm_ref
  357.4 0.6 broadcast_5_off_ref.2.off_ref
  358.0 0.0 copy-done.8
  358.0 100.7 %p1.3 = (f32[3072,2048]{1,0:T(8,128)}, f32[3072,128]{1,0:T(8,128)}, f32[32,3072]{1,0:T(8,128)}, f32[128,2048]{1,0:T(8,128)}) custom-call(s32[2]{0:T(128)} %broadcast_5_off_ref.2.off_ref, bf16[3072,1024]{1,0:T(8,128)(2,1)} %get-tuple-element.27.u_ref, f32[24,1024]{1,0:T(8,128)} %copy-done.8, f32[1,1024]{1,0:T(1,128)} %get-tuple-element.49.nw_ref, ...), custom_call_target="tpu_custom_call" | custom-call | flops 215040000000 | bytes 36864000 | tf_op jit(solution)/shard_map/p1/pallas_call | solution.py:291
  458.7 1.8 collective-permute-start.2
  460.4 0.6 add_multiply_fusion.off_ref
  461.0 1.4 collective-permute-done.2.s_ref
  462.4 1.0 copy-done.6
  463.4 59.1 %p2.3 = (bf16[6144,1024]{1,0:T(8,128)(2,1)}, f32[3072,1024]{1,0:T(8,128)}) custom-call(s32[2]{0:T(128)} %add_multiply_fusion.off_ref, bf16[3072,1024]{1,0:T(8,128)(2,1)} %get-tuple-element.27.u_ref, f32[1,1024]{1,0:T(1,128)} %get-tuple-element.49.nw_ref, f32[32,256,256]{2,1,0:T(8,128)} %all-gather.5.cloned.1.call-done.wz_ref, f32[32,256,256]{2,1,0:T(8,128)} %bitcast.74, ...), custom_call_target="tpu_custom_call" | custom-call | flops 92160000000 | bytes 36864000 | tf_op jit(solution)/shard_map/p2/pallas_call | solution.py:378
  522.5 0.4 collective-permute-start.3
  522.9 18.8 %collective-permute-done.3.f_ref = f32[3072,1024]{1,0:T(8,128)} collective-permute-done((f32[3072,1024]{1,0:T(8,128)}, f32[3072,1024]{1,0:T(8,128)}, u32[]{:S(2)}, u32[]{:S(2)}) %collective-permute-start.3) | collective-permute-done | bytes 12582944 | tf_op jit(solution)/shard_map/ppermute | solution.py:566
  541.7 9.5 %finish.1 = bf16[6144,1024]{1,0:T(8,128)(2,1)} custom-call(s32[1]{0:T(128)} %bitcast.off_ref, bf16[6144,1024]{1,0:T(8,128)(2,1)} %get-tuple-element.33.buf_ref, f32[3072,1024]{1,0:T(8,128)} %collective-permute-done.3.f_ref), custom_call_target="tpu_custom_call", output_to_operand_aliasing={{}: (1, {})} | custom-call | flops 3145728 | bytes 18874368 | tf_op jit(solution)/shard_map/finish/pallas_call | solution.py:399
  (32 shorter events, 0.3 us)
Async XLA Ops:
  6.5 350.8 %all-gather.7.cloned.1.call-start = ((), (), s32[]{:S(2)}) async-start(), calls=%async_computation.1 | async-start | bytes 9732096 | tf_op jit(solution)/shard_map/all_gather | solution.py:532
  11.8 10.5 %copy-start.5 = (s32[32]{0:T(128)S(1)}, s32[32]{0:T(128)}, u32[]{:S(2)}) copy-start(s32[32]{0:T(128)} %constant.62) | copy-start | bytes 388
  13.5 9.9 %copy-start.2 = (bf16[2,1024]{1,0:T(2,128)(2,1)S(1)}, bf16[2,1024]{1,0:T(2,128)(2,1)}, u32[]{:S(2)}) copy-start(bf16[2,1024]{1,0:T(2,128)(2,1)} %param.17) | copy-start | bytes 12292
  13.5 447.5 %all-gather.9.cloned.1.call-start = ((), (), s32[]{:S(2)}) async-start(), calls=%async_computation.2 | async-start | bytes 8650752 | tf_op jit(solution)/shard_map/all_gather | solution.py:532
  14.9 10.3 %copy-start.3 = (bf16[2,4,256]{2,1,0:T(4,128)(2,1)S(1)}, bf16[2,4,256]{2,1,0:T(4,128)(2,1)}, u32[]{:S(2)}) copy-start(bf16[2,4,256]{2,1,0:T(4,128)(2,1)} %param.23) | copy-start | bytes 12292
  14.9 10.8 %copy-start.4 = (bf16[2,256]{1,0:T(2,128)(2,1)S(1)}, bf16[2,256]{1,0:T(2,128)(2,1)}, u32[]{:S(2)}) copy-start(bf16[2,256]{1,0:T(2,128)(2,1)} %param.25) | copy-start | bytes 3076
  15.7 8.4 %copy-start = (bf16[2,1024,256]{2,1,0:T(8,128)(2,1)S(1)}, bf16[2,1024,256]{2,1,0:T(8,128)(2,1)}, u32[]{:S(2)}) copy-start(bf16[2,1024,256]{2,1,0:T(8,128)(2,1)} %param.20) | copy-start | bytes 3145732
  16.4 444.6 %all-gather.5.cloned.1.call-start = ((), (), s32[]{:S(2)}) async-start(), calls=%async_computation | async-start | bytes 8650752 | tf_op jit(solution)/shard_map/all_gather | solution.py:532
  23.5 161.3 %copy-start.1 = (bf16[96,2048]{1,0:T(8,128)(2,1)}, bf16[96,2048]{1,0:T(8,128)(2,1)S(1)}, u32[]{:S(2)}) copy-start(bf16[96,2048]{1,0:T(8,128)(2,1)S(1)} %constant_dynamic-update-slice_fusion.e3_ref) | copy-start | bytes 1179652
  287.4 4.5 collective-permute-start
  291.9 1.0 copy-start.7
  353.4 4.0 collective-permute-start.1
  357.3 0.7 copy-start.8
  458.7 3.8 collective-permute-start.2
  462.4 1.0 copy-start.6
  522.5 19.2 %collective-permute-start.3 = (f32[3072,1024]{1,0:T(8,128)}, f32[3072,1024]{1,0:T(8,128)}, u32[]{:S(2)}, u32[]{:S(2)}) collective-permute-start(f32[3072,1024]{1,0:T(8,128)} %get-tuple-element.34), channel_id=1, source_target_pairs={{0,1},{1,0},{2,3},{3,2},{4,5},{5,4},{6,7},{7,6},{8,9},{9,8},{10,11... | collective-permute-start | bytes 37748744 | tf_op jit(solution)/shard_map/ppermute | solution.py:566
Sparse Core Ops, SparseCore 0:
  13.6 139.9 all-gather.6
  156.7 81.1 all-gather.8
  357.4 73.6 all-gather.4

commit v4 on v3

--- a/solution.py
+++ b/solution.py
@@ -15,8 +15,7 @@
 
 
 def silu(v):
-    half = 0.5 * v
-    return half + half * jnp.tanh(half)
+    return v / (1.0 + jnp.exp2(v * -LOG2E))
 
 
 def split3(v):
@@ -75,6 +74,14 @@
 EARLY = (2, 4, 6)
 
 
+def comm_sems(shards):
+    return [pltpu.SemaphoreType.DMA((Gather.N_SEM * len(shards),)) for _ in range(2)] if shards else []
+
+
+def comm_outs(shards, n_tp):
+    return [jax.ShapeDtypeStruct((v.shape[0], n_tp) + v.shape[1:], F32) for v in shards]
+
+
 def head_row(h, heads):
     return (h % 2) * (heads // 2) + h // 2
 
@@ -103,14 +110,18 @@
         jnp.concatenate([z, r * lo], axis=1), jnp.concatenate([z, r * hi], axis=1)], axis=0)
 
 
-def p1_body(off_ref, u_ref, halo_ref, nw_ref, wf_ref, sm_ref, wbc_ref, cbc_ref, bbc_ref, e3_ref,
-            y_ref, c_ref, ac_ref, send_ref, wxb, wdt, cst, st, xcar, qcar, aoff, ubuf, *, geom, mixed):
+def p1_body(u_ref, halo_ref, nw_ref, wf_ref, sm_ref, wbc_ref, cbc_ref, bbc_ref, e3_ref, *refs, geom, mixed, plan):
+    nc = len(plan)
+    ins, (y_ref, c_ref, ac_ref, send_ref), outs = refs[:nc], refs[nc:nc + 4], refs[nc + 4:2 * nc + 4]
+    wxb, wdt, cst, st, xcar, qcar, aoff, ubuf, *sems = refs[2 * nc + 4:]
     n_dp, n_tp, hd, width, heads = geom
     i = pl.program_id(0)
     nst = 128
     pc = width // n_tp
     hp = heads // n_tp
     sub = BLK // 2
+    if nc:
+        background(i, ins, outs, *sems, plan)
 
     @pl.when(i == 0)
     def _():
@@ -260,46 +271,51 @@
         send_ref[...] = st[...]
 
 
-def p1(u, off, halo, nw, wf, wbc, cbc, bbc, e3, n, n_dp, n_tp, mixed, interpret=False):
+def p1(u, base, halo, nw, wf, wbc, cbc, bbc, e3, n, n_dp, n_tp, mixed, shards=(), plan=(), cid=None, interpret=False):
     d_model = u.shape[1]
     width = 256 * n_tp
     heads = width // 64
     rows = d_model // n_dp
     geom = (n_dp, n_tp, 64, width, heads)
     nb = n // BLK
-    full = lambda shp: pl.BlockSpec(shp, lambda i, o: (0,) * len(shp), pipeline_mode=pl.Buffered(1))
-    gs = pltpu.PrefetchScalarGridSpec(
-        num_scalar_prefetch=1, grid=(nb,),
+    full = lambda shp: pl.BlockSpec(shp, lambda i: (0,) * len(shp), pipeline_mode=pl.Buffered(1))
+    gs = dict(
+        grid=(nb,),
         in_specs=[
-            pl.BlockSpec((BLK, d_model), lambda i, o: (o[0] + i, 0)),
+            pl.BlockSpec((BLK, d_model), lambda i: (base() + i, 0)),
             full((24, d_model)), full((1, d_model)),
             full((n_dp * n_tp, rows, 256)),
-            pl.BlockSpec((n_tp, 32, 256), lambda i, o: (0, rows // 32, 0), pipeline_mode=pl.Buffered(1)),
+            pl.BlockSpec((n_tp, 32, 256), lambda i: (0, rows // 32, 0), pipeline_mode=pl.Buffered(1)),
             full((d_model, 256)), full((4, 256)), full((1, 256)), full((3 * heads, width)),
-        ],
+        ] + [pl.BlockSpec(memory_space=pl.ANY)] * len(shards),
         out_specs=[
-            pl.BlockSpec((BLK, width), lambda i, o: (i, 0)),
-            pl.BlockSpec((BLK, 128), lambda i, o: (i, 0)),
-            pl.BlockSpec((heads, BLK), lambda i, o: (0, i)),
-            pl.BlockSpec((128, width), lambda i, o: (0, 0)),
-        ],
+            pl.BlockSpec((BLK, width), lambda i: (i, 0)),
+            pl.BlockSpec((BLK, 128), lambda i: (i, 0)),
+            pl.BlockSpec((heads, BLK), lambda i: (0, i)),
+            pl.BlockSpec((128, width), lambda i: (0, 0)),
+        ] + [pl.BlockSpec(memory_space=pl.ANY)] * len(shards),
         scratch_shapes=[
             pltpu.VMEM((d_model, width), BF16), pltpu.VMEM((heads, d_model), BF16), pltpu.VMEM((2 * heads, 256), F32),
             pltpu.VMEM((128, width), F32), pltpu.VMEM((24, width), F32), pltpu.VMEM((24, 256), F32),
             pltpu.VMEM((heads, 128), F32), pltpu.VMEM((d_model // 128 * BLK, 128), F32),
-        ])
+        ] + comm_sems(shards))
     return pl.pallas_call(
-        functools.partial(p1_body, geom=geom, mixed=mixed), grid_spec=gs, name="p1",
+        functools.partial(p1_body, geom=geom, mixed=mixed, plan=plan), name="p1",
         out_shape=[jax.ShapeDtypeStruct((n, width), F32), jax.ShapeDtypeStruct((n, 128), F32),
-                   jax.ShapeDtypeStruct((heads, n), F32), jax.ShapeDtypeStruct((128, width), F32)],
-        compiler_params=pltpu.CompilerParams(dimension_semantics=("arbitrary",), vmem_limit_bytes=60 << 20),
+                   jax.ShapeDtypeStruct((heads, n), F32), jax.ShapeDtypeStruct((128, width), F32)] + comm_outs(shards, n_tp),
+        compiler_params=pltpu.CompilerParams(dimension_semantics=("arbitrary",), vmem_limit_bytes=60 << 20, collective_id=cid, has_side_effects=bool(shards)),
         cost_estimate=pl.CostEstimate(flops=n * 70_000_000, bytes_accessed=n * 12000, transcendentals=0),
-        interpret=interpret,
-    )(off, u, halo, nw, wf, wf, wbc, cbc, bbc, e3)
-
-
-def p2_body(off_ref, u_ref, nw_ref, wz_ref, wo_ref, sm_ref, y_ref, c_ref, ac_ref, s_ref, e3_ref,
-            o_ref, f_ref, wzb, wob, s3, ubuf, *, geom, mix_in, mix_out):
+        interpret=interpret, **gs,
+    )(u, halo, nw, wf, wf, wbc, cbc, bbc, e3, *shards)
+
+
+def p2_body(u_ref, nw_ref, wz_ref, wo_ref, sm_ref, y_ref, c_ref, ac_ref, s_ref, e3_ref, *refs,
+            geom, mix_in, mix_out, plan):
+    nc = len(plan)
+    ins, (o_ref, f_ref), outs = refs[:nc], refs[nc:nc + 2], refs[nc + 2:2 * nc + 2]
+    wzb, wob, s3, ubuf, *sems = refs[2 * nc + 2:]
+    if nc:
+        background(pl.program_id(0), ins, outs, *sems, plan)
     n_dp, n_tp, hd, width, heads = geom
     pc = width // n_tp
     rows_z = wzb.shape[0] // n_dp
@@ -352,36 +368,37 @@
             wb_ref[t * rows:(t + 1) * rows, d * cols:(d + 1) * cols] = wf_ref[d * n_tp + t].astype(BF16)
 
 
-def p2(u, off, nw, wz, wo, wsm, y, c, ac, s, e3, n, n_dp, n_tp, mix_in, mix_out, out_rows=None, interpret=False):
+def p2(u, base, obase, nw, wz, wo, wsm, y, c, ac, s, e3, n, n_dp, n_tp, mix_in, mix_out, out_rows=None, shards=(), plan=(), cid=None, interpret=False):
     d_model = u.shape[1]
     width = 256 * n_tp
     heads = width // 64
     rows = d_model // n_dp
     geom = (n_dp, n_tp, 64, width, heads)
     nb = n // BLK2
-    full = lambda shp: pl.BlockSpec(shp, lambda i, o: (0,) * len(shp), pipeline_mode=pl.Buffered(1))
-    gs = pltpu.PrefetchScalarGridSpec(
-        num_scalar_prefetch=1, grid=(nb,),
+    full = lambda shp: pl.BlockSpec(shp, lambda i: (0,) * len(shp), pipeline_mode=pl.Buffered(1))
+    gs = dict(
+        grid=(nb,),
         in_specs=[
-            pl.BlockSpec((BLK2, d_model), lambda i, o: (o[0] + i, 0)),
+            pl.BlockSpec((BLK2, d_model), lambda i: (base() + i, 0)),
             full((1, d_model)),
             full((n_dp * n_tp, rows, 256)), full((n_dp * n_tp, 256, d_model // n_dp)),
-            pl.BlockSpec((n_tp, 32, 256), lambda i, o: (0, rows // 32, 0), pipeline_mode=pl.Buffered(1)),
-            pl.BlockSpec((BLK2, width), lambda i, o: (i, 0)),
-            pl.BlockSpec((BLK2, 128), lambda i, o: (i, 0)),
-            pl.BlockSpec((heads, BLK2), lambda i, o: (0, i)),
+            pl.BlockSpec((n_tp, 32, 256), lambda i: (0, rows // 32, 0), pipeline_mode=pl.Buffered(1)),
+            pl.BlockSpec((BLK2, width), lambda i: (i, 0)),
+            pl.BlockSpec((BLK2, 128), lambda i: (i, 0)),
+            pl.BlockSpec((heads, BLK2), lambda i: (0, i)),
             full((128, width)), full((3 * heads, width)),
-        ],
-        out_specs=[pl.BlockSpec((BLK2, d_model), lambda i, o: (o[1] + i, 0)), pl.BlockSpec((BLK2, d_model), lambda i, o: (i, 0))],
+        ] + [pl.BlockSpec(memory_space=pl.ANY)] * len(shards),
+        out_specs=[pl.BlockSpec((BLK2, d_model), lambda i: (obase() + i, 0)), pl.BlockSpec((BLK2, d_model), lambda i: (i, 0))]
+        + [pl.BlockSpec(memory_space=pl.ANY)] * len(shards),
         scratch_shapes=[pltpu.VMEM((d_model, width), BF16), pltpu.VMEM((width, d_model), BF16),
-                        pltpu.VMEM((3, 256, width), BF16), pltpu.VMEM((d_model // 128 * BLK2, 128), F32)])
+                        pltpu.VMEM((3, 256, width), BF16), pltpu.VMEM((d_model // 128 * BLK2, 128), F32)] + comm_sems(shards))
     return pl.pallas_call(
-        functools.partial(p2_body, geom=geom, mix_in=mix_in, mix_out=mix_out), grid_spec=gs, name="p2",
-        out_shape=[jax.ShapeDtypeStruct((out_rows or n, d_model), BF16), jax.ShapeDtypeStruct((n, d_model), F32)],
-        compiler_params=pltpu.CompilerParams(dimension_semantics=("arbitrary",), vmem_limit_bytes=60 << 20),
+        functools.partial(p2_body, geom=geom, mix_in=mix_in, mix_out=mix_out, plan=plan), name="p2",
+        out_shape=[jax.ShapeDtypeStruct((out_rows or n, d_model), BF16), jax.ShapeDtypeStruct((n, d_model), F32)] + comm_outs(shards, n_tp),
+        compiler_params=pltpu.CompilerParams(dimension_semantics=("arbitrary",), vmem_limit_bytes=60 << 20, collective_id=cid, has_side_effects=bool(shards)),
         cost_estimate=pl.CostEstimate(flops=n * 30_000_000, bytes_accessed=n * 12000, transcendentals=0),
-        interpret=interpret,
-    )(off, u, nw, wz, wo, wsm, y, c, ac, s, e3)
+        interpret=interpret, **gs,
+    )(u, nw, wz, wo, wsm, y, c, ac, s, e3, *shards)
 
 
 def fin_body(off_ref, buf_ref, f_ref, o_ref, ubuf):
@@ -492,6 +509,26 @@
         g.step3()
 
 
+def background(i, ins, outs, send, recv, plan):
+    gs = [Gather(a, g, send, recv, Gather.N_SEM * k) for k, (a, g) in enumerate(zip(ins, outs))]
+
+    @pl.when(i == 0)
+    def _():
+        entry_barrier(gs[0].peers())
+        for g in gs:
+            g.step0()
+
+    for g, at in zip(gs, plan):
+        for j, dz in enumerate((1, 3, 2)):
+            pl.when(i == at[j])(functools.partial(g.step1, dz))
+            pl.when(i == at[3 + j])(functools.partial(g.step2, dz))
+
+    @pl.when(i == pl.num_programs(0) - 1)
+    def _():
+        for g in gs:
+            g.step3()
+
+
 def gather_all(shards, n_tp, cid):
     n = len(shards)
     return pl.pallas_call(
@@ -529,7 +566,6 @@
         dp, tp = lax.axis_index('dp'), lax.axis_index('tp')
         core = tp % 2
         rows, ocols = d_model // n_dp, d_model // n_dp
-        gather = lambda v: lax.all_gather(v, ('dp', 'tp'))
         e3 = expand_mat(heads)
         up = [(2 * k, 2 * k + 1) for k in range(n_tp // 2)]
         swap = [(k, k ^ 1) for k in range(n_tp)]
@@ -541,28 +577,26 @@
 
         sm = [small_rows(conv_x[l], bias_x[l], gate_w[l], d_skip[l], dt_bias[l], a_log[l], w_dt[l]) for l in range(2)]
         sx = [jnp.concatenate([cut(w_x[l]), jnp.broadcast_to(sm[l], (n_dp,) + sm[l].shape)], axis=1) for l in range(2)]
-        wxs, wzs, wos = [None, None], [None, None], [None, None]
-        wxs[0], wzs[0], wos[0] = gather_all([sx[0], cut(w_z[0]), cut_o(w_out[0])], n_tp, 1)
-        part = lambda v: lax.dynamic_index_in_dim(v, dp, 0, keepdims=False)
-        wxs[1] = gather(part(sx[1]))
-        wzs[1] = gather(part(cut(w_z[1])))
-        wos[1] = gather(part(cut_o(w_out[1])))
         flat = lambda v: v.reshape((n_dp * n_tp,) + v.shape[2:])
-        wxs[0], wzs[0], wos[0] = flat(wxs[0]), flat(wzs[0]), flat(wos[0])
+        sz, so = [cut(w_z[l]) for l in range(2)], [cut_o(w_out[l]) for l in range(2)]
+        wx, = gather_all([sx[0]], n_tp, 1)
+        wx = flat(wx)
         cur = u
-        off = jnp.stack([core * (n // BLK), 0 * core])
-        zero = jnp.zeros((2,), jnp.int32)
+        mine = lambda blk: (lambda: lax.axis_index('tp') % 2 * (n // blk))
+        none = lambda: 0
         tail = u[n - 64:n].astype(F32).reshape(8, 8, d_model).transpose(1, 0, 2).reshape(64, d_model)[40:]
         halo = jnp.where(core == 1, tail, 0.0)
         for l in range(2):
             nw = norm_w[l].astype(F32)[None]
-            y, c, ac, s_end = p1(cur, off, halo, nw, wxs[l], w_bc[l], conv_bc[l].astype(F32), bias_bc[l].astype(F32)[None], e3, n, n_dp, n_tp, l > 0)
+            y, c, ac, s_end, wz, wo = p1(cur, mine(BLK) if l == 0 else none, halo, nw, wx, w_bc[l], conv_bc[l].astype(F32), bias_bc[l].astype(F32)[None], e3, n, n_dp, n_tp, l > 0,
+                                         shards=(sz[l], so[l]), plan=((4, 6, 8, 12, 14, 16), (9, 11, 13, 18, 20, 22)), cid=2 + l)
             s = lax.ppermute(s_end, 'tp', up)
-            off2 = jnp.stack([core, 0 * core] if l == 0 else [0 * core, core]) * (n // BLK2)
-            o, f = p2(cur, off2, nw, wzs[l], wos[l], wxs[l], y, c, ac, s, e3, n, n_dp, n_tp, l > 0, l == 0, out_rows=n if l == 0 else steps)
-            cur, off = o, zero
+            more = dict(shards=(sx[1],), plan=((3, 4, 5, 8, 9, 10),), cid=4) if l == 0 else {}
+            o, f, *nxt = p2(cur, mine(BLK2) if l == 0 else none, none if l == 0 else mine(BLK2), nw, flat(wz), flat(wo), wx, y, c, ac, s, e3, n, n_dp, n_tp, l > 0, l == 0, out_rows=n if l == 0 else steps, **more)
+            cur = o
             if l == 0:
                 halo = lax.ppermute(f[n - 24:], 'tp', up)
+                wx = flat(nxt[0])
         other = lax.ppermute(f, 'tp', swap)
         return finish(o, other, jnp.reshape((1 - core) * (n // 512), (1,)))[None]
 

time: 558 us -> 477 us (0.85)
  Pallas kernels: 487 us -> 420 us
  between operations: 13.4 us -> 0.31 us
    pallas_call x1, Pallas kernels: 156 us -> 56.7 us  [gather_all(): pl.pallas_call(functools.partial(gather_body, n=n), name='gather', out_sh...]
    pallas_call x2, Pallas kernels: 203 us -> 220 us  [p1(): pl.pallas_call(functools.partial(p1_body, geom=geom, mixed=mixed, plan=pl...]
    pallas_call x2, Pallas kernels: 119 us -> 134 us  [p2(): pl.pallas_call(functools.partial(p2_body, geom=geom, mix_in=mix_in, mix_o...]
  transfers between devices with their start and end apart: 7 -> 4, of which waited for: 3 -> 3; matrix products, arithmetic and copies ran while one was open for 3% -> 1% of each run, Pallas kernels for 75% -> 0%
where the time goes in v4:
time: 477 us
  Pallas kernels  420 us (88%)
  waiting for transfers between devices  21.2 us (4%)
  local copies, waits for them, and re-layouts  17.9 us (4%)
  other arithmetic  12.2 us (3%)
  starting transfers between devices  5.48 us (1%)
    pallas_call x2, Pallas kernels, p1(): pl.pallas_call(functools.partial(p1_body, geom=geom, mixed=mixed, plan=pl...  220 us
    pallas_call x2, Pallas kernels, p2(): pl.pallas_call(functools.partial(p2_body, geom=geom, mix_in=mix_in, mix_o...  134 us
    pallas_call x1, Pallas kernels, gather_all(): pl.pallas_call(functools.partial(gather_body, n=n), name='gather', out_sh...  56.7 us
    ppermute x1, waiting for transfers between devices, device_forward(): other = lax.ppermute(f, 'tp', swap)  18.8 us
  transfers between devices with their start and end apart: 4, of which 3 were waited for; matrix products, arithmetic and copies ran while one was open for 1% of the time, Pallas kernels for 0%

profile of v4, /device:TPU:0, one launch (start us, length us, event | category | flops | bytes accessed | tf_op | source)
XLA Modules:
  0.0 477.0 jit_solution(15690952189882012628)
XLA Ops:
  0.0 0.9 slice_bitcast_fusion.2
  0.9 0.1 copy.27
  1.0 1.3 convert_bitcast_fusion
  2.3 1.3 bitcast_convert_fusion.1
  3.6 1.3 slice_bitcast_fusion.3
  4.9 1.3 multiply_bitcast_fusion
  6.2 1.3 slice_bitcast_fusion.4
  7.5 0.1 broadcast_in_dim.60
  7.6 0.1 broadcast_in_dim_reshape.6
  7.6 2.1 fusion.3
  9.7 0.1 convert.21
  9.8 1.4 slice_convert_fusion.3
  11.2 0.1 broadcast_in_dim.62
  11.2 0.1 broadcast_in_dim.63
  11.4 1.1 pad_maximum_fusion.refs_0_
  12.5 56.7 %gather.7 = f32[4,8,288,256]{3,2,1,0:T(8,128)} custom-call(f32[4,288,256]{2,1,0:T(8,128)} %pad_maximum_fusion.refs_0_), custom_call_target="tpu_custom_call" | custom-call | flops 10000000000 | bytes 16000000 | tf_op jit(solution)/shard_map/gather/pallas_call | solution.py:534
  69.2 0.0 copy-start.13
  69.2 0.0 copy-start.14
  69.2 0.6 gather_fusion
  69.8 0.2 broadcast_in_dim.66
  70.0 0.3 reshape.98
  70.4 0.0 copy-done.8
  70.4 0.0 copy-start.6
  70.4 0.7 slice_convert_fusion
  71.1 0.9 fusion.1
  71.9 0.2 copy.24
  72.1 1.2 copy.21
  73.4 0.9 fusion.2
  74.2 1.1 convert.25.refs_0_
  75.3 2.2 slice_bitcast_fusion
  77.6 0.6 bitcast_convert_fusion
  78.1 0.6 slice_convert_fusion.2
  78.7 0.7 select_bitcast_fusion.halo_ref
  79.5 110.2 %p1.2 = (f32[3072,2048]{1,0:T(8,128)}, f32[3072,128]{1,0:T(8,128)}, f32[32,3072]{1,0:T(8,128)}, f32[128,2048]{1,0:T(8,128)}, f32[4,8,256,256]{3,2,1,0:T(8,128)}, /*index=5*/f32[4,8,256,256]{3,2,1,0:T(8,128)}) custom-call(bf16[6144,1024]{1,0:T(8,128)(2,1)} %bitcast.77, f32[24,1024]{1,0:T(8,128)} %select_bitcast_fusion.halo_ref, ...), custom_call_target="tpu_custom_call" | custom-call | flops 215040000000 | bytes 36864000 | tf_op jit(solution)/shard_map/p1/pallas_call | solution.py:302
  189.7 2.2 collective-permute-start
  191.9 0.0 copy-done.17
  192.0 0.1 broadcast_in_dim.67
  192.0 0.1 broadcast_in_dim_reshape.7
  192.1 0.0 copy-done
  192.1 0.1 convert.27
  192.2 0.1 broadcast_in_dim.69
  192.3 0.0 copy-done.16
  192.3 0.1 broadcast_in_dim.70
  192.4 0.0 copy-done.12
  192.4 1.1 pad_maximum_fusion.1.refs_0_
  193.5 0.4 collective-permute-done.s_ref
  193.9 1.0 copy-done.19
  194.9 75.0 %p2.2 = (bf16[3072,1024]{1,0:T(8,128)(2,1)}, f32[3072,1024]{1,0:T(8,128)}, f32[4,8,288,256]{3,2,1,0:T(8,128)}) custom-call(bf16[6144,1024]{1,0:T(8,128)(2,1)} %bitcast.78, f32[1,1024]{1,0:T(1,128)} %get-tuple-element.52.nw_ref, f32[32,256,256]{2,1,0:T(8,128)} %bitcast.85, f32[32,256,256]{2,1,0:T(8,128)} %bitcast.86, f32[32,288,256]{2,1,0:T(8,128)} %bitcast.81, ...), custom_call_target="tpu_custom_call" | custom-call | flops 92160000000 | bytes 36864000 | tf_op jit(solution)/shard_map/p2/pallas_call | solution.py:395
  269.9 0.9 slice.124
  270.8 1.3 collective-permute-start.1
  272.1 0.2 copy.25
  272.3 1.2 copy.23
  273.5 0.0 copy-done.1
  273.5 1.1 convert.31.refs_0_
  274.6 0.0 collective-permute-done.1.halo_ref
  274.6 0.6 copy-done.21
  275.2 109.6 %p1.3 = (f32[3072,2048]{1,0:T(8,128)}, f32[3072,128]{1,0:T(8,128)}, f32[32,3072]{1,0:T(8,128)}, f32[128,2048]{1,0:T(8,128)}, f32[4,8,256,256]{3,2,1,0:T(8,128)}, /*index=5*/f32[4,8,256,256]{3,2,1,0:T(8,128)}) custom-call(bf16[3072,1024]{1,0:T(8,128)(2,1)} %get-tuple-element.28.u_ref, f32[24,1024]{1,0:T(8,128)} %copy-done.21, ...), custom_call_target="tpu_custom_call" | custom-call | flops 215040000000 | bytes 36864000 | tf_op jit(solution)/shard_map/p1/pallas_call | solution.py:302
  384.8 1.6 collective-permute-start.2
  386.4 2.0 collective-permute-done.2.s_ref
  388.4 1.0 copy-done.20
  389.4 58.9 %p2.3 = (bf16[6144,1024]{1,0:T(8,128)(2,1)}, f32[3072,1024]{1,0:T(8,128)}) custom-call(bf16[3072,1024]{1,0:T(8,128)(2,1)} %get-tuple-element.28.u_ref, f32[1,1024]{1,0:T(1,128)} %get-tuple-element.51.nw_ref, f32[32,256,256]{2,1,0:T(8,128)} %bitcast.87, f32[32,256,256]{2,1,0:T(8,128)} %bitcast.88, f32[32,288,256]{2,1,0:T(8,128)} %bitcast.84, ...), custom_call_target="tpu_custom_call" | custom-call | flops 92160000000 | bytes 36864000 | tf_op jit(solution)/shard_map/p2/pallas_call | solution.py:395
  448.2 0.4 collective-permute-start.3
  448.7 18.8 %collective-permute-done.3.f_ref = f32[3072,1024]{1,0:T(8,128)} collective-permute-done((f32[3072,1024]{1,0:T(8,128)}, f32[3072,1024]{1,0:T(8,128)}, u32[]{:S(2)}, u32[]{:S(2)}) %collective-permute-start.3) | collective-permute-done | bytes 12582944 | tf_op jit(solution)/shard_map/ppermute | solution.py:600
  467.5 9.5 %finish.1 = bf16[6144,1024]{1,0:T(8,128)(2,1)} custom-call(s32[1]{0:T(128)} %bitcast.off_ref, bf16[6144,1024]{1,0:T(8,128)(2,1)} %get-tuple-element.37.buf_ref, f32[3072,1024]{1,0:T(8,128)} %collective-permute-done.3.f_ref), custom_call_target="tpu_custom_call", output_to_operand_aliasing={{}: (1, {})} | custom-call | flops 3145728 | bytes 18874368 | tf_op jit(solution)/shard_map/finish/pallas_call | solution.py:416
  (44 shorter events, 0.3 us)
Async XLA Ops:
  11.3 57.9 %copy-start.9 = (f32[1,256]{1,0:T(1,128)}, f32[1,256]{1,0:T(1,128)S(1)}, u32[]{:S(2)}) copy-start(f32[1,256]{1,0:T(1,128)S(1)} %broadcast.22) | copy-start | bytes 3076
  12.5 56.7 %copy-start.18 = (s32[32]{0:T(128)S(1)}, s32[32]{0:T(128)}, u32[]{:S(2)}) copy-start(s32[32]{0:T(128)} %constant.40) | copy-start | bytes 388
  12.5 57.9 %copy-start.8 = (bf16[2,1024]{1,0:T(2,128)(2,1)S(1)}, bf16[2,1024]{1,0:T(2,128)(2,1)}, u32[]{:S(2)}) copy-start(bf16[2,1024]{1,0:T(2,128)(2,1)} %param.17) | copy-start | bytes 12292
  12.5 58.6 %copy-start.3 = (bf16[2,256,1024]{2,1,0:T(8,128)(2,1)S(1)}, bf16[2,256,1024]{2,1,0:T(8,128)(2,1)}, u32[]{:S(2)}) copy-start(bf16[2,256,1024]{2,1,0:T(8,128)(2,1)} %param.30) | copy-start | bytes 3145732
  12.5 60.9 %copy-start.4 = (bf16[2,1024,256]{2,1,0:T(8,128)(2,1)S(1)}, bf16[2,1024,256]{2,1,0:T(8,128)(2,1)}, u32[]{:S(2)}) copy-start(bf16[2,1024,256]{2,1,0:T(8,128)(2,1)} %param.18) | copy-start | bytes 3145732
  69.2 8.3 %copy-start.13 = (bf16[2,4,256]{2,1,0:T(4,128)(2,1)S(1)}, bf16[2,4,256]{2,1,0:T(4,128)(2,1)}, u32[]{:S(2)}) copy-start(bf16[2,4,256]{2,1,0:T(4,128)(2,1)} %param.23) | copy-start | bytes 12292
  69.2 8.9 %copy-start.14 = (bf16[2,256]{1,0:T(2,128)(2,1)S(1)}, bf16[2,256]{1,0:T(2,128)(2,1)}, u32[]{:S(2)}) copy-start(bf16[2,256]{1,0:T(2,128)(2,1)} %param.25) | copy-start | bytes 3076
  70.4 9.0 %copy-start.6 = (bf16[96,2048]{1,0:T(8,128)(2,1)}, bf16[96,2048]{1,0:T(8,128)(2,1)S(1)}, u32[]{:S(2)}) copy-start(bf16[96,2048]{1,0:T(8,128)(2,1)S(1)} %constant_dynamic-update-slice_fusion.e3_ref) | copy-start | bytes 1179652
  79.4 112.5 %copy-start.5 = (f32[4,1024]{1,0:T(4,128)S(1)}, f32[4,1024]{1,0:T(4,128)}, u32[]{:S(2)}) copy-start(f32[4,1024]{1,0:T(4,128)} %get-tuple-element.47) | copy-start | bytes 49156
  79.4 112.5 %copy-start.17 = (f32[4]{0:T(128)S(1)}, f32[4]{0:T(128)}, u32[]{:S(2)}) copy-start(f32[4]{0:T(128)} %get-tuple-element.61) | copy-start | bytes 52
  79.4 112.7 %copy-start = (bf16[1,1024,256]{2,1,0:T(8,128)(2,1)S(1)}, bf16[1,1024,256]{2,1,0:T(8,128)(2,1)}, u32[]{:S(2)}) copy-start(bf16[1,1024,256]{2,1,0:T(8,128)(2,1)} %get-tuple-element.45) | copy-start | bytes 1572868
  79.4 112.8 %copy-start.15 = (f32[4]{0:T(128)S(1)}, f32[4]{0:T(128)}, u32[]{:S(2)}) copy-start(f32[4]{0:T(128)} %get-tuple-element.59) | copy-start | bytes 52
  79.4 112.9 %copy-start.16 = (f32[4]{0:T(128)S(1)}, f32[4]{0:T(128)}, u32[]{:S(2)}) copy-start(f32[4]{0:T(128)} %get-tuple-element.57) | copy-start | bytes 52
  79.4 112.9 %copy-start.7 = (f32[4,256]{1,0:T(4,128)S(1)}, f32[4,256]{1,0:T(4,128)}, u32[]{:S(2)}) copy-start(f32[4,256]{1,0:T(4,128)} %get-tuple-element.53) | copy-start | bytes 12292
  79.4 112.9 %copy-start.10 = (f32[1,256]{1,0:T(1,128)S(1)}, f32[1,256]{1,0:T(1,128)}, u32[]{:S(2)}) copy-start(f32[1,256]{1,0:T(1,128)} %copy-done.9) | copy-start | bytes 3076
  79.5 112.9 %copy-start.11 = (f32[1,256]{1,0:T(1,128)S(1)}, f32[1,256]{1,0:T(1,128)}, u32[]{:S(2)}) copy-start(f32[1,256]{1,0:T(1,128)} %get-tuple-element.63) | copy-start | bytes 3076
  79.5 112.9 %copy-start.12 = (f32[1,256]{1,0:T(1,128)S(1)}, f32[1,256]{1,0:T(1,128)}, u32[]{:S(2)}) copy-start(f32[1,256]{1,0:T(1,128)} %get-tuple-element.68) | copy-start | bytes 3076
  189.7 4.2 collective-permute-start
  193.9 1.0 copy-start.19
  194.9 77.2 %copy-start.2 = (bf16[1,256,1024]{2,1,0:T(8,128)(2,1)S(1)}, bf16[1,256,1024]{2,1,0:T(8,128)(2,1)}, u32[]{:S(2)}) copy-start(bf16[1,256,1024]{2,1,0:T(8,128)(2,1)} %get-tuple-element.39) | copy-start | bytes 1572868
  194.9 78.6 %copy-start.1 = (bf16[1,1024,256]{2,1,0:T(8,128)(2,1)S(1)}, bf16[1,1024,256]{2,1,0:T(8,128)(2,1)}, u32[]{:S(2)}) copy-start(bf16[1,1024,256]{2,1,0:T(8,128)(2,1)} %get-tuple-element.41) | copy-start | bytes 1572868
  270.8 3.8 collective-permute-start.1
  274.6 0.6 copy-start.21
  384.8 3.6 collective-permute-start.2
  388.4 1.0 copy-start.20
  448.2 19.2 %collective-permute-start.3 = (f32[3072,1024]{1,0:T(8,128)}, f32[3072,1024]{1,0:T(8,128)}, u32[]{:S(2)}, u32[]{:S(2)}) collective-permute-start(f32[3072,1024]{1,0:T(8,128)} %get-tuple-element.38), channel_id=1, source_target_pairs={{0,1},{1,0},{2,3},{3,2},{4,5},{5,4},{6,7},{7,6},{8,9},{9,8},{10,11... | collective-permute-start | bytes 37748744 | tf_op jit(solution)/shard_map/ppermute | solution.py:600

commit v5 on v0

v5 whole, which is shorter than its diff:
```python
import functools
import jax
import jax.numpy as jnp
from jax import lax
from jax.experimental import pallas as pl
from jax.experimental.pallas import tpu as pltpu
from jax.sharding import PartitionSpec as P

EPS = 1e-5
LOG2E = 1.4426950408889634
HI = lax.Precision.HIGHEST
F32 = jnp.float32
BF16 = jnp.bfloat16
MESH = pl.DeviceIdType.MESH
LANES = 128
BLK = 128
SUB = 64
BLK2 = 256
NBS = 4
PC = 256
HD = 64
NST = 128
CAR = 24
SMALL = 32
SEMS = 26
VMEM_CAP = 60 << 20


def silu(v):
    return v / (1.0 + jnp.exp2(v * -LOG2E))


def split3(v):
    a = v.astype(BF16)
    r = v - a.astype(F32)
    b = r.astype(BF16)
    return a, b, (r - b.astype(F32)).astype(BF16)


def round_bf16(v):
    return v.astype(BF16).astype(F32)


def rms(u, nw):
    return (u * lax.rsqrt(jnp.mean(u * u, axis=-1, keepdims=True) + EPS) * nw).astype(BF16)


def dot(a, b, prec=None):
    return jnp.dot(a, b, preferred_element_type=F32, precision=prec)


def dott(a, b, prec=None):
    return lax.dot_general(a, b, (((1,), (1,)), ((), ())), preferred_element_type=F32, precision=prec)


def rows_cat(*v):
    return jnp.concatenate(v, axis=0)


def lanes_cat(*v):
    return jnp.concatenate(v, axis=1)


def time_of(r):
    return 8 * (r % 8) + r // 8


def roll8(v):
    c = v.shape[-1]
    return pltpu.roll(v.reshape(CAR // 8, 8, c), 1, 1).reshape(CAR, c)


def conv_block(cur, prev, taps, bias, first):
    now = roll8(cur[SUB - CAR:])
    sh = jnp.where(first, prev, now)
    out = bias + cur * taps[-1]
    for k in range(1, 4):
        out = out + rows_cat(sh[CAR - 8 * k:], cur[:SUB - 8 * k]) * taps[3 - k]
    return out, now


def unmix(v, buf):
    n, c = v.shape
    for j in range(c // LANES):
        buf[n * j:n * (j + 1), :] = v[:, LANES * j:LANES * (j + 1)]
    cols = [rows_cat(*[buf[pl.ds(n * j + b + k, 8, stride=8), :] for b in range(0, n, SUB) for k in range(8)])
            for j in range(c // LANES)]
    return lanes_cat(*cols)


def head_row(h, heads):
    return (h % 2) * (heads // 2) + h // 2


def expand_mat(heads):
    order = sorted(range(heads), key=lambda h: head_row(h, heads))
    one = jnp.repeat(jnp.eye(heads, dtype=BF16)[jnp.array(order)], HD, axis=1)
    return rows_cat(one, one, one)


def kcat6(parts):
    a, b, c = parts
    return lanes_cat(a, b, c, a), lanes_cat(b, a)


def kcat6r(parts):
    a, b, c = parts
    return rows_cat(a, a, a, b), rows_cat(b, c)


def block_diag(x, lo, hi):
    z = jnp.zeros((x.shape[0], LANES), BF16)
    l, r = x[:, :LANES], x[:, LANES:]
    return rows_cat(lanes_cat(l * lo, z), lanes_cat(l * hi, z), lanes_cat(z, r * lo), lanes_cat(z, r * hi))


def here():
    dp, tp = lax.axis_index('dp'), lax.axis_index('tp')
    return dp, tp, tp // 2, tp % 2


def source(dz):
    return (here()[2] + 4 - dz) % 4


class Gather:
    def __init__(self, piece, g, send, recv, base):
        self.piece, self.g, self.send, self.recv, self.base = piece, g, send, recv, base
        self.dp, self.tp, self.z, self.c = here()
        x, y = self.dp // 2, self.dp % 2
        self.side = ((1 - x) * 2 + y, x * 2 + 1 - y)
        self.partner = (self.dp, 2 * self.z + 1 - self.c)
        self.quarters = g.shape[0]

    def rdma(self, k, src, dst, dev):
        return pltpu.make_async_remote_copy(src_ref=src, dst_ref=dst, send_sem=self.send.at[self.base + k],
                                            recv_sem=self.recv.at[self.base + k], device_id=dev, device_id_type=MESH)

    def local(self, q):
        return pltpu.make_async_copy(self.piece(q), self.g.at[q, self.tp], self.send.at[self.base + q])

    def own(self, q):
        return self.rdma(4 + q, self.piece(q), self.g.at[q, self.tp], self.partner)

    def line(self, dz):
        return self.rdma(7 + dz, self.piece(self.dp), self.g.at[self.dp, self.tp],
                         (self.dp, 2 * ((self.z + dz) % 4) + self.c))

    def cross(self, dz, n):
        ref = self.g.at[self.dp, 2 * source(dz) + self.c]
        return self.rdma(9 + 2 * dz + n, ref, ref, (self.side[n], self.tp))

    def relay(self, dz, n):
        half = self.g.shape[2] // 2
        ref = self.g.at[self.side[n], 2 * source(dz) + self.c, pl.ds(n * half, half)]
        return self.rdma(15 + 2 * dz + n, ref, ref, (self.side[1 - n], self.tp))

    def over(self, dz):
        ref = self.g.at[:, 2 * source(dz) + self.c]
        return self.rdma(22 + dz, ref, ref, self.partner)

    def peers(self):
        return ([(self.dp, 2 * ((self.z + dz) % 4) + self.c) for dz in (1, 2, 3)]
                + [(p, self.tp) for p in self.side] + [self.partner])

    def start(self):
        for dz in (1, 3, 2):
            self.line(dz).start()
        for q in range(self.quarters):
            self.own(q).start()
            self.local(q).start()

    def spread(self, dz):
        self.line(dz).wait_recv()
        for n in range(2):
            self.cross(dz, n).start()

    def pass_on(self, dz):
        for n in range(2):
            self.cross(dz, n).wait_recv()
            self.relay(dz, n).start()

    def hand(self, dz):
        for n in range(2):
            self.relay(dz, n).wait_recv()
        self.over(dz).start()

    def settle_own(self):
        for q in range(self.quarters):
            self.local(q).wait()
            self.own(q).wait_recv()

    def settle(self, dz):
        self.over(dz).wait_recv()

    def drain(self):
        for q in range(self.quarters):
            self.own(q).wait_send()
        for dz in (1, 2, 3):
            self.line(dz).wait_send()
            self.over(dz).wait_send()
            for n in range(2):
                self.cross(dz, n).wait_send()
                self.relay(dz, n).wait_send()

    def plan(self, s):
        s = bytes.fromhex(s)
        acts = [(s[0], self.start)]
        for k, f in enumerate((self.spread, self.pass_on, self.hand)):
            acts += [(s[1 + 3 * k + j], functools.partial(f, dz)) for j, dz in enumerate((1, 3, 2))]
        return acts

    def finish(self):
        self.settle_own()
        for dz in (1, 2, 3):
            self.settle(dz)
        self.drain()


class Small:
    def __init__(self, a, g, send, recv):
        self.a, self.g, self.send, self.recv = a, g, send, recv
        self.dp, self.tp, _, _ = here()

    def copy(self, k):
        return pltpu.make_async_remote_copy(src_ref=self.a, dst_ref=self.g.at[self.tp], send_sem=self.send.at[k],
                                            recv_sem=self.recv.at[k], device_id=(self.dp, (self.tp + k) % 8),
                                            device_id_type=MESH)

    def local(self):
        return pltpu.make_async_copy(self.a, self.g.at[self.tp], self.send.at[0])

    def peers(self):
        return [(self.dp, (self.tp + k) % 8) for k in range(1, 8)]

    def start(self):
        self.local().start()
        for k in range(1, 8):
            self.copy(k).start()

    def finish(self):
        self.local().wait()
        for k in range(1, 8):
            self.copy(k).wait()


def entry_barrier(peers):
    sem = pltpu.get_barrier_semaphore()
    for p in peers:
        pl.semaphore_signal(sem, inc=1, device_id=p, device_id_type=MESH)
    pl.semaphore_wait(sem, len(peers))


def at_steps(step, acts):
    for k in sorted({k for k, _ in acts}):
        @pl.when(step == k)
        def _():
            for j, f in acts:
                if j == k:
                    f()


def piece_rows(ref, layer):
    return lambda q: ref.at[layer, pl.ds(q * PC, PC)]


def piece_cols(ref, layer):
    return lambda q: ref.at[layer, :, pl.ds(pl.multiple_of(q * PC, PC) if not isinstance(q, int) else q * PC, PC)]


def p1_body(*refs, geom, mixed, layer, fetch_x, plans):
    n_dp, n_tp, heads, nb = geom
    (u_ref, halo_ref, nw_ref, wbc_ref, cbc_ref, bbc_ref, e3_ref), refs = refs[:7], refs[7:]
    if fetch_x:
        (ax, asm, az, ao), (y_ref, c_ref, ac_ref, send_ref), (gx, gs, gz, go), refs = refs[:4], refs[4:8], refs[8:12], refs[12:]
    else:
        (gx, gs, az, ao), (y_ref, c_ref, ac_ref, send_ref), (gz, go), refs = refs[:4], refs[4:8], refs[8:10], refs[10:]
    (wf, wb, wsem, sm, wdt, cst, st, hcar, xcar, qcar, aoff, ubuf, h_s, la1_s, la2_s, lb1_s, lb2_s, cc_s, cbd_s, row_s, aw_s,
     send, recv), sems = refs[:23], refs[23:]
    p, i = pl.program_id(0), pl.program_id(1)
    np_, ni = pl.num_programs(0), pl.num_programs(1)
    step = p * ni + i
    d_model = u_ref.shape[-1]
    quad = 2 * PC
    dz = p + p // 2 * (1 - 2 * (p % 2))
    zs = source(dz)

    zg = Gather(piece_rows(az, layer), gz, send, recv, 0)
    og = Gather(piece_cols(ao, layer), go, send, recv, SEMS)
    acts = zg.plan(plans[0]) + og.plan(plans[1])
    if fetch_x:
        xg = Gather(piece_rows(ax, layer), gx, send, recv, 2 * SEMS)
        small = Small(asm, gs, *sems)
        acts += xg.plan(plans[2])

    def load_w(slot, zsrc):
        return pltpu.make_async_copy(gx.at[:, pl.ds(2 * zsrc, 2)], wf.at[slot], wsem.at[slot])

    @pl.when(step == 0)
    def _():
        entry_barrier((small.peers() + [(s, here()[1]) for s in zg.side]) if fetch_x else zg.peers())
        if fetch_x:
            small.start()
    at_steps(step, acts)

    @pl.when(step == 0)
    def _():
        if fetch_x:
            small.finish()
            xg.settle_own()
        load_w(0, zs).start()
        cp = pltpu.make_async_copy(gs.at[:, pl.ds(layer * SMALL, SMALL)], sm, wsem.at[2])
        cp.start()
        cp.wait()
        kc = d_model // PC
        hp = heads // n_tp
        for t in range(n_tp):
            for k in range(hp):
                r = head_row(hp * t + k, heads)
                for c in range(kc):
                    wdt[r:r + 1, c * PC:(c + 1) * PC] = sm[t, 16 + kc * k + c:17 + kc * k + c, :].astype(BF16)
                cst[r:r + 1, :] = sm[t, 8 + k:9 + k, :]
                cst[heads + r:heads + r + 1, :] = sm[t, 12 + k:13 + k, :]
        aoff[...] = jnp.zeros_like(aoff)
        hh = rms(halo_ref[...], nw_ref[...])
        hcar[...] = hh
        qcar[...] = roll8(round_bf16(dot(hh, wbc_ref[...])))

    first = lax.broadcasted_iota(jnp.int32, (CAR, PC), 0) % 8 == 0

    def conv(cur, prev, taps, bias):
        a, now = conv_block(cur[:SUB], prev, taps, bias, first)
        b, now = conv_block(cur[SUB:], now, taps, bias, first)
        return silu(rows_cat(a, b)), now

    ri = lax.broadcasted_iota(jnp.int32, (BLK, BLK), 0)
    ci = lax.broadcasted_iota(jnp.int32, (BLK, BLK), 1)

    def prologue(b, h):
        j = i * NBS + b
        blk = pl.ds(pl.multiple_of(j * BLK, BLK), BLK)
        h_s[blk, :] = h
        rT = round_bf16(dott(wdt[...], h))
        bc, qcar[...] = conv(round_bf16(dot(h, wbc_ref[...])), qcar[...],
                             [cbc_ref[k:k + 1, :] for k in range(4)], bbc_ref[...])
        bmat, cmat = bc[:, :NST], bc[:, NST:]
        here_rows = slice(b * BLK, (b + 1) * BLK)
        c_ref[here_rows, :] = cmat
        pre = rT + cst[:heads, :BLK]
        dtT = jnp.maximum(pre, 0.0) + jnp.log1p(jnp.exp(-jnp.abs(pre)))
        aT = dtT * cst[heads:, :BLK]
        tr, tc = ri // SUB * SUB + time_of(ri % SUB), ci // SUB * SUB + time_of(ci % SUB)
        acT = dot(aT, jnp.where(tr <= tc, 1.0, 0.0), HI)
        mid, alast = acT[:, SUB - 1:SUB], acT[:, BLK - 1:BLK]
        low = ci[:heads] < SUB
        wT = dtT * jnp.exp2(jnp.where(low, mid, alast) - acT)
        pad = jnp.zeros((BLK - 3 * heads, BLK), BF16)
        aw_s[blk, :] = lanes_cat(rows_cat(*split3(acT), pad).T, rows_cat(*split3(wT), pad).T)
        ac_ref[:, here_rows] = acT + aoff[:, :1]
        aoff[...] = aoff[...] + alast

        def pair_rows(v):
            ev, od = v[:heads // 2], v[heads // 2:]
            l = low[:heads // 2]
            return jnp.where(l, ev, pltpu.roll(od, SUB, 1)), jnp.where(l, pltpu.roll(ev, SUB, 1), od)

        for half, (a, d) in enumerate(zip(pair_rows(acT), pair_rows(dtT))):
            row_s[2 * j + half] = rows_cat(*[v[4 * z:4 * z + 4] for z in range(heads // 8) for v in (a, d)])
        cb = dott(cmat, bmat, HI)
        lowr, tri = ci[:SUB] < SUB, time_of(ri[:SUB]) >= time_of(ci[:SUB] % SUB)
        ca, cd = cb[:SUB], cb[SUB:]
        cbd_s[blk, :] = rows_cat(jnp.where(tri, jnp.where(lowr, ca, pltpu.roll(ca, SUB, 1)), 0.0),
                                 jnp.where(tri, jnp.where(lowr, pltpu.roll(cd, SUB, 1), cd), 0.0))
        bT = bmat.T
        big = pl.ds(pl.multiple_of(j * (NST + SUB), SUB), NST + SUB)
        la1_s[big, :], la2_s[big, :] = kcat6(split3(rows_cat(bT[:, :SUB], cd[:, :SUB])))
        lb1_s[blk, :], lb2_s[blk, :] = kcat6(split3(pltpu.roll(bT, SUB, 1)[:, :SUB]))
        c1, c2, c3 = split3(cmat)
        cc_s[blk, :] = lanes_cat(c1, c2, c1, c3)

    @pl.when(p == 0)
    def _():
        u = u_ref[...].astype(F32)
        h = rms(u if mixed else unmix(u, ubuf), nw_ref[...])
        for b in range(NBS):
            prologue(b, h[b * BLK:(b + 1) * BLK])

    @pl.when(i == 0)
    def _():
        slot = p % 2
        load_w(slot, zs).wait()
        for q in range(n_dp):
            for k in range(2):
                wb[q * PC:(q + 1) * PC, k * PC:(k + 1) * PC] = wf[slot, q, k].astype(BF16)
        xcar[...] = roll8(round_bf16(dot(hcar[...], wb[...])))
        st[...] = jnp.zeros_like(st)

    @pl.when((i == ni - 1) & (p < np_ - 1))
    def _():
        nd = p + 1
        nd = nd + nd // 2 * (1 - 2 * (nd % 2))
        if fetch_x:
            for d in (1, 2, 3):
                pl.when(nd == d)(functools.partial(xg.settle, d))
        load_w((p + 1) % 2, source(nd)).start()

    lane = lax.broadcasted_iota(jnp.int32, (SUB, LANES), 1)
    lo = jnp.where(lane < HD, 1.0, 0.0).astype(BF16)
    hi = jnp.where(lane < HD, 0.0, 1.0).astype(BF16)
    x0 = [dot(h_s[pl.ds(pl.multiple_of(i * NBS * BLK, BLK), NBS * BLK), :], wb[:, k * PC:(k + 1) * PC]) for k in range(2)]

    def place(b):
        j = i * NBS + b
        return j, pl.ds(pl.multiple_of(j * BLK, BLK), BLK), pl.ds(pl.multiple_of(j * (NST + SUB), SUB), NST + SUB)

    def lanes_of(k):
        return slice(k * PC, (k + 1) * PC), pl.ds(pl.multiple_of((2 * zs + k) * PC, PC), PC)

    def pre(b, k):
        (_, blk, _), (sl, gl) = place(b), lanes_of(k)
        s1, s2, s3 = split3(st[:, sl])
        c12, c13 = cc_s[blk, :2 * NST], cc_s[blk, 2 * NST:]
        inter = dot(c12, rows_cat(s1, s1)) + dot(c12, rows_cat(s2, s2)) + dot(c13, rows_cat(s3, s1))
        n3 = e3_ref.shape[0]
        acx = dot(aw_s[blk, :n3], e3_ref[:, gl])
        wx = dot(aw_s[blk, BLK:BLK + n3], e3_ref[:, gl])
        return x0[k][b * BLK:(b + 1) * BLK], acx, wx, inter

    def mid_(b, k, x0, acx, wx, inter):
        (j, blk, _), (sl, _) = place(b), lanes_of(k)
        t = 2 * zs + k
        x, xcar[:, sl] = conv(round_bf16(x0), xcar[:, sl], [sm[t, r:r + 1, :] for r in range(4)], sm[t, 4:5, :])
        xw = split3(x * wx)
        r = kcat6r([v[:SUB] for v in xw]) + kcat6r([v[SUB:] for v in xw])
        ms, xs = [], []
        for half in range(2):
            rows = slice(half * SUB, (half + 1) * SUB)
            row = row_s[2 * j + half, pl.ds(pl.multiple_of(8 * zs, 8), 8), :]
            cbd = cbd_s[pl.ds(pl.multiple_of(j * BLK + half * SUB, SUB), SUB), :]
            m = []
            for g in range(2):
                seg = acx[rows, g * LANES:(g + 1) * LANES] - row[2 * k + g:2 * k + g + 1]
                m.append(jnp.exp2(jnp.minimum(seg, 0.0)) * cbd * row[4 + 2 * k + g:5 + 2 * k + g])
            ms.append(split3(lanes_cat(*m)))
            xs.append([block_diag(v, lo, hi) for v in split3(x[rows])])
        return x, acx, inter, r, ms, xs

    def fin(b, k, x, acx, inter, r, ms, xs):
        (j, blk, big), (sl, _) = place(b), lanes_of(k)
        ra = dot(la1_s[big, :], r[0]) + dot(la2_s[big, :], r[1])
        rb = dot(lb1_s[blk, :], r[2]) + dot(lb2_s[blk, :], r[3])
        am, al = acx[SUB - 1:SUB], acx[BLK - 1:BLK]
        st[:, sl] = st[:, sl] * jnp.exp2(al) + ra[:NST] * jnp.exp2(al - am) + rb
        skip = sm[2 * zs + k, 6:7, :]
        for half in range(2):
            rows = slice(half * SUB, (half + 1) * SUB)
            (m1, m2, m3), (x1, x2, x3) = ms[half], xs[half]
            r1 = dot(rows_cat(m1, m2, m3), x1)
            r2 = dot(rows_cat(m1, m2), x2)
            y = r1[:SUB] + r1[SUB:2 * SUB] + r1[2 * SUB:] + r2[:SUB] + r2[SUB:] + dot(m1, x3)
            y = y + inter[rows] * jnp.exp2(acx[rows])
            if half:
                y = y + ra[NST:] * jnp.exp2(acx[rows] - am)
            y_ref[b * BLK + half * SUB:b * BLK + (half + 1) * SUB, sl] = y + skip * x[rows]

    units = [(b, k) for b in range(NBS) for k in range(2)]
    m = mid_(*units[0], *pre(*units[0]))
    for a, nxt in zip(units, units[1:] + [None]):
        if nxt:
            v = pre(*nxt)
        fin(*a, *m)
        if nxt:
            m = mid_(*nxt, *v)

    @pl.when(i == ni - 1)
    def _():
        send_ref[...] = st[...]

    @pl.when(step == np_ * ni - 1)
    def _():
        zg.finish()
        og.finish()
        if fetch_x:
            xg.drain()


def p1(u, base, halo, nw, wbc, cbc, bbc, e3, comm, n, n_dp, n_tp, mixed, layer, fetch_x, plans, cid):
    d_model, heads = u.shape[1], PC // HD * n_tp
    width, nb, rows = PC * n_tp, n // BLK, BLK * NBS
    ni = nb // NBS
    fixed = lambda shp: pl.BlockSpec(shp, lambda p, i: (0,) * len(shp), pipeline_mode=pl.Buffered(1))
    once = lambda p, i: jnp.where(p == 0, i, ni - 1)
    col = lambda p: source(p + p // 2 * (1 - 2 * (p % 2)))
    hbm = pl.BlockSpec(memory_space=pl.ANY)
    gathered = lambda r: jax.ShapeDtypeStruct((n_dp, n_tp, r, PC), F32)
    outs = [jax.ShapeDtypeStruct((n, width), F32), jax.ShapeDtypeStruct((n, NST), F32),
            jax.ShapeDtypeStruct((heads, n), F32), jax.ShapeDtypeStruct((NST, width), F32)]
    more = ([gathered(PC), jax.ShapeDtypeStruct((n_tp,) + comm[1].shape, F32)] if fetch_x else []) + [gathered(PC)] * 2
    vm = pltpu.VMEM
    dma = lambda k: [pltpu.SemaphoreType.DMA((k,))] * 2
    return pl.pallas_call(
        functools.partial(p1_body, geom=(n_dp, n_tp, heads, nb), mixed=mixed, layer=layer, fetch_x=fetch_x, plans=plans),
        name="p1", grid=(4, ni),
        in_specs=[pl.BlockSpec((rows, d_model), lambda p, i: (base() + once(p, i), 0)),
                  fixed((CAR, d_model)), fixed((1, d_model)), fixed((d_model, PC)), fixed((4, PC)), fixed((1, PC)),
                  fixed((3 * heads, width))] + [hbm] * 4,
        out_specs=[pl.BlockSpec((rows, 2 * PC), lambda p, i: (i, col(p))),
                   pl.BlockSpec((rows, NST), lambda p, i: (once(p, i), 0)),
                   pl.BlockSpec((heads, rows), lambda p, i: (0, once(p, i))),
                   pl.BlockSpec((NST, 2 * PC), lambda p, i: (0, col(p)))] + [hbm] * len(more),
        out_shape=outs + more,
        scratch_shapes=[
            vm((2, n_dp, 2, PC, PC), F32), vm((d_model, 2 * PC), BF16), pltpu.SemaphoreType.DMA((3,)),
            vm((n_tp, SMALL, PC), F32), vm((heads, d_model), BF16), vm((2 * heads, PC), F32), vm((NST, 2 * PC), F32),
            vm((CAR, d_model), BF16), vm((CAR, 2 * PC), F32), vm((CAR, PC), F32), vm((heads, LANES), F32),
            vm((d_model // LANES * rows, LANES), F32), vm((n, d_model), BF16),
            vm((nb * (NST + SUB), 4 * SUB), BF16), vm((nb * (NST + SUB), 2 * SUB), BF16),
            vm((n, 4 * SUB), BF16), vm((n, 2 * SUB), BF16), vm((n, 4 * NST), BF16), vm((n, LANES), F32),
            vm((2 * nb, 2 * heads // 2, LANES), F32), vm((n, 2 * BLK), BF16)]
        + dma(3 * SEMS) + (dma(8) if fetch_x else []),
        compiler_params=pltpu.CompilerParams(dimension_semantics=("arbitrary", "arbitrary"), vmem_limit_bytes=VMEM_CAP,
                                             collective_id=cid, has_side_effects=True),
        cost_estimate=pl.CostEstimate(flops=n * 70 * 10 ** 6, bytes_accessed=n * 12000, transcendentals=0),
    )(u, halo, nw, wbc, cbc, bbc, e3, *comm)


def p2_body(*refs, geom, mix_in, layer, fetch_x, plans):
    n_dp, n_tp, heads = geom
    (u_ref, nw_ref, wz_ref, wo_ref, sm_ref, y_ref, c_ref, ac_ref, s_ref, e3_ref), refs = refs[:10], refs[10:]
    if fetch_x:
        (ax, o_ref, f_ref, gx), refs = refs[:4], refs[4:]
    else:
        (o_ref, r_ref), refs = refs[:2], refs[2:]
    (wzb, wob, s3, ubuf, send, recv), refs = refs[:6], refs[6:]
    i = pl.program_id(0)
    width = PC * n_tp
    if fetch_x:
        xg = Gather(piece_rows(ax, layer + 1), gx, send, recv, 0)

        @pl.when(i == 0)
        def _():
            entry_barrier(xg.peers())
        at_steps(i, xg.plan(plans))
    else:
        fbuf, = refs
        dp, tp, z, c = here()

        def swap(k):
            return pltpu.make_async_remote_copy(
                src_ref=fbuf.at[k % 2], dst_ref=r_ref.at[pl.ds(pl.multiple_of(k * BLK2, BLK2), BLK2)],
                send_sem=send.at[k % 2], recv_sem=recv.at[0], device_id=(dp, 2 * z + 1 - c), device_id_type=MESH)

        @pl.when(i == 0)
        def _():
            entry_barrier([(dp, 2 * z + 1 - c)])

        @pl.when(i > 1)
        def _():
            swap(i - 2).wait_send()

        @pl.when(i > 0)
        def _():
            swap(i - 1).start()

    @pl.when(i == 0)
    def _():
        for d in range(n_dp):
            for t in range(n_tp):
                a, b = slice(d * PC, (d + 1) * PC), slice(t * PC, (t + 1) * PC)
                wzb[a, b] = wz_ref[d, t].astype(BF16)
                wob[b, a] = wo_ref[d, t].astype(BF16)
        a, b, c_ = split3(s_ref[...])
        for k, (v, w) in enumerate(((a, a), (b, b), (c_, a))):
            s3[k] = rows_cat(v, w)

    u = u_ref[...].astype(F32)
    u = u if mix_in else unmix(u, ubuf)
    h = rms(u, nw_ref[...])
    c1, c2, c3 = split3(c_ref[...])
    c12, c13 = lanes_cat(c1, c2), lanes_cat(c1, c3)
    eT = rows_cat(*split3(jnp.exp2(ac_ref[...]))).T
    vs, ss = [], 0.0
    for t in range(n_tp):
        sl = slice(t * PC, (t + 1) * PC)
        z_ = round_bf16(dot(h, wzb[:, sl]))
        cor = dot(c12, s3[0, :, sl]) + dot(c12, s3[1, :, sl]) + dot(c13, s3[2, :, sl])
        v = (y_ref[:, sl] + cor * dot(eT, e3_ref[:, sl])) * silu(z_)
        ss = ss + jnp.sum(v * v, axis=-1, keepdims=True)
        vs.append(v)
    sc = lax.rsqrt(ss / width + EPS)
    g = lanes_cat(*[(v * sc * sm_ref[t, 5:6, :]).astype(BF16) for t, v in enumerate(vs)])
    un = round_bf16(u + dot(g, wob[...]))
    if fetch_x:
        o_ref[...] = un.astype(BF16)
        f_ref[...] = un[BLK2 - CAR:]
    else:
        fbuf[i % 2] = un
        o_ref[...] = unmix(un, ubuf).astype(BF16)

    @pl.when(i == pl.num_programs(0) - 1)
    def _():
        if fetch_x:
            xg.finish()
        else:
            swap(i).start()
            for k in range(2):
                swap(i - 1 + k).wait_send()
            whole = pltpu.make_async_copy(r_ref, r_ref, recv.at[0])
            whole.wait()


def p2(u, base, nw, wz, wo, sm, y, c, ac, s, e3, comm, n, n_dp, n_tp, mix_in, layer, fetch_x, plans, cid):
    d_model, heads = u.shape[1], PC // HD * n_tp
    width = PC * n_tp
    fixed = lambda shp: pl.BlockSpec(shp, lambda i: (0,) * len(shp), pipeline_mode=pl.Buffered(1))
    hbm = pl.BlockSpec(memory_space=pl.ANY)
    rows = lambda w: pl.BlockSpec((BLK2, w), lambda i: (i, 0))
    shape = lambda *s: jax.ShapeDtypeStruct(s, F32)
    vm = pltpu.VMEM
    outs = [jax.ShapeDtypeStruct((n, d_model), BF16)]
    specs = [rows(d_model)]
    if fetch_x:
        outs += [shape(CAR, d_model), shape(n_dp, n_tp, PC, PC)]
        specs += [pl.BlockSpec((CAR, d_model), lambda i: (0, 0)), hbm]
    else:
        outs += [shape(n, d_model)]
        specs += [hbm]
    return pl.pallas_call(
        functools.partial(p2_body, geom=(n_dp, n_tp, heads), mix_in=mix_in, layer=layer, fetch_x=fetch_x, plans=plans),
        name="p2", grid=(n // BLK2,),
        in_specs=[pl.BlockSpec((BLK2, d_model), lambda i: (base() + i, 0)), fixed((1, d_model)),
                  fixed((n_dp, n_tp, PC, PC)), fixed((n_dp, n_tp, PC, PC)),
                  pl.BlockSpec((n_tp, SMALL, PC), lambda i: (0, layer, 0), pipeline_mode=pl.Buffered(1)),
                  rows(width), rows(NST), pl.BlockSpec((heads, BLK2), lambda i: (0, i)),
                  fixed((NST, width)), fixed((3 * heads, width))] + [hbm] * len(comm),
        out_specs=specs, out_shape=outs,
        scratch_shapes=[vm((d_model, width), BF16), vm((width, d_model), BF16), vm((3, 2 * NST, width), BF16),
                        vm((d_model // LANES * BLK2, LANES), F32)]
        + [pltpu.SemaphoreType.DMA((SEMS,))] * 2 + ([] if fetch_x else [vm((2, BLK2, d_model), F32)]),
        compiler_params=pltpu.CompilerParams(dimension_semantics=("arbitrary",), vmem_limit_bytes=VMEM_CAP,
                                             collective_id=cid, has_side_effects=True),
        cost_estimate=pl.CostEstimate(flops=n * 30 * 10 ** 6, bytes_accessed=n * 12000, transcendentals=0),
    )(u, nw, wz, wo, sm, y, c, ac, s, e3, *comm)


def finish_body(own_ref, other_ref, o_ref, ubuf):
    mine = pl.program_id(0) == here()[3]

    @pl.when(mine)
    def _():
        o_ref[...] = own_ref[...]

    @pl.when(jnp.logical_not(mine))
    def _():
        o_ref[...] = unmix(other_ref[...], ubuf).astype(BF16)


def finish(own, other):
    n, d_model = own.shape
    rows = 512
    ni = n // rows
    pick = lambda w: (lambda j, i: (jnp.where((j == here()[3]) == w, i, ni - 1), 0))
    return pl.pallas_call(
        finish_body, name="finish", grid=(2, ni),
        in_specs=[pl.BlockSpec((rows, d_model), pick(True)), pl.BlockSpec((rows, d_model), pick(False))],
        out_specs=pl.BlockSpec((rows, d_model), lambda j, i: (j * ni + i, 0)),
        out_shape=jax.ShapeDtypeStruct((2 * n, d_model), BF16),
        scratch_shapes=[pltpu.VMEM((d_model // LANES * rows, LANES), F32)],
        compiler_params=pltpu.CompilerParams(dimension_semantics=("arbitrary", "arbitrary")),
        cost_estimate=pl.CostEstimate(flops=n * d_model, bytes_accessed=n * d_model * 8, transcendentals=0),
    )(own, other)


def small_rows(conv, bias, gate, skip, dtb, al, wdt):
    f = lambda v: v.astype(F32)
    hp = skip.shape[0]
    wide = lambda v: jnp.broadcast_to(v[:, None], (hp, PC))
    return rows_cat(f(conv), f(bias)[None], f(gate)[None], jnp.repeat(skip, HD)[None], jnp.zeros((1, PC), F32),
                    wide(dtb), wide(-jnp.exp(al) * LOG2E), f(wdt).T.reshape(-1, PC))


PLAN_X = "00020305030506040608"
PLAN_Z0 = "04090a0c0b0c0e0c0e10"
PLAN_O0 = "0a0e1012101214121416"
PLAN_Z1 = "00020305030507050709"
PLAN_O1 = "0407090b090b0d0b0d10"
PLAN_X1 = "00020305030506040608"


def solution(mesh):
    n_tp, n_dp = mesh.shape['tp'], mesh.shape['dp']
    rep, col, vec = P(), P(None, None, 'tp'), P(None, 'tp')
    in_specs = (P('dp'), rep, col, col, rep, col, col, rep, vec, rep, vec, vec, vec, vec, P(None, 'tp', None))

    def device_forward(hidden, norm_w, w_z, w_x, w_bc, w_dt, conv_x, conv_bc, bias_x, bias_bc, dt_bias, a_log, d_skip, gate_w, w_out):
        u = hidden[0]
        steps, d_model = u.shape
        n = steps // 2
        core = lax.axis_index('tp') % 2
        e3 = expand_mat(dt_bias.shape[1] * n_tp)
        up = [(2 * k, 2 * k + 1) for k in range(n_tp // 2)]
        ax, az, ao = w_x.astype(F32), w_z.astype(F32), w_out.astype(F32)
        small = rows_cat(*[small_rows(conv_x[l], bias_x[l], gate_w[l], d_skip[l], dt_bias[l], a_log[l], w_dt[l]) for l in range(2)])
        tail = u[n - SUB:n].astype(F32).reshape(8, 8, d_model).transpose(1, 0, 2).reshape(SUB, d_model)[SUB - CAR:]
        halo = jnp.where(core == 1, tail, 0.0)
        half = lambda blk: (lambda: lax.axis_index('tp') % 2 * (n // blk))
        none = lambda: 0
        row = lambda v: v.astype(F32)[None]
        common = (n, n_dp, n_tp)
        bc = lambda l: (row(norm_w[l]), w_bc[l], conv_bc[l].astype(F32), row(bias_bc[l]), e3)

        y, c, ac, s, gx, gs, gz, go = p1(u, half(BLK * NBS), halo, *bc(0), (ax, small, az, ao), *common, False, 0, True,
                                         (PLAN_Z0, PLAN_O0, PLAN_X), 1)
        s = lax.ppermute(s, 'tp', up)
        u, f, gx = p2(u, half(BLK2), row(norm_w[0]), gz, go, gs, y, c, ac, s, e3, (ax,), *common, False, 0, True, PLAN_X1, 2)
        halo = lax.ppermute(f, 'tp', up)
        y, c, ac, s, gz, go = p1(u, none, halo, *bc(1), (gx, gs, az, ao), *common, True, 1, False, (PLAN_Z1, PLAN_O1), 3)
        s = lax.ppermute(s, 'tp', up)
        own, other = p2(u, none, row(norm_w[1]), gz, go, gs, y, c, ac, s, e3, (), *common, True, 1, False, None, 4)
        return finish(own, other)[None]

    return jax.shard_map(device_forward, mesh=mesh, in_specs=in_specs, out_specs=P('dp'), check_vma=False)
```

time: 1450 us -> 498 us (0.34)
  waiting for transfers between devices: 976 us -> 4.66 us
  Pallas kernels: 0 us -> 460 us
  matrix products: 208 us -> 0 us
  local copies, waits for them, and re-layouts: 95.3 us -> 12.9 us
  other arithmetic: 92 us -> 14.5 us
  blocking collectives: 58.1 us -> 0 us
    psum x2 -> x0, waiting for transfers between devices: 976 us -> none  [mixer_layer(): full_out = lax.psum(part_out, 'tp')]
    pallas_call x0 -> x5, Pallas kernels: none -> 460 us  [the longest x2 304 us: p1(): pl.pallas_call(functools.partial(p1_body, geom=(n_dp, n_tp, heads, nb), m...]
    dot_general x20 -> x0, matrix products: 208 us -> none  [the longest x2 62.4 us: ssd_blocks(): jnp.einsum('bchij,bcjhp->bcihp', mix_mat, x_dt, precision=FULL_PRECISION)]
    psum x2 -> x0, blocking collectives: 58.1 us -> none  [mixer_layer(): total_sq = lax.psum(part_sq, 'tp')]
    reshape x7 -> x3, local copies, waits for them, and re-layouts: 49.5 us -> 0.3 us  [the longest x1 0.27 us: expand_mat(): one = jnp.repeat(jnp.eye(heads, dtype=BF16)[jnp.array(order)], HD, axis=1)]
    mul x8 -> x1, other arithmetic: 33.7 us -> 0.76 us  [small_rows(): -jnp.exp(al) * LOG2E]
    reduce_sum x2 -> x0, other arithmetic: 20.2 us -> none  [mixer_layer(): jnp.mean(residual * residual, axis=-1, keepdims=True) + EPSILON]
    another operation x10 -> x0, other arithmetic: 16.9 us -> none
  transfers between devices with their start and end apart: 2 -> 3, of which waited for: 2 -> 3; matrix products, arithmetic and copies ran while one was open for 0% -> 0% of each run, Pallas kernels for 0% -> 0%
where the time goes in v5:
time: 498 us; the launch traced here: 497 us
  Pallas kernels  460 us (92%)
  other arithmetic  14.5 us (3%)
  local copies, waits for them, and re-layouts  12.9 us (3%)
    pallas_call x2, Pallas kernels, p1(): pl.pallas_call(functools.partial(p1_body, geom=(n_dp, n_tp, heads, nb), m...  304 us
    pallas_call x2, Pallas kernels, p2(): pl.pallas_call(functools.partial(p2_body, geom=(n_dp, n_tp, heads), mix_i...  139 us
    pallas_call x1, Pallas kernels, finish(): pl.pallas_call(finish_body, name='finish', grid=(2, ni), in_specs=[pl.Blo...  16.7 us
  transfers between devices with their start and end apart: 3, of which 3 were waited for; matrix products, arithmetic and copies ran while one was open for 0% of the time, Pallas kernels for 0%

profile of v5, /device:TPU:0, one launch (start us, length us, event | category | flops | bytes accessed | tf_op | source)
XLA Modules:
  0.0 497.1 jit_solution(14675584204844032311)
XLA Ops:
  0.0 0.0 copy-start
  0.0 0.0 copy-start.2
  0.0 0.0 copy-start.3
  0.0 0.8 slice_bitcast_fusion.3
  0.8 0.8 multiply_bitcast_fusion
  1.6 0.8 slice_bitcast_fusion.4
  2.3 0.1 broadcast_in_dim.62
  2.4 0.1 broadcast_in_dim_reshape.7
  2.5 0.1 broadcast_in_dim.29
  2.6 0.1 broadcast_in_dim_reshape.6
  2.6 1.4 slice_convert_fusion.2
  4.0 0.7 pad_clamp_fusion
  4.7 1.4 slice_convert_fusion
  6.0 0.7 bitcast_convert_fusion.1
  6.7 1.3 bitcast_convert_fusion
  8.0 0.7 convert_bitcast_fusion
  8.8 0.9 slice_bitcast_fusion.2
  9.7 0.1 copy.19
  9.8 0.6 gather_fusion
  10.4 0.2 broadcast_in_dim.28
  10.6 0.3 reshape.61
  10.9 0.0 copy-start.1
  10.9 2.4 slice_bitcast_fusion
  13.3 2.7 convert_element_type.98.refs_9_
  16.0 2.7 convert_element_type.87.refs_7_.refs_10_
  18.7 0.0 copy-done
  18.7 1.6 convert_element_type.99.refs_10_
  20.3 0.0 copy-done.2
  20.3 0.0 copy-done.3
  20.3 0.6 select_bitcast_fusion.refs_1_
  21.0 0.1 broadcast_in_dim.65
  21.0 0.1 broadcast_in_dim.64
  21.1 0.1 broadcast_in_dim.61
  21.2 0.1 broadcast_in_dim.60
  21.2 3.6 concatenate.7.refs_8_
  24.9 0.0 copy-done.1
  24.9 176.3 %p1.2 = (f32[3072,2048]{1,0:T(8,128)}, f32[3072,128]{1,0:T(8,128)}, f32[32,3072]{1,0:T(8,128)}, f32[128,2048]{1,0:T(8,128)}, f32[4,8,256,256]{3,2,1,0:T(8,128)},...) custom-call(bf16[6144,1024]{1,0:T(8,128)(2,1)} %bitcast.48, ...), custom_call_target="tpu_custom_call" | custom-call | flops 215040000000 | bytes 36864000 | tf_op jit(solution)/shard_map/p1/pallas_call | solution.py:501
  201.1 1.5 collective-permute-start
  202.7 2.0 collective-permute-done.refs_8_
  204.7 0.0 copy-start.5
  204.7 1.0 copy-done.5
  205.7 77.6 %p2.2 = (bf16[3072,1024]{1,0:T(8,128)(2,1)}, f32[24,1024]{1,0:T(8,128)}, f32[4,8,256,256]{3,2,1,0:T(8,128)}) custom-call(bf16[6144,1024]{1,0:T(8,128)(2,1)} %bitcast.49, f32[1,1024]{1,0:T(1,128)} %get-tuple-element.48.refs_2_.refs_1_, f32[4,8,256,256]{3,2,1,0:T(8,128)} %get-tuple-element.23.refs_2_, f32[4,8,256,256]{3,2,1,0:T(8,128)} %get-tuple-element.24.refs_3_, ...), custom_call_target="tpu_custom_call" | custom-call | flops 92160000000 | bytes 36864000 | tf_op jit(solution)/shard_map/p2/pallas_call | solution.py:628
  283.3 1.5 collective-permute-start.1
  284.9 0.7 collective-permute-done.1.refs_1_
  285.6 0.0 copy-start.6
  285.6 0.6 copy-done.6
  286.2 128.1 %p1.3 = (f32[3072,2048]{1,0:T(8,128)}, f32[3072,128]{1,0:T(8,128)}, f32[32,3072]{1,0:T(8,128)}, f32[128,2048]{1,0:T(8,128)}, f32[4,8,256,256]{3,2,1,0:T(8,128)}, /*index=5*/f32[4,8,256,256]{3,2,1,0:T(8,128)}) custom-call(bf16[3072,1024]{1,0:T(8,128)(2,1)} %get-tuple-element.30.refs_0_, f32[24,1024]{1,0:T(8,128)} %copy-done.6, ...), custom_call_target="tpu_custom_call" | custom-call | flops 215040000000 | bytes 36864000 | tf_op jit(solution)/shard_map/p1/pallas_call | solution.py:501
  414.2 1.7 collective-permute-start.2
  416.0 1.9 collective-permute-done.2.refs_8_
  417.9 0.0 copy-start.4
  417.9 1.0 copy-done.4
  418.9 61.5 %p2.3 = (bf16[3072,1024]{1,0:T(8,128)(2,1)}, f32[3072,1024]{1,0:T(8,128)}) custom-call(bf16[3072,1024]{1,0:T(8,128)(2,1)} %get-tuple-element.30.refs_0_, f32[1,1024]{1,0:T(1,128)} %get-tuple-element.47.refs_2_.refs_1_, f32[4,8,256,256]{3,2,1,0:T(8,128)} %get-tuple-element.33.refs_2_, f32[4,8,256,256]{3,2,1,0:T(8,128)} %get-tuple-element.34.refs_3_, ...), custom_call_target="tpu_custom_call" | custom-call | flops 92160000000 | bytes 36864000 | tf_op jit(solution)/shard_map/p2/pallas_call | solution.py:628
  480.4 16.7 %finish.1 = bf16[6144,1024]{1,0:T(8,128)(2,1)} custom-call(bf16[3072,1024]{1,0:T(8,128)(2,1)} %get-tuple-element.39.own_ref, f32[3072,1024]{1,0:T(8,128)} %get-tuple-element.40.other_ref), custom_call_target="tpu_custom_call" | custom-call | flops 3145728 | bytes 25165824 | tf_op jit(solution)/shard_map/finish/pallas_call | solution.py:663
  (8 shorter events, 0.1 us)
Async XLA Ops:
  0.0 18.7 %copy-start = (bf16[2,256,1024]{2,1,0:T(8,128)(2,1)S(1)}, bf16[2,256,1024]{2,1,0:T(8,128)(2,1)}, u32[]{:S(2)}) copy-start(bf16[2,256,1024]{2,1,0:T(8,128)(2,1)} %param.30) | copy-start | bytes 3145732
  0.0 20.3 %copy-start.2 = (bf16[2,256]{1,0:T(2,128)(2,1)S(1)}, bf16[2,256]{1,0:T(2,128)(2,1)}, u32[]{:S(2)}) copy-start(bf16[2,256]{1,0:T(2,128)(2,1)} %param.29) | copy-start | bytes 3076
  0.0 20.3 %copy-start.3 = (bf16[2,256]{1,0:T(2,128)(2,1)S(1)}, bf16[2,256]{1,0:T(2,128)(2,1)}, u32[]{:S(2)}) copy-start(bf16[2,256]{1,0:T(2,128)(2,1)} %param.24) | copy-start | bytes 3076
  10.9 14.0 %copy-start.1 = (bf16[96,2048]{1,0:T(8,128)(2,1)}, bf16[96,2048]{1,0:T(8,128)(2,1)S(1)}, u32[]{:S(2)}) copy-start(bf16[96,2048]{1,0:T(8,128)(2,1)S(1)} %constant_dynamic-update-slice_fusion.refs_6_.refs_9_) | copy-start | bytes 1179652
  201.1 3.6 collective-permute-start
  204.7 1.0 copy-start.5
  283.3 2.2 collective-permute-start.1
  285.6 0.6 copy-start.6
  414.2 3.7 collective-permute-start.2
  417.9 1.0 copy-start.4

commit v6 on v5

--- a/solution.py
+++ b/solution.py
@@ -124,13 +124,13 @@
 
 
 class Gather:
-    def __init__(self, piece, g, send, recv, base):
+    def __init__(self, piece, g, send, recv, base, keep=True):
         self.piece, self.g, self.send, self.recv, self.base = piece, g, send, recv, base
         self.dp, self.tp, self.z, self.c = here()
         x, y = self.dp // 2, self.dp % 2
         self.side = ((1 - x) * 2 + y, x * 2 + 1 - y)
         self.partner = (self.dp, 2 * self.z + 1 - self.c)
-        self.quarters = g.shape[0]
+        self.quarters, self.keep = g.shape[0], keep
 
     def rdma(self, k, src, dst, dev):
         return pltpu.make_async_remote_copy(src_ref=src, dst_ref=dst, send_sem=self.send.at[self.base + k],
@@ -168,7 +168,8 @@
             self.line(dz).start()
         for q in range(self.quarters):
             self.own(q).start()
-            self.local(q).start()
+            if self.keep:
+                self.local(q).start()
 
     def spread(self, dz):
         self.line(dz).wait_recv()
@@ -187,8 +188,9 @@
 
     def settle_own(self):
         for q in range(self.quarters):
-            self.local(q).wait()
             self.own(q).wait_recv()
+            if self.keep:
+                self.local(q).wait()
 
     def settle(self, dz):
         self.over(dz).wait_recv()
@@ -274,7 +276,7 @@
     if fetch_x:
         (ax, asm, az, ao), (y_ref, c_ref, ac_ref, send_ref), (gx, gs, gz, go), refs = refs[:4], refs[4:8], refs[8:12], refs[12:]
     else:
-        (gx, gs, az, ao), (y_ref, c_ref, ac_ref, send_ref), (gz, go), refs = refs[:4], refs[4:8], refs[8:10], refs[10:]
+        (ax, gx, gs, az, ao), (y_ref, c_ref, ac_ref, send_ref), (gz, go), refs = refs[:5], refs[5:9], refs[9:11], refs[11:]
     (wf, wb, wsem, sm, wdt, cst, st, hcar, xcar, qcar, aoff, ubuf, h_s, la1_s, la2_s, lb1_s, lb2_s, cc_s, cbd_s, row_s, aw_s,
      send, recv), sems = refs[:23], refs[23:]
     p, i = pl.program_id(0), pl.program_id(1)
@@ -289,12 +291,17 @@
     og = Gather(piece_cols(ao, layer), go, send, recv, SEMS)
     acts = zg.plan(plans[0]) + og.plan(plans[1])
     if fetch_x:
-        xg = Gather(piece_rows(ax, layer), gx, send, recv, 2 * SEMS)
+        xg = Gather(piece_rows(ax, layer), gx, send, recv, 2 * SEMS, False)
         small = Small(asm, gs, *sems)
         acts += xg.plan(plans[2])
 
     def load_w(slot, zsrc):
         return pltpu.make_async_copy(gx.at[:, pl.ds(2 * zsrc, 2)], wf.at[slot], wsem.at[slot])
+
+    def load_own():
+        _, tp, _, c = here()
+        return ([pltpu.make_async_copy(piece_rows(ax, layer)(q), wf.at[0, q, c], wsem.at[0]) for q in range(n_dp)]
+                + [pltpu.make_async_copy(gx.at[q, tp + 1 - 2 * c], wf.at[0, q, 1 - c], wsem.at[0]) for q in range(n_dp)])
 
     @pl.when(step == 0)
     def _():
@@ -308,7 +315,8 @@
         if fetch_x:
             small.finish()
             xg.settle_own()
-        load_w(0, zs).start()
+        for v in load_own():
+            v.start()
         cp = pltpu.make_async_copy(gs.at[:, pl.ds(layer * SMALL, SMALL)], sm, wsem.at[2])
         cp.start()
         cp.wait()
@@ -388,7 +396,15 @@
     @pl.when(i == 0)
     def _():
         slot = p % 2
-        load_w(slot, zs).wait()
+
+        @pl.when(p == 0)
+        def _():
+            for v in load_own():
+                v.wait()
+
+        @pl.when(p > 0)
+        def _():
+            load_w(slot, zs).wait()
         for q in range(n_dp):
             for k in range(2):
                 wb[q * PC:(q + 1) * PC, k * PC:(k + 1) * PC] = wf[slot, q, k].astype(BF16)
@@ -503,7 +519,7 @@
         name="p1", grid=(4, ni),
         in_specs=[pl.BlockSpec((rows, d_model), lambda p, i: (base() + once(p, i), 0)),
                   fixed((CAR, d_model)), fixed((1, d_model)), fixed((d_model, PC)), fixed((4, PC)), fixed((1, PC)),
-                  fixed((3 * heads, width))] + [hbm] * 4,
+                  fixed((3 * heads, width))] + [hbm] * len(comm),
         out_specs=[pl.BlockSpec((rows, 2 * PC), lambda p, i: (i, col(p))),
                    pl.BlockSpec((rows, NST), lambda p, i: (once(p, i), 0)),
                    pl.BlockSpec((heads, rows), lambda p, i: (0, once(p, i))),
@@ -535,7 +551,7 @@
     i = pl.program_id(0)
     width = PC * n_tp
     if fetch_x:
-        xg = Gather(piece_rows(ax, layer + 1), gx, send, recv, 0)
+        xg = Gather(piece_rows(ax, layer + 1), gx, send, recv, 0, False)
 
         @pl.when(i == 0)
         def _():
@@ -594,8 +610,9 @@
         o_ref[...] = un.astype(BF16)
         f_ref[...] = un[BLK2 - CAR:]
     else:
+        un = unmix(un, ubuf)
         fbuf[i % 2] = un
-        o_ref[...] = unmix(un, ubuf).astype(BF16)
+        o_ref[...] = un.astype(BF16)
 
     @pl.when(i == pl.num_programs(0) - 1)
     def _():
@@ -643,7 +660,7 @@
     )(u, nw, wz, wo, sm, y, c, ac, s, e3, *comm)
 
 
-def finish_body(own_ref, other_ref, o_ref, ubuf):
+def finish_body(own_ref, other_ref, o_ref):
     mine = pl.program_id(0) == here()[3]
 
     @pl.when(mine)
@@ -652,7 +669,7 @@
 
     @pl.when(jnp.logical_not(mine))
     def _():
-        o_ref[...] = unmix(other_ref[...], ubuf).astype(BF16)
+        o_ref[...] = other_ref[...].astype(BF16)
 
 
 def finish(own, other):
@@ -665,7 +682,6 @@
         in_specs=[pl.BlockSpec((rows, d_model), pick(True)), pl.BlockSpec((rows, d_model), pick(False))],
         out_specs=pl.BlockSpec((rows, d_model), lambda j, i: (j * ni + i, 0)),
         out_shape=jax.ShapeDtypeStruct((2 * n, d_model), BF16),
-        scratch_shapes=[pltpu.VMEM((d_model // LANES * rows, LANES), F32)],
         compiler_params=pltpu.CompilerParams(dimension_semantics=("arbitrary", "arbitrary")),
         cost_estimate=pl.CostEstimate(flops=n * d_model, bytes_accessed=n * d_model * 8, transcendentals=0),
     )(own, other)
@@ -714,7 +730,7 @@
         s = lax.ppermute(s, 'tp', up)
         u, f, gx = p2(u, half(BLK2), row(norm_w[0]), gz, go, gs, y, c, ac, s, e3, (ax,), *common, False, 0, True, PLAN_X1, 2)
         halo = lax.ppermute(f, 'tp', up)
-        y, c, ac, s, gz, go = p1(u, none, halo, *bc(1), (gx, gs, az, ao), *common, True, 1, False, (PLAN_Z1, PLAN_O1), 3)
+        y, c, ac, s, gz, go = p1(u, none, halo, *bc(1), (ax, gx, gs, az, ao), *common, True, 1, False, (PLAN_Z1, PLAN_O1), 3)
         s = lax.ppermute(s, 'tp', up)
         own, other = p2(u, none, row(norm_w[1]), gz, go, gs, y, c, ac, s, e3, (), *common, True, 1, False, None, 4)
         return finish(own, other)[None]

time: 498 us -> 481 us (0.966)
  Pallas kernels: 460 us -> 442 us
    pallas_call x2, Pallas kernels: 304 us -> 281 us  [p1(): pl.pallas_call(functools.partial(p1_body, geom=(n_dp, n_tp, heads, nb), m...]
    pallas_call x2, Pallas kernels: 139 us -> 145 us  [p2(): pl.pallas_call(functools.partial(p2_body, geom=(n_dp, n_tp, heads), mix_i...]
where the time goes in v6:
time: 481 us; the launch traced here: 480 us
  Pallas kernels  442 us (92%)
  other arithmetic  14.5 us (3%)
  local copies, waits for them, and re-layouts  12.9 us (3%)
  starting transfers between devices  5.59 us (1%)
    pallas_call x2, Pallas kernels, p1(): pl.pallas_call(functools.partial(p1_body, geom=(n_dp, n_tp, heads, nb), m...  281 us
    pallas_call x2, Pallas kernels, p2(): pl.pallas_call(functools.partial(p2_body, geom=(n_dp, n_tp, heads), mix_i...  145 us
    pallas_call x1, Pallas kernels, finish(): pl.pallas_call(finish_body, name='finish', grid=(2, ni), in_specs=[pl.Blo...  15.5 us
  transfers between devices with their start and end apart: 3, of which 3 were waited for; matrix products, arithmetic and copies ran while one was open for 0% of the time, Pallas kernels for 0%

profile of v6, /device:TPU:0, one launch (start us, length us, event | category | flops | bytes accessed | tf_op | source)
XLA Modules:
  0.0 480.1 jit_solution(4037134222141923707)
XLA Ops:
  0.0 0.0 copy-start
  0.0 0.0 copy-start.2
  0.0 0.0 copy-start.3
  0.0 0.8 slice_bitcast_fusion.3
  0.8 0.8 multiply_bitcast_fusion
  1.6 0.8 slice_bitcast_fusion.4
  2.3 0.1 broadcast_in_dim.62
  2.4 0.1 broadcast_in_dim_reshape.7
  2.5 0.1 broadcast_in_dim.29
  2.6 0.1 broadcast_in_dim_reshape.6
  2.6 1.3 slice_convert_fusion.2
  4.0 0.7 pad_clamp_fusion
  4.6 1.4 slice_convert_fusion
  6.0 0.7 bitcast_convert_fusion.1
  6.7 1.3 bitcast_convert_fusion
  8.0 0.7 convert_bitcast_fusion
  8.8 0.9 slice_bitcast_fusion.2
  9.7 0.1 copy.19
  9.8 0.6 gather_fusion
  10.4 0.2 broadcast_in_dim.28
  10.6 0.3 reshape.61
  10.9 0.0 copy-start.1
  10.9 2.4 slice_bitcast_fusion
  13.3 2.7 convert_element_type.87.refs_7_.refs_10_
  16.0 2.7 convert_element_type.98.refs_9_.refs_10_
  18.7 0.0 copy-done
  18.7 1.6 convert_element_type.99.refs_10_.refs_11_
  20.3 0.0 copy-done.2
  20.3 0.0 copy-done.3
  20.3 0.6 select_bitcast_fusion.refs_1_
  20.9 0.1 broadcast_in_dim.65
  21.0 0.1 broadcast_in_dim.64
  21.1 0.1 broadcast_in_dim.61
  21.2 0.1 broadcast_in_dim.60
  21.2 3.6 concatenate.7.refs_8_
  24.9 0.0 copy-done.1
  24.9 153.4 %p1.2 = (f32[3072,2048]{1,0:T(8,128)}, f32[3072,128]{1,0:T(8,128)}, f32[32,3072]{1,0:T(8,128)}, f32[128,2048]{1,0:T(8,128)}, f32[4,8,256,256]{3,2,1,0:T(8,128)},...) custom-call(bf16[6144,1024]{1,0:T(8,128)(2,1)} %bitcast.48, ...), custom_call_target="tpu_custom_call" | custom-call | flops 215040000000 | bytes 36864000 | tf_op jit(solution)/shard_map/p1/pallas_call | solution.py:517
  178.2 2.4 collective-permute-start
  180.6 2.0 collective-permute-done.refs_8_
  182.6 0.0 copy-start.5
  182.6 1.0 copy-done.5
  183.6 83.7 %p2.2 = (bf16[3072,1024]{1,0:T(8,128)(2,1)}, f32[24,1024]{1,0:T(8,128)}, f32[4,8,256,256]{3,2,1,0:T(8,128)}) custom-call(bf16[6144,1024]{1,0:T(8,128)(2,1)} %bitcast.49, f32[1,1024]{1,0:T(1,128)} %get-tuple-element.48.refs_2_.refs_1_, f32[4,8,256,256]{3,2,1,0:T(8,128)} %get-tuple-element.23.refs_2_, f32[4,8,256,256]{3,2,1,0:T(8,128)} %get-tuple-element.24.refs_3_, ...), custom_call_target="tpu_custom_call" | custom-call | flops 92160000000 | bytes 36864000 | tf_op jit(solution)/shard_map/p2/pallas_call | solution.py:645
  267.3 1.5 collective-permute-start.1
  268.8 0.7 collective-permute-done.1.refs_1_
  269.5 0.0 copy-start.6
  269.5 0.6 copy-done.6
  270.1 128.1 %p1.3 = (f32[3072,2048]{1,0:T(8,128)}, f32[3072,128]{1,0:T(8,128)}, f32[32,3072]{1,0:T(8,128)}, f32[128,2048]{1,0:T(8,128)}, f32[4,8,256,256]{3,2,1,0:T(8,128)}, /*index=5*/f32[4,8,256,256]{3,2,1,0:T(8,128)}) custom-call(bf16[3072,1024]{1,0:T(8,128)(2,1)} %get-tuple-element.30.refs_0_, f32[24,1024]{1,0:T(8,128)} %copy-done.6, ...), custom_call_target="tpu_custom_call" | custom-call | flops 215040000000 | bytes 36864000 | tf_op jit(solution)/shard_map/p1/pallas_call | solution.py:517
  398.2 1.7 collective-permute-start.2
  399.9 1.9 collective-permute-done.2.refs_8_
  401.9 0.0 copy-start.4
  401.9 1.0 copy-done.4
  402.9 61.7 %p2.3 = (bf16[3072,1024]{1,0:T(8,128)(2,1)}, f32[3072,1024]{1,0:T(8,128)}) custom-call(bf16[3072,1024]{1,0:T(8,128)(2,1)} %get-tuple-element.30.refs_0_, f32[1,1024]{1,0:T(1,128)} %get-tuple-element.47.refs_2_.refs_1_, f32[4,8,256,256]{3,2,1,0:T(8,128)} %get-tuple-element.33.refs_2_, f32[4,8,256,256]{3,2,1,0:T(8,128)} %get-tuple-element.34.refs_3_, ...), custom_call_target="tpu_custom_call" | custom-call | flops 92160000000 | bytes 36864000 | tf_op jit(solution)/shard_map/p2/pallas_call | solution.py:645
  464.6 15.5 %finish.1 = bf16[6144,1024]{1,0:T(8,128)(2,1)} custom-call(bf16[3072,1024]{1,0:T(8,128)(2,1)} %get-tuple-element.39.own_ref, f32[3072,1024]{1,0:T(8,128)} %get-tuple-element.40.other_ref), custom_call_target="tpu_custom_call" | custom-call | flops 3145728 | bytes 25165824 | tf_op jit(solution)/shard_map/finish/pallas_call | solution.py:680
  (8 shorter events, 0.1 us)
Async XLA Ops:
  0.0 18.7 %copy-start = (bf16[2,256,1024]{2,1,0:T(8,128)(2,1)S(1)}, bf16[2,256,1024]{2,1,0:T(8,128)(2,1)}, u32[]{:S(2)}) copy-start(bf16[2,256,1024]{2,1,0:T(8,128)(2,1)} %param.30) | copy-start | bytes 3145732
  0.0 20.3 %copy-start.2 = (bf16[2,256]{1,0:T(2,128)(2,1)S(1)}, bf16[2,256]{1,0:T(2,128)(2,1)}, u32[]{:S(2)}) copy-start(bf16[2,256]{1,0:T(2,128)(2,1)} %param.29) | copy-start | bytes 3076
  0.0 20.3 %copy-start.3 = (bf16[2,256]{1,0:T(2,128)(2,1)S(1)}, bf16[2,256]{1,0:T(2,128)(2,1)}, u32[]{:S(2)}) copy-start(bf16[2,256]{1,0:T(2,128)(2,1)} %param.24) | copy-start | bytes 3076
  10.9 14.0 %copy-start.1 = (bf16[96,2048]{1,0:T(8,128)(2,1)}, bf16[96,2048]{1,0:T(8,128)(2,1)S(1)}, u32[]{:S(2)}) copy-start(bf16[96,2048]{1,0:T(8,128)(2,1)S(1)} %constant_dynamic-update-slice_fusion.refs_6_.refs_9_) | copy-start | bytes 1179652
  178.2 4.4 collective-permute-start
  182.6 1.0 copy-start.5
  267.3 2.2 collective-permute-start.1
  269.5 0.6 copy-start.6
  398.2 3.7 collective-permute-start.2
  401.9 1.0 copy-start.4

commit v7 on v6

--- a/solution.py
+++ b/solution.py
@@ -1,6 +1,7 @@
 import functools
 import jax
 import jax.numpy as jnp
+import numpy as np
 from jax import lax
 from jax.experimental import pallas as pl
 from jax.experimental.pallas import tpu as pltpu
@@ -94,8 +95,8 @@
 
 def expand_mat(heads):
     order = sorted(range(heads), key=lambda h: head_row(h, heads))
-    one = jnp.repeat(jnp.eye(heads, dtype=BF16)[jnp.array(order)], HD, axis=1)
-    return rows_cat(one, one, one)
+    one = np.repeat(np.eye(heads)[order], HD, axis=1)
+    return jnp.asarray(np.tile(one, (3, 1)), BF16)
 
 
 def kcat6(parts):
@@ -164,11 +165,12 @@
                 + [(p, self.tp) for p in self.side] + [self.partner])
 
     def start(self):
+        for q in range(self.quarters):
+            self.own(q).start()
         for dz in (1, 3, 2):
             self.line(dz).start()
-        for q in range(self.quarters):
-            self.own(q).start()
-            if self.keep:
+        if self.keep:
+            for q in range(self.quarters):
                 self.local(q).start()
 
     def spread(self, dz):
@@ -271,8 +273,9 @@
 
 
 def p1_body(*refs, geom, mixed, layer, fetch_x, plans):
-    n_dp, n_tp, heads, nb = geom
+    n_dp, n_tp, heads, nb, nbs, sp = geom
     (u_ref, halo_ref, nw_ref, wbc_ref, cbc_ref, bbc_ref, e3_ref), refs = refs[:7], refs[7:]
+    nw, cbc, bbc = nw_ref[...].astype(F32), cbc_ref[...].astype(F32), bbc_ref[...].astype(F32)
     if fetch_x:
         (ax, asm, az, ao), (y_ref, c_ref, ac_ref, send_ref), (gx, gs, gz, go), refs = refs[:4], refs[4:8], refs[8:12], refs[12:]
     else:
@@ -283,9 +286,8 @@
     np_, ni = pl.num_programs(0), pl.num_programs(1)
     step = p * ni + i
     d_model = u_ref.shape[-1]
-    quad = 2 * PC
-    dz = p + p // 2 * (1 - 2 * (p % 2))
-    zs = source(dz)
+    by_z = sp < n_tp
+    zs = source(p + p // 2 * (1 - 2 * (p % 2))) if by_z else 0
 
     zg = Gather(piece_rows(az, layer), gz, send, recv, 0)
     og = Gather(piece_cols(ao, layer), go, send, recv, SEMS)
@@ -296,7 +298,7 @@
         acts += xg.plan(plans[2])
 
     def load_w(slot, zsrc):
-        return pltpu.make_async_copy(gx.at[:, pl.ds(2 * zsrc, 2)], wf.at[slot], wsem.at[slot])
+        return pltpu.make_async_copy(gx.at[:, pl.ds(2 * zsrc, sp)], wf.at[slot], wsem.at[slot])
 
     def load_own():
         _, tp, _, c = here()
@@ -315,8 +317,11 @@
         if fetch_x:
             small.finish()
             xg.settle_own()
-        for v in load_own():
-            v.start()
+        if by_z:
+            for v in load_own():
+                v.start()
+        else:
+            load_w(0, 0).start()
         cp = pltpu.make_async_copy(gs.at[:, pl.ds(layer * SMALL, SMALL)], sm, wsem.at[2])
         cp.start()
         cp.wait()
@@ -330,7 +335,7 @@
                 cst[r:r + 1, :] = sm[t, 8 + k:9 + k, :]
                 cst[heads + r:heads + r + 1, :] = sm[t, 12 + k:13 + k, :]
         aoff[...] = jnp.zeros_like(aoff)
-        hh = rms(halo_ref[...], nw_ref[...])
+        hh = rms(halo_ref[...], nw)
         hcar[...] = hh
         qcar[...] = roll8(round_bf16(dot(hh, wbc_ref[...])))
 
@@ -345,12 +350,12 @@
     ci = lax.broadcasted_iota(jnp.int32, (BLK, BLK), 1)
 
     def prologue(b, h):
-        j = i * NBS + b
+        j = i * nbs + b
         blk = pl.ds(pl.multiple_of(j * BLK, BLK), BLK)
         h_s[blk, :] = h
         rT = round_bf16(dott(wdt[...], h))
         bc, qcar[...] = conv(round_bf16(dot(h, wbc_ref[...])), qcar[...],
-                             [cbc_ref[k:k + 1, :] for k in range(4)], bbc_ref[...])
+                             [cbc[k:k + 1] for k in range(4)], bbc)
         bmat, cmat = bc[:, :NST], bc[:, NST:]
         here_rows = slice(b * BLK, (b + 1) * BLK)
         c_ref[here_rows, :] = cmat
@@ -386,27 +391,29 @@
         c1, c2, c3 = split3(cmat)
         cc_s[blk, :] = lanes_cat(c1, c2, c1, c3)
 
-    @pl.when(p == 0)
-    def _():
+    def all_prologues():
         u = u_ref[...].astype(F32)
-        h = rms(u if mixed else unmix(u, ubuf), nw_ref[...])
-        for b in range(NBS):
+        h = rms(u if mixed else unmix(u, ubuf), nw)
+        for b in range(nbs):
             prologue(b, h[b * BLK:(b + 1) * BLK])
 
+    if by_z:
+        pl.when(p == 0)(all_prologues)
+
     @pl.when(i == 0)
     def _():
-        slot = p % 2
+        slot = p % 2 if by_z else 0
 
         @pl.when(p == 0)
         def _():
-            for v in load_own():
+            for v in load_own() if by_z else [load_w(0, 0)]:
                 v.wait()
 
         @pl.when(p > 0)
         def _():
             load_w(slot, zs).wait()
         for q in range(n_dp):
-            for k in range(2):
+            for k in range(sp):
                 wb[q * PC:(q + 1) * PC, k * PC:(k + 1) * PC] = wf[slot, q, k].astype(BF16)
         xcar[...] = roll8(round_bf16(dot(hcar[...], wb[...])))
         st[...] = jnp.zeros_like(st)
@@ -420,13 +427,15 @@
                 pl.when(nd == d)(functools.partial(xg.settle, d))
         load_w((p + 1) % 2, source(nd)).start()
 
+    if not by_z:
+        all_prologues()
     lane = lax.broadcasted_iota(jnp.int32, (SUB, LANES), 1)
     lo = jnp.where(lane < HD, 1.0, 0.0).astype(BF16)
     hi = jnp.where(lane < HD, 0.0, 1.0).astype(BF16)
-    x0 = [dot(h_s[pl.ds(pl.multiple_of(i * NBS * BLK, BLK), NBS * BLK), :], wb[:, k * PC:(k + 1) * PC]) for k in range(2)]
+    x0 = [dot(h_s[pl.ds(pl.multiple_of(i * nbs * BLK, BLK), nbs * BLK), :], wb[:, k * PC:(k + 1) * PC]) for k in range(sp)]
 
     def place(b):
-        j = i * NBS + b
+        j = i * nbs + b
         return j, pl.ds(pl.multiple_of(j * BLK, BLK), BLK), pl.ds(pl.multiple_of(j * (NST + SUB), SUB), NST + SUB)
 
     def lanes_of(k):
@@ -451,12 +460,12 @@
         ms, xs = [], []
         for half in range(2):
             rows = slice(half * SUB, (half + 1) * SUB)
-            row = row_s[2 * j + half, pl.ds(pl.multiple_of(8 * zs, 8), 8), :]
+            row = row_s[2 * j + half, pl.ds(pl.multiple_of(8 * (zs + k // 2), 8), 8), :]
             cbd = cbd_s[pl.ds(pl.multiple_of(j * BLK + half * SUB, SUB), SUB), :]
             m = []
             for g in range(2):
-                seg = acx[rows, g * LANES:(g + 1) * LANES] - row[2 * k + g:2 * k + g + 1]
-                m.append(jnp.exp2(jnp.minimum(seg, 0.0)) * cbd * row[4 + 2 * k + g:5 + 2 * k + g])
+                seg = acx[rows, g * LANES:(g + 1) * LANES] - row[2 * (k % 2) + g:2 * (k % 2) + g + 1]
+                m.append(jnp.exp2(jnp.minimum(seg, 0.0)) * cbd * row[4 + 2 * (k % 2) + g:5 + 2 * (k % 2) + g])
             ms.append(split3(lanes_cat(*m)))
             xs.append([block_diag(v, lo, hi) for v in split3(x[rows])])
         return x, acx, inter, r, ms, xs
@@ -479,7 +488,7 @@
                 y = y + ra[NST:] * jnp.exp2(acx[rows] - am)
             y_ref[b * BLK + half * SUB:b * BLK + (half + 1) * SUB, sl] = y + skip * x[rows]
 
-    units = [(b, k) for b in range(NBS) for k in range(2)]
+    units = [(b, k) for b in range(nbs) for k in range(sp)]
     m = mid_(*units[0], *pre(*units[0]))
     for a, nxt in zip(units, units[1:] + [None]):
         if nxt:
@@ -501,12 +510,14 @@
 
 
 def p1(u, base, halo, nw, wbc, cbc, bbc, e3, comm, n, n_dp, n_tp, mixed, layer, fetch_x, plans, cid):
-    d_model, heads = u.shape[1], PC // HD * n_tp
-    width, nb, rows = PC * n_tp, n // BLK, BLK * NBS
-    ni = nb // NBS
+    d_model, heads = u.shape[-1], PC // HD * n_tp
+    sp, nbs = (2, NBS) if fetch_x else (n_tp, 1)
+    width, nb, rows = PC * n_tp, n // BLK, BLK * nbs
+    ni = nb // nbs
     fixed = lambda shp: pl.BlockSpec(shp, lambda p, i: (0,) * len(shp), pipeline_mode=pl.Buffered(1))
+    own_layer = lambda *shp: pl.BlockSpec((None,) + shp, lambda p, i: (layer, 0, 0), pipeline_mode=pl.Buffered(1))
     once = lambda p, i: jnp.where(p == 0, i, ni - 1)
-    col = lambda p: source(p + p // 2 * (1 - 2 * (p % 2)))
+    col = (lambda p: source(p + p // 2 * (1 - 2 * (p % 2)))) if fetch_x else (lambda p: 0)
     hbm = pl.BlockSpec(memory_space=pl.ANY)
     gathered = lambda r: jax.ShapeDtypeStruct((n_dp, n_tp, r, PC), F32)
     outs = [jax.ShapeDtypeStruct((n, width), F32), jax.ShapeDtypeStruct((n, NST), F32),
@@ -515,20 +526,20 @@
     vm = pltpu.VMEM
     dma = lambda k: [pltpu.SemaphoreType.DMA((k,))] * 2
     return pl.pallas_call(
-        functools.partial(p1_body, geom=(n_dp, n_tp, heads, nb), mixed=mixed, layer=layer, fetch_x=fetch_x, plans=plans),
-        name="p1", grid=(4, ni),
+        functools.partial(p1_body, geom=(n_dp, n_tp, heads, nb, nbs, sp), mixed=mixed, layer=layer, fetch_x=fetch_x, plans=plans),
+        name="p1", grid=(n_tp // sp, ni),
         in_specs=[pl.BlockSpec((rows, d_model), lambda p, i: (base() + once(p, i), 0)),
-                  fixed((CAR, d_model)), fixed((1, d_model)), fixed((d_model, PC)), fixed((4, PC)), fixed((1, PC)),
+                  fixed((CAR, d_model)), own_layer(1, d_model), own_layer(d_model, PC), own_layer(4, PC), own_layer(1, PC),
                   fixed((3 * heads, width))] + [hbm] * len(comm),
-        out_specs=[pl.BlockSpec((rows, 2 * PC), lambda p, i: (i, col(p))),
+        out_specs=[pl.BlockSpec((rows, sp * PC), lambda p, i: (i, col(p))),
                    pl.BlockSpec((rows, NST), lambda p, i: (once(p, i), 0)),
                    pl.BlockSpec((heads, rows), lambda p, i: (0, once(p, i))),
-                   pl.BlockSpec((NST, 2 * PC), lambda p, i: (0, col(p)))] + [hbm] * len(more),
+                   pl.BlockSpec((NST, sp * PC), lambda p, i: (0, col(p)))] + [hbm] * len(more),
         out_shape=outs + more,
         scratch_shapes=[
-            vm((2, n_dp, 2, PC, PC), F32), vm((d_model, 2 * PC), BF16), pltpu.SemaphoreType.DMA((3,)),
-            vm((n_tp, SMALL, PC), F32), vm((heads, d_model), BF16), vm((2 * heads, PC), F32), vm((NST, 2 * PC), F32),
-            vm((CAR, d_model), BF16), vm((CAR, 2 * PC), F32), vm((CAR, PC), F32), vm((heads, LANES), F32),
+            vm((2 if fetch_x else 1, n_dp, sp, PC, PC), F32), vm((d_model, sp * PC), BF16), pltpu.SemaphoreType.DMA((3,)),
+            vm((n_tp, SMALL, PC), F32), vm((heads, d_model), BF16), vm((2 * heads, PC), F32), vm((NST, sp * PC), F32),
+            vm((CAR, d_model), BF16), vm((CAR, sp * PC), F32), vm((CAR, PC), F32), vm((heads, LANES), F32),
             vm((d_model // LANES * rows, LANES), F32), vm((n, d_model), BF16),
             vm((nb * (NST + SUB), 4 * SUB), BF16), vm((nb * (NST + SUB), 2 * SUB), BF16),
             vm((n, 4 * SUB), BF16), vm((n, 2 * SUB), BF16), vm((n, 4 * NST), BF16), vm((n, LANES), F32),
@@ -551,7 +562,7 @@
     i = pl.program_id(0)
     width = PC * n_tp
     if fetch_x:
-        xg = Gather(piece_rows(ax, layer + 1), gx, send, recv, 0, False)
+        xg = Gather(piece_rows(ax, layer + 1), gx, send, recv, 0)
 
         @pl.when(i == 0)
         def _():
@@ -591,7 +602,7 @@
 
     u = u_ref[...].astype(F32)
     u = u if mix_in else unmix(u, ubuf)
-    h = rms(u, nw_ref[...])
+    h = rms(u, nw_ref[...].astype(F32))
     c1, c2, c3 = split3(c_ref[...])
     c12, c13 = lanes_cat(c1, c2), lanes_cat(c1, c3)
     eT = rows_cat(*split3(jnp.exp2(ac_ref[...]))).T
@@ -627,7 +638,7 @@
 
 
 def p2(u, base, nw, wz, wo, sm, y, c, ac, s, e3, comm, n, n_dp, n_tp, mix_in, layer, fetch_x, plans, cid):
-    d_model, heads = u.shape[1], PC // HD * n_tp
+    d_model, heads = u.shape[-1], PC // HD * n_tp
     width = PC * n_tp
     fixed = lambda shp: pl.BlockSpec(shp, lambda i: (0,) * len(shp), pipeline_mode=pl.Buffered(1))
     hbm = pl.BlockSpec(memory_space=pl.ANY)
@@ -645,7 +656,8 @@
     return pl.pallas_call(
         functools.partial(p2_body, geom=(n_dp, n_tp, heads), mix_in=mix_in, layer=layer, fetch_x=fetch_x, plans=plans),
         name="p2", grid=(n // BLK2,),
-        in_specs=[pl.BlockSpec((BLK2, d_model), lambda i: (base() + i, 0)), fixed((1, d_model)),
+        in_specs=[pl.BlockSpec((BLK2, d_model), lambda i: (base() + i, 0)),
+                  pl.BlockSpec((None, 1, d_model), lambda i: (layer, 0, 0)),
                   fixed((n_dp, n_tp, PC, PC)), fixed((n_dp, n_tp, PC, PC)),
                   pl.BlockSpec((n_tp, SMALL, PC), lambda i: (0, layer, 0), pipeline_mode=pl.Buffered(1)),
                   rows(width), rows(NST), pl.BlockSpec((heads, BLK2), lambda i: (0, i)),
@@ -674,7 +686,7 @@
 
 def finish(own, other):
     n, d_model = own.shape
-    rows = 512
+    rows = n // 3
     ni = n // rows
     pick = lambda w: (lambda j, i: (jnp.where((j == here()[3]) == w, i, ni - 1), 0))
     return pl.pallas_call(
@@ -689,18 +701,21 @@
 
 def small_rows(conv, bias, gate, skip, dtb, al, wdt):
     f = lambda v: v.astype(F32)
-    hp = skip.shape[0]
-    wide = lambda v: jnp.broadcast_to(v[:, None], (hp, PC))
-    return rows_cat(f(conv), f(bias)[None], f(gate)[None], jnp.repeat(skip, HD)[None], jnp.zeros((1, PC), F32),
-                    wide(dtb), wide(-jnp.exp(al) * LOG2E), f(wdt).T.reshape(-1, PC))
-
-
-PLAN_X = "00020305030506040608"
-PLAN_Z0 = "04090a0c0b0c0e0c0e10"
-PLAN_O0 = "0a0e1012101214121416"
-PLAN_Z1 = "00020305030507050709"
-PLAN_O1 = "0407090b090b0d0b0d10"
-PLAN_X1 = "00020305030506040608"
+    n, hp = skip.shape
+    wide = lambda v: jnp.broadcast_to(v[:, :, None], (n, hp, PC))
+    one = lambda v: v.reshape(n, 1, PC)
+    skip = jnp.broadcast_to(skip[:, :, None], (n, hp, HD))
+    v = [f(conv), one(f(bias)), one(f(gate)), one(skip), jnp.zeros((n, 1, PC), F32), wide(dtb), wide(-jnp.exp(al) * LOG2E),
+         f(wdt).transpose(0, 2, 1).reshape(n, -1, PC)]
+    return jnp.concatenate(v, axis=1).reshape(-1, PC)
+
+
+PLAN_X = "00020405030607040809"
+PLAN_Z0 = "04090a0c0b0c0e0d0e10"
+PLAN_O0 = "090d0f110f1113111315"
+PLAN_Z1 = "0002040604060906080b"
+PLAN_O1 = "06090b0e0b0e100d1013"
+PLAN_X1 = "0003050705070907090a"
 
 
 def solution(mesh):
@@ -716,23 +731,24 @@
         e3 = expand_mat(dt_bias.shape[1] * n_tp)
         up = [(2 * k, 2 * k + 1) for k in range(n_tp // 2)]
         ax, az, ao = w_x.astype(F32), w_z.astype(F32), w_out.astype(F32)
-        small = rows_cat(*[small_rows(conv_x[l], bias_x[l], gate_w[l], d_skip[l], dt_bias[l], a_log[l], w_dt[l]) for l in range(2)])
+        small = small_rows(conv_x, bias_x, gate_w, d_skip, dt_bias, a_log, w_dt)
         tail = u[n - SUB:n].astype(F32).reshape(8, 8, d_model).transpose(1, 0, 2).reshape(SUB, d_model)[SUB - CAR:]
         halo = jnp.where(core == 1, tail, 0.0)
         half = lambda blk: (lambda: lax.axis_index('tp') % 2 * (n // blk))
         none = lambda: 0
-        row = lambda v: v.astype(F32)[None]
+        row = lambda v: v.reshape(v.shape[0], 1, v.shape[1])
         common = (n, n_dp, n_tp)
-        bc = lambda l: (row(norm_w[l]), w_bc[l], conv_bc[l].astype(F32), row(bias_bc[l]), e3)
-
-        y, c, ac, s, gx, gs, gz, go = p1(u, half(BLK * NBS), halo, *bc(0), (ax, small, az, ao), *common, False, 0, True,
+        nw = row(norm_w)
+        bc = (nw, w_bc, conv_bc, row(bias_bc), e3)
+
+        y, c, ac, s, gx, gs, gz, go = p1(u, half(BLK * NBS), halo, *bc, (ax, small, az, ao), *common, False, 0, True,
                                          (PLAN_Z0, PLAN_O0, PLAN_X), 1)
         s = lax.ppermute(s, 'tp', up)
-        u, f, gx = p2(u, half(BLK2), row(norm_w[0]), gz, go, gs, y, c, ac, s, e3, (ax,), *common, False, 0, True, PLAN_X1, 2)
+        u, f, gx = p2(u, half(BLK2), nw, gz, go, gs, y, c, ac, s, e3, (ax,), *common, False, 0, True, PLAN_X1, 2)
         halo = lax.ppermute(f, 'tp', up)
-        y, c, ac, s, gz, go = p1(u, none, halo, *bc(1), (ax, gx, gs, az, ao), *common, True, 1, False, (PLAN_Z1, PLAN_O1), 3)
+        y, c, ac, s, gz, go = p1(u, none, halo, *bc, (ax, gx, gs, az, ao), *common, True, 1, False, (PLAN_Z1, PLAN_O1), 3)
         s = lax.ppermute(s, 'tp', up)
-        own, other = p2(u, none, row(norm_w[1]), gz, go, gs, y, c, ac, s, e3, (), *common, True, 1, False, None, 4)
+        own, other = p2(u, none, nw, gz, go, gs, y, c, ac, s, e3, (), *common, True, 1, False, None, 4)
         return finish(own, other)[None]
 
     return jax.shard_map(device_forward, mesh=mesh, in_specs=in_specs, out_specs=P('dp'), check_vma=False)

time: 481 us -> 457 us (0.950)
  Pallas kernels: 442 us -> 422 us
    pallas_call x2, Pallas kernels: 145 us -> 134 us  [p2(): pl.pallas_call(functools.partial(p2_body, geom=(n_dp, n_tp, heads), mix_i...]
    pallas_call x2, Pallas kernels: 281 us -> 275 us  [p1(): pl.pallas_call(functools.partial(p1_body, geom=(n_dp, n_tp, heads, nb, nb...]
where the time goes in v7:
time: 457 us; the launch traced here: 455 us
  Pallas kernels  422 us (92%)
  other arithmetic  11.7 us (3%)
  local copies, waits for them, and re-layouts  8.98 us (2%)
  starting transfers between devices  7.33 us (2%)
  waiting for transfers between devices  4.93 us (1%)
    pallas_call x2, Pallas kernels, p1(): pl.pallas_call(functools.partial(p1_body, geom=(n_dp, n_tp, heads, nb, nb...  275 us
    pallas_call x2, Pallas kernels, p2(): pl.pallas_call(functools.partial(p2_body, geom=(n_dp, n_tp, heads), mix_i...  134 us
    pallas_call x1, Pallas kernels, finish(): pl.pallas_call(finish_body, name='finish', grid=(2, ni), in_specs=[pl.Blo...  12.8 us
  transfers between devices with their start and end apart: 3, of which 3 were waited for; matrix products, arithmetic and copies ran while one was open for 0% of the time, Pallas kernels for 0%

profile of v7, /device:TPU:0, one launch (start us, length us, event | category | flops | bytes accessed | tf_op | source)
XLA Modules:
  0.0 454.7 jit_solution(11930788530269055755)
XLA Ops:
  0.0 0.0 copy-start
  0.0 0.0 copy-start.1
  0.0 0.7 negate_multiply_fusion
  0.7 1.3 copy.24.refs_5_
  2.0 0.7 bitcast_convert_fusion.1
  2.7 0.7 bitcast_convert_fusion
  3.4 0.7 broadcast_in_dim.15
  4.1 0.1 reshape.49
  4.2 1.3 copy.25.refs_2_.refs_1_
  5.5 0.7 convert_bitcast_fusion
  6.2 0.9 slice_bitcast_fusion
  7.1 0.1 copy.30
  7.2 2.7 convert_element_type.21.refs_7_.refs_10_
  9.9 2.7 convert_element_type.23.refs_9_.refs_10_
  12.6 2.8 convert_element_type.24.refs_10_.refs_11_
  15.5 0.6 select_bitcast_fusion.refs_1_
  16.1 0.1 broadcast_in_dim.32
  16.2 0.0 copy-done.1
  16.2 0.1 broadcast_in_dim.31
  16.2 0.0 copy-done
  16.2 1.8 concatenate.3
  18.1 150.3 %p1.2 = (f32[3072,2048]{1,0:T(8,128)}, f32[3072,128]{1,0:T(8,128)}, f32[32,3072]{1,0:T(8,128)}, f32[128,2048]{1,0:T(8,128)}, f32[4,8,256,256]{3,2,1,0:T(8,128)},...) custom-call(bf16[6144,1024]{1,0:T(8,128)(2,1)} %bitcast.23, ...), custom_call_target="tpu_custom_call" | custom-call | flops 215040000000 | bytes 36864000 | tf_op jit(solution)/shard_map/p1/pallas_call | solution.py:528
  168.4 4.2 collective-permute-start
  172.7 2.0 collective-permute-done.refs_8_
  174.7 0.0 copy-start.3
  174.7 1.0 copy-done.3
  175.7 72.1 %p2.2 = (bf16[3072,1024]{1,0:T(8,128)(2,1)}, f32[24,1024]{1,0:T(8,128)}, f32[4,8,256,256]{3,2,1,0:T(8,128)}) custom-call(bf16[6144,1024]{1,0:T(8,128)(2,1)} %bitcast.24, bf16[2,1,1024]{2,1,0:T(2,128)(2,1)} %copy.25.refs_2_.refs_1_, f32[4,8,256,256]{3,2,1,0:T(8,128)} %get-tuple-element.23.refs_2_, f32[4,8,256,256]{3,2,1,0:T(8,128)} %get-tuple-element.24.refs_3_, ...), custom_call_target="tpu_custom_call" | custom-call | flops 92160000000 | bytes 36864000 | tf_op jit(solution)/shard_map/p2/pallas_call | solution.py:656
  247.7 1.5 collective-permute-start.1
  249.3 0.9 collective-permute-done.1.refs_1_
  250.2 0.0 copy-start.4
  250.2 0.6 copy-done.4
  250.8 124.7 %p1.3 = (f32[3072,2048]{1,0:T(8,128)}, f32[3072,128]{1,0:T(8,128)}, f32[32,3072]{1,0:T(8,128)}, f32[128,2048]{1,0:T(8,128)}, f32[4,8,256,256]{3,2,1,0:T(8,128)}, /*index=5*/f32[4,8,256,256]{3,2,1,0:T(8,128)}) custom-call(bf16[3072,1024]{1,0:T(8,128)(2,1)} %get-tuple-element.30.refs_0_, f32[24,1024]{1,0:T(8,128)} %copy-done.4, ...), custom_call_target="tpu_custom_call" | custom-call | flops 215040000000 | bytes 36864000 | tf_op jit(solution)/shard_map/p1/pallas_call | solution.py:528
  375.6 1.6 collective-permute-start.2
  377.2 2.0 collective-permute-done.2.refs_8_
  379.1 0.0 copy-start.2
  379.2 1.0 copy-done.2
  380.1 61.7 %p2.3 = (bf16[3072,1024]{1,0:T(8,128)(2,1)}, f32[3072,1024]{1,0:T(8,128)}) custom-call(bf16[3072,1024]{1,0:T(8,128)(2,1)} %get-tuple-element.30.refs_0_, bf16[2,1,1024]{2,1,0:T(2,128)(2,1)} %copy.25.refs_2_.refs_1_, f32[4,8,256,256]{3,2,1,0:T(8,128)} %get-tuple-element.33.refs_2_, f32[4,8,256,256]{3,2,1,0:T(8,128)} %get-tuple-element.34.refs_3_, ...), custom_call_target="tpu_custom_call" | custom-call | flops 92160000000 | bytes 36864000 | tf_op jit(solution)/shard_map/p2/pallas_call | solution.py:656
  441.9 12.8 %finish.1 = bf16[6144,1024]{1,0:T(8,128)(2,1)} custom-call(bf16[3072,1024]{1,0:T(8,128)(2,1)} %get-tuple-element.39.own_ref, f32[3072,1024]{1,0:T(8,128)} %get-tuple-element.40.other_ref), custom_call_target="tpu_custom_call" | custom-call | flops 3145728 | bytes 25165824 | tf_op jit(solution)/shard_map/finish/pallas_call | solution.py:692
  (4 shorter events, 0.0 us)
Async XLA Ops:
  0.0 16.2 %copy-start = (bf16[2,4,256]{2,1,0:T(4,128)(2,1)S(1)}, bf16[2,4,256]{2,1,0:T(4,128)(2,1)}, u32[]{:S(2)}) copy-start(bf16[2,4,256]{2,1,0:T(4,128)(2,1)} %param.22) | copy-start | bytes 12292
  0.0 16.2 %copy-start.1 = (f32[2,4]{1,0:T(2,128)S(1)}, f32[2,4]{1,0:T(2,128)}, u32[]{:S(2)}) copy-start(f32[2,4]{1,0:T(2,128)} %param.26) | copy-start | bytes 100
  168.4 6.3 %collective-permute-start = (f32[128,2048]{1,0:T(8,128)}, f32[128,2048]{1,0:T(8,128)S(1)}, u32[]{:S(2)}, u32[]{:S(2)}) collective-permute-start(f32[128,2048]{1,0:T(8,128)} %get-tuple-element.29), channel_id=1, source_target_pairs={{0,1},{2,3},{4,5},{6,7},{8,9},{10,11},{12,13},{14,15},{16,17},{18,... | collective-permute-start | bytes 3145736 | tf_op jit(solution)/shard_map/ppermute | solution.py:746
  174.7 1.0 copy-start.3
  247.7 2.5 collective-permute-start.1
  250.2 0.6 copy-start.4
  375.6 3.6 collective-permute-start.2
  379.1 1.0 copy-start.2

commit v8 on v7

--- a/solution.py
+++ b/solution.py
@@ -23,6 +23,8 @@
 NST = 128
 CAR = 24
 SMALL = 32
+ORDER = (1, 3, 2)
+EARLY = 6
 SEMS = 26
 VMEM_CAP = 60 << 20
 
@@ -161,13 +163,13 @@
         return self.rdma(22 + dz, ref, ref, self.partner)
 
     def peers(self):
-        return ([(self.dp, 2 * ((self.z + dz) % 4) + self.c) for dz in (1, 2, 3)]
+        return ([(self.dp, 2 * ((self.z + dz) % 4) + self.c) for dz in ORDER]
                 + [(p, self.tp) for p in self.side] + [self.partner])
 
     def start(self):
         for q in range(self.quarters):
             self.own(q).start()
-        for dz in (1, 3, 2):
+        for dz in ORDER:
             self.line(dz).start()
         if self.keep:
             for q in range(self.quarters):
@@ -200,7 +202,7 @@
     def drain(self):
         for q in range(self.quarters):
             self.own(q).wait_send()
-        for dz in (1, 2, 3):
+        for dz in ORDER:
             self.line(dz).wait_send()
             self.over(dz).wait_send()
             for n in range(2):
@@ -211,12 +213,12 @@
         s = bytes.fromhex(s)
         acts = [(s[0], self.start)]
         for k, f in enumerate((self.spread, self.pass_on, self.hand)):
-            acts += [(s[1 + 3 * k + j], functools.partial(f, dz)) for j, dz in enumerate((1, 3, 2))]
+            acts += [(s[1 + 3 * k + j], functools.partial(f, dz)) for j, dz in enumerate(ORDER)]
         return acts
 
     def finish(self):
         self.settle_own()
-        for dz in (1, 2, 3):
+        for dz in ORDER:
             self.settle(dz)
         self.drain()
 
@@ -275,19 +277,28 @@
 def p1_body(*refs, geom, mixed, layer, fetch_x, plans):
     n_dp, n_tp, heads, nb, nbs, sp = geom
     (u_ref, halo_ref, nw_ref, wbc_ref, cbc_ref, bbc_ref, e3_ref), refs = refs[:7], refs[7:]
-    nw, cbc, bbc = nw_ref[...].astype(F32), cbc_ref[...].astype(F32), bbc_ref[...].astype(F32)
+    row = slice(layer, layer + 1)
+    nw, cbc, bbc = nw_ref[row].astype(F32), cbc_ref[...].astype(F32), bbc_ref[row].astype(F32)
     if fetch_x:
-        (ax, asm, az, ao), (y_ref, c_ref, ac_ref, send_ref), (gx, gs, gz, go), refs = refs[:4], refs[4:8], refs[8:12], refs[12:]
+        (ax, asm, az, ao), (y_ref, c_ref, ac_ref, s_in), (gx, gs, gz, go), refs = refs[:4], refs[4:8], refs[8:12], refs[12:]
     else:
-        (ax, gx, gs, az, ao), (y_ref, c_ref, ac_ref, send_ref), (gz, go), refs = refs[:5], refs[5:9], refs[9:11], refs[11:]
+        (ax, gx, gs, az, ao), (y_ref, c_ref, ac_ref, s_in), (gz, go), refs = refs[:5], refs[5:9], refs[9:11], refs[11:]
     (wf, wb, wsem, sm, wdt, cst, st, hcar, xcar, qcar, aoff, ubuf, h_s, la1_s, la2_s, lb1_s, lb2_s, cc_s, cbd_s, row_s, aw_s,
-     send, recv), sems = refs[:23], refs[23:]
+     sbuf, hsem, send, recv), sems = refs[:25], refs[25:]
     p, i = pl.program_id(0), pl.program_id(1)
     np_, ni = pl.num_programs(0), pl.num_programs(1)
     step = p * ni + i
     d_model = u_ref.shape[-1]
     by_z = sp < n_tp
-    zs = source(p + p // 2 * (1 - 2 * (p % 2))) if by_z else 0
+    zs_of = (lambda p: source(p + p // 2 * (1 - 2 * (p % 2)))) if by_z else (lambda p: 0)
+    zs = zs_of(p)
+    upper = here()[3] == 1
+
+    def state_out(p):
+        dp, tp, _, c = here()
+        cols = pl.ds(pl.multiple_of(2 * zs_of(p) * PC, PC), sp * PC)
+        return pltpu.make_async_remote_copy(src_ref=sbuf, dst_ref=s_in.at[:, cols], send_sem=hsem.at[0], recv_sem=hsem.at[1],
+                                            device_id=(dp, tp + 1 - 2 * c), device_id_type=MESH)
 
     zg = Gather(piece_rows(az, layer), gz, send, recv, 0)
     og = Gather(piece_cols(ao, layer), go, send, recv, SEMS)
@@ -349,12 +360,11 @@
     ri = lax.broadcasted_iota(jnp.int32, (BLK, BLK), 0)
     ci = lax.broadcasted_iota(jnp.int32, (BLK, BLK), 1)
 
-    def prologue(b, h):
-        j = i * nbs + b
-        blk = pl.ds(pl.multiple_of(j * BLK, BLK), BLK)
-        h_s[blk, :] = h
+    def prologue(h, b, hook):
+        q0 = dot(h, wbc_ref[...])
         rT = round_bf16(dott(wdt[...], h))
-        bc, qcar[...] = conv(round_bf16(dot(h, wbc_ref[...])), qcar[...],
+        hook(h, 2)
+        bc, qcar[...] = conv(round_bf16(q0), qcar[...],
                              [cbc[k:k + 1] for k in range(4)], bbc)
         bmat, cmat = bc[:, :NST], bc[:, NST:]
         here_rows = slice(b * BLK, (b + 1) * BLK)
@@ -368,7 +378,7 @@
         low = ci[:heads] < SUB
         wT = dtT * jnp.exp2(jnp.where(low, mid, alast) - acT)
         pad = jnp.zeros((BLK - 3 * heads, BLK), BF16)
-        aw_s[blk, :] = lanes_cat(rows_cat(*split3(acT), pad).T, rows_cat(*split3(wT), pad).T)
+        a3, w3 = rows_cat(*split3(acT), pad).T, rows_cat(*split3(wT), pad).T
         ac_ref[:, here_rows] = acT + aoff[:, :1]
         aoff[...] = aoff[...] + alast
 
@@ -377,28 +387,56 @@
             l = low[:heads // 2]
             return jnp.where(l, ev, pltpu.roll(od, SUB, 1)), jnp.where(l, pltpu.roll(ev, SUB, 1), od)
 
-        for half, (a, d) in enumerate(zip(pair_rows(acT), pair_rows(dtT))):
-            row_s[2 * j + half] = rows_cat(*[v[4 * z:4 * z + 4] for z in range(heads // 8) for v in (a, d)])
+        rows = [rows_cat(*[w for zz in zip(*[jnp.split(v, n_tp // 2) for v in ad]) for w in zz])
+                for ad in zip(pair_rows(acT), pair_rows(dtT))]
+        hook(h, 4)
         cb = dott(cmat, bmat, HI)
+        hook(h, EARLY)
         lowr, tri = ci[:SUB] < SUB, time_of(ri[:SUB]) >= time_of(ci[:SUB] % SUB)
         ca, cd = cb[:SUB], cb[SUB:]
-        cbd_s[blk, :] = rows_cat(jnp.where(tri, jnp.where(lowr, ca, pltpu.roll(ca, SUB, 1)), 0.0),
-                                 jnp.where(tri, jnp.where(lowr, pltpu.roll(cd, SUB, 1), cd), 0.0))
+        cbd = [jnp.where(tri, jnp.where(lowr, ca, pltpu.roll(ca, SUB, 1)), 0.0),
+               jnp.where(tri, jnp.where(lowr, pltpu.roll(cd, SUB, 1), cd), 0.0)]
         bT = bmat.T
-        big = pl.ds(pl.multiple_of(j * (NST + SUB), SUB), NST + SUB)
-        la1_s[big, :], la2_s[big, :] = kcat6(split3(rows_cat(bT[:, :SUB], cd[:, :SUB])))
-        lb1_s[blk, :], lb2_s[blk, :] = kcat6(split3(pltpu.roll(bT, SUB, 1)[:, :SUB]))
+        la = kcat6(split3(rows_cat(bT[:, :SUB], cd[:, :SUB])))
+        lb = kcat6(split3(pltpu.roll(bT, SUB, 1)[:, :SUB]))
         c1, c2, c3 = split3(cmat)
-        cc_s[blk, :] = lanes_cat(c1, c2, c1, c3)
-
-    def all_prologues():
+        return h, a3, w3, rows, cbd, la, lb, (lanes_cat(c1, c2), lanes_cat(c1, c3))
+
+    def spots(b):
+        j = i * nbs + b
+        at = lambda r: pl.ds(pl.multiple_of(j * r, SUB), r)
+        return j, at(BLK), at(NST + SUB)
+
+    def keep(b, vals):
+        h, a3, w3, rows, cbd, la, lb, cc = vals
+        j, blk, big = spots(b)
+        h_s[blk, :] = h
+        aw_s[blk, :] = lanes_cat(a3, w3)
+        for half in range(2):
+            row_s[2 * j + half] = rows[half]
+        cbd_s[blk, :] = rows_cat(*cbd)
+        la1_s[big, :], la2_s[big, :] = la
+        lb1_s[blk, :], lb2_s[blk, :] = lb
+        cc_s[blk, :] = lanes_cat(*cc)
+
+    def kept(b):
+        j, blk, big = spots(b)
+        eight = pl.ds(pl.multiple_of(8 * zs, 8), 8)
+        return (None, aw_s[blk, :BLK], aw_s[blk, BLK:], [row_s[2 * j + half, eight, :] for half in range(2)],
+                [cbd_s[pl.ds(pl.multiple_of(j * BLK + half * SUB, SUB), SUB), :] for half in range(2)],
+                (la1_s[big, :], la2_s[big, :]), (lb1_s[blk, :], lb2_s[blk, :]), (cc_s[blk, :2 * NST], cc_s[blk, 2 * NST:]))
+
+
+    def all_prologues(hook):
         u = u_ref[...].astype(F32)
         h = rms(u if mixed else unmix(u, ubuf), nw)
-        for b in range(nbs):
-            prologue(b, h[b * BLK:(b + 1) * BLK])
+        return [prologue(h[b * BLK:(b + 1) * BLK], b, hook) for b in range(nbs)]
 
     if by_z:
-        pl.when(p == 0)(all_prologues)
+        @pl.when(p == 0)
+        def _():
+            for b, v in enumerate(all_prologues(lambda h, k: None)):
+                keep(b, v)
 
     @pl.when(i == 0)
     def _():
@@ -415,6 +453,9 @@
         for q in range(n_dp):
             for k in range(sp):
                 wb[q * PC:(q + 1) * PC, k * PC:(k + 1) * PC] = wf[slot, q, k].astype(BF16)
+        @pl.when((p > 0) & jnp.logical_not(upper))
+        def _():
+            state_out(p - 1).start()
         xcar[...] = roll8(round_bf16(dot(hcar[...], wb[...])))
         st[...] = jnp.zeros_like(st)
 
@@ -423,45 +464,51 @@
         nd = p + 1
         nd = nd + nd // 2 * (1 - 2 * (nd % 2))
         if fetch_x:
-            for d in (1, 2, 3):
+            for d in ORDER:
                 pl.when(nd == d)(functools.partial(xg.settle, d))
         load_w((p + 1) % 2, source(nd)).start()
 
-    if not by_z:
-        all_prologues()
     lane = lax.broadcasted_iota(jnp.int32, (SUB, LANES), 1)
     lo = jnp.where(lane < HD, 1.0, 0.0).astype(BF16)
     hi = jnp.where(lane < HD, 0.0, 1.0).astype(BF16)
-    x0 = [dot(h_s[pl.ds(pl.multiple_of(i * nbs * BLK, BLK), nbs * BLK), :], wb[:, k * PC:(k + 1) * PC]) for k in range(sp)]
-
-    def place(b):
-        j = i * nbs + b
-        return j, pl.ds(pl.multiple_of(j * BLK, BLK), BLK), pl.ds(pl.multiple_of(j * (NST + SUB), SUB), NST + SUB)
+    x0 = {}
+
+    def proj(hs, upto):
+        for k in range(len(x0), min(sp, upto)):
+            x0[k] = dot(hs, wb[:, k * PC:(k + 1) * PC])
+
+    if by_z:
+        vals = [kept(b) for b in range(nbs)]
+        hs = h_s[pl.ds(pl.multiple_of(i * nbs * BLK, BLK), nbs * BLK), :]
+        proj(hs, sp)
+    else:
+        vals = all_prologues(proj)
+        hs = vals[0][0]
 
     def lanes_of(k):
         return slice(k * PC, (k + 1) * PC), pl.ds(pl.multiple_of((2 * zs + k) * PC, PC), PC)
 
     def pre(b, k):
-        (_, blk, _), (sl, gl) = place(b), lanes_of(k)
+        (sl, gl), (_, a3, w3, _, _, _, _, (c12, c13)) = lanes_of(k), vals[b]
         s1, s2, s3 = split3(st[:, sl])
-        c12, c13 = cc_s[blk, :2 * NST], cc_s[blk, 2 * NST:]
         inter = dot(c12, rows_cat(s1, s1)) + dot(c12, rows_cat(s2, s2)) + dot(c13, rows_cat(s3, s1))
         n3 = e3_ref.shape[0]
-        acx = dot(aw_s[blk, :n3], e3_ref[:, gl])
-        wx = dot(aw_s[blk, BLK:BLK + n3], e3_ref[:, gl])
+        acx = dot(a3[:, :n3], e3_ref[:, gl])
+        wx = dot(w3[:, :n3], e3_ref[:, gl])
+        proj(hs, k + EARLY + 1)
         return x0[k][b * BLK:(b + 1) * BLK], acx, wx, inter
 
     def mid_(b, k, x0, acx, wx, inter):
-        (j, blk, _), (sl, _) = place(b), lanes_of(k)
+        (sl, _), (_, _, _, rws, cbds, _, _, _) = lanes_of(k), vals[b]
         t = 2 * zs + k
+        base = 0 if by_z else k // 2 * 8
         x, xcar[:, sl] = conv(round_bf16(x0), xcar[:, sl], [sm[t, r:r + 1, :] for r in range(4)], sm[t, 4:5, :])
         xw = split3(x * wx)
         r = kcat6r([v[:SUB] for v in xw]) + kcat6r([v[SUB:] for v in xw])
         ms, xs = [], []
         for half in range(2):
             rows = slice(half * SUB, (half + 1) * SUB)
-            row = row_s[2 * j + half, pl.ds(pl.multiple_of(8 * (zs + k // 2), 8), 8), :]
-            cbd = cbd_s[pl.ds(pl.multiple_of(j * BLK + half * SUB, SUB), SUB), :]
+            row, cbd = rws[half][base:base + 8], cbds[half]
             m = []
             for g in range(2):
                 seg = acx[rows, g * LANES:(g + 1) * LANES] - row[2 * (k % 2) + g:2 * (k % 2) + g + 1]
@@ -471,9 +518,9 @@
         return x, acx, inter, r, ms, xs
 
     def fin(b, k, x, acx, inter, r, ms, xs):
-        (j, blk, big), (sl, _) = place(b), lanes_of(k)
-        ra = dot(la1_s[big, :], r[0]) + dot(la2_s[big, :], r[1])
-        rb = dot(lb1_s[blk, :], r[2]) + dot(lb2_s[blk, :], r[3])
+        (sl, _), (_, _, _, _, _, la, lb, _) = lanes_of(k), vals[b]
+        ra = dot(la[0], r[0]) + dot(la[1], r[1])
+        rb = dot(lb[0], r[2]) + dot(lb[1], r[3])
         am, al = acx[SUB - 1:SUB], acx[BLK - 1:BLK]
         st[:, sl] = st[:, sl] * jnp.exp2(al) + ra[:NST] * jnp.exp2(al - am) + rb
         skip = sm[2 * zs + k, 6:7, :]
@@ -499,7 +546,10 @@
 
     @pl.when(i == ni - 1)
     def _():
-        send_ref[...] = st[...]
+        @pl.when((p > 0) & jnp.logical_not(upper))
+        def _():
+            state_out(p - 1).wait_send()
+        sbuf[...] = st[...]
 
     @pl.when(step == np_ * ni - 1)
     def _():
@@ -507,6 +557,15 @@
         og.finish()
         if fetch_x:
             xg.drain()
+
+        @pl.when(jnp.logical_not(upper))
+        def _():
+            state_out(p).start()
+            state_out(p).wait_send()
+
+        @pl.when(upper)
+        def _():
+            pltpu.make_async_copy(s_in, s_in, hsem.at[1]).wait()
 
 
 def p1(u, base, halo, nw, wbc, cbc, bbc, e3, comm, n, n_dp, n_tp, mixed, layer, fetch_x, plans, cid):
@@ -529,12 +588,12 @@
         functools.partial(p1_body, geom=(n_dp, n_tp, heads, nb, nbs, sp), mixed=mixed, layer=layer, fetch_x=fetch_x, plans=plans),
         name="p1", grid=(n_tp // sp, ni),
         in_specs=[pl.BlockSpec((rows, d_model), lambda p, i: (base() + once(p, i), 0)),
-                  fixed((CAR, d_model)), own_layer(1, d_model), own_layer(d_model, PC), own_layer(4, PC), own_layer(1, PC),
+                  fixed((CAR, d_model)), fixed((2, d_model)), own_layer(d_model, PC), own_layer(4, PC), fixed((2, PC)),
                   fixed((3 * heads, width))] + [hbm] * len(comm),
         out_specs=[pl.BlockSpec((rows, sp * PC), lambda p, i: (i, col(p))),
                    pl.BlockSpec((rows, NST), lambda p, i: (once(p, i), 0)),
                    pl.BlockSpec((heads, rows), lambda p, i: (0, once(p, i))),
-                   pl.BlockSpec((NST, sp * PC), lambda p, i: (0, col(p)))] + [hbm] * len(more),
+                   hbm] + [hbm] * len(more),
         out_shape=outs + more,
         scratch_shapes=[
             vm((2 if fetch_x else 1, n_dp, sp, PC, PC), F32), vm((d_model, sp * PC), BF16), pltpu.SemaphoreType.DMA((3,)),
@@ -543,7 +602,7 @@
             vm((d_model // LANES * rows, LANES), F32), vm((n, d_model), BF16),
             vm((nb * (NST + SUB), 4 * SUB), BF16), vm((nb * (NST + SUB), 2 * SUB), BF16),
             vm((n, 4 * SUB), BF16), vm((n, 2 * SUB), BF16), vm((n, 4 * NST), BF16), vm((n, LANES), F32),
-            vm((2 * nb, 2 * heads // 2, LANES), F32), vm((n, 2 * BLK), BF16)]
+            vm((2 * nb, 2 * heads // 2, LANES), F32), vm((n, 2 * BLK), BF16), vm((NST, sp * PC), F32), pltpu.SemaphoreType.DMA((2,))]
         + dma(3 * SEMS) + (dma(8) if fetch_x else []),
         compiler_params=pltpu.CompilerParams(dimension_semantics=("arbitrary", "arbitrary"), vmem_limit_bytes=VMEM_CAP,
                                              collective_id=cid, has_side_effects=True),
@@ -596,13 +655,13 @@
                 a, b = slice(d * PC, (d + 1) * PC), slice(t * PC, (t + 1) * PC)
                 wzb[a, b] = wz_ref[d, t].astype(BF16)
                 wob[b, a] = wo_ref[d, t].astype(BF16)
-        a, b, c_ = split3(s_ref[...])
+        a, b, c_ = split3(jnp.where(here()[3] == 1, s_ref[...], 0.0))
         for k, (v, w) in enumerate(((a, a), (b, b), (c_, a))):
             s3[k] = rows_cat(v, w)
 
     u = u_ref[...].astype(F32)
     u = u if mix_in else unmix(u, ubuf)
-    h = rms(u, nw_ref[...].astype(F32))
+    h = rms(u, nw_ref[layer:layer + 1].astype(F32))
     c1, c2, c3 = split3(c_ref[...])
     c12, c13 = lanes_cat(c1, c2), lanes_cat(c1, c3)
     eT = rows_cat(*split3(jnp.exp2(ac_ref[...]))).T
@@ -657,7 +716,7 @@
         functools.partial(p2_body, geom=(n_dp, n_tp, heads), mix_in=mix_in, layer=layer, fetch_x=fetch_x, plans=plans),
         name="p2", grid=(n // BLK2,),
         in_specs=[pl.BlockSpec((BLK2, d_model), lambda i: (base() + i, 0)),
-                  pl.BlockSpec((None, 1, d_model), lambda i: (layer, 0, 0)),
+                  fixed((2, d_model)),
                   fixed((n_dp, n_tp, PC, PC)), fixed((n_dp, n_tp, PC, PC)),
                   pl.BlockSpec((n_tp, SMALL, PC), lambda i: (0, layer, 0), pipeline_mode=pl.Buffered(1)),
                   rows(width), rows(NST), pl.BlockSpec((heads, BLK2), lambda i: (0, i)),
@@ -736,19 +795,15 @@
         halo = jnp.where(core == 1, tail, 0.0)
         half = lambda blk: (lambda: lax.axis_index('tp') % 2 * (n // blk))
         none = lambda: 0
-        row = lambda v: v.reshape(v.shape[0], 1, v.shape[1])
         common = (n, n_dp, n_tp)
-        nw = row(norm_w)
-        bc = (nw, w_bc, conv_bc, row(bias_bc), e3)
+        bc = (norm_w, w_bc, conv_bc, bias_bc, e3)
 
         y, c, ac, s, gx, gs, gz, go = p1(u, half(BLK * NBS), halo, *bc, (ax, small, az, ao), *common, False, 0, True,
                                          (PLAN_Z0, PLAN_O0, PLAN_X), 1)
-        s = lax.ppermute(s, 'tp', up)
-        u, f, gx = p2(u, half(BLK2), nw, gz, go, gs, y, c, ac, s, e3, (ax,), *common, False, 0, True, PLAN_X1, 2)
+        u, f, gx = p2(u, half(BLK2), norm_w, gz, go, gs, y, c, ac, s, e3, (ax,), *common, False, 0, True, PLAN_X1, 2)
         halo = lax.ppermute(f, 'tp', up)
         y, c, ac, s, gz, go = p1(u, none, halo, *bc, (ax, gx, gs, az, ao), *common, True, 1, False, (PLAN_Z1, PLAN_O1), 3)
-        s = lax.ppermute(s, 'tp', up)
-        own, other = p2(u, none, nw, gz, go, gs, y, c, ac, s, e3, (), *common, True, 1, False, None, 4)
+        own, other = p2(u, none, norm_w, gz, go, gs, y, c, ac, s, e3, (), *common, True, 1, False, None, 4)
         return finish(own, other)[None]
 
     return jax.shard_map(device_forward, mesh=mesh, in_specs=in_specs, out_specs=P('dp'), check_vma=False)

time: 457 us -> 440 us (0.963)
  starting transfers between devices: 7.33 us -> 1.54 us
    ppermute x2 -> x0, starting transfers between devices: 5.8 us -> none  [device_forward(): s = lax.ppermute(s, 'tp', up)]
    pallas_call x2, Pallas kernels: 275 us -> 270 us  [p1(): pl.pallas_call(functools.partial(p1_body, geom=(n_dp, n_tp, heads, nb, nb...]
  transfers between devices with their start and end apart: 3 -> 1, of which waited for: 3 -> 1; matrix products, arithmetic and copies ran while one was open for 0% -> 0% of each run, Pallas kernels for 0% -> 0%
where the time goes in v8:
time: 440 us; the launch traced here: 438 us
  Pallas kernels  419 us (95%)
  other arithmetic  11.7 us (3%)
  local copies, waits for them, and re-layouts  4.49 us (1%)
    pallas_call x2, Pallas kernels, p1(): pl.pallas_call(functools.partial(p1_body, geom=(n_dp, n_tp, heads, nb, nb...  270 us
    pallas_call x2, Pallas kernels, p2(): pl.pallas_call(functools.partial(p2_body, geom=(n_dp, n_tp, heads), mix_i...  136 us
    pallas_call x1, Pallas kernels, finish(): pl.pallas_call(finish_body, name='finish', grid=(2, ni), in_specs=[pl.Blo...  12.8 us
  transfers between devices with their start and end apart: 1, of which 1 were waited for; matrix products, arithmetic and copies ran while one was open for 0% of the time, Pallas kernels for 0%

profile of v8, /device:TPU:0, one launch (start us, length us, event | category | flops | bytes accessed | tf_op | source)
XLA Modules:
  0.0 437.6 jit_solution(6322373452092966340)
XLA Ops:
  0.0 0.0 copy-start
  0.0 0.0 copy-start.1
  0.0 0.7 negate_multiply_fusion
  0.7 0.7 bitcast_convert_fusion.1
  1.4 0.7 bitcast_convert_fusion
  2.1 0.7 broadcast_in_dim.15
  2.8 0.1 reshape.41
  2.9 0.7 convert_bitcast_fusion
  3.7 0.9 slice_bitcast_fusion
  4.6 0.1 copy.21
  4.7 2.7 convert_element_type.21.refs_7_.refs_10_
  7.4 2.7 convert_element_type.23.refs_9_.refs_10_
  10.1 2.8 convert_element_type.24.refs_10_.refs_11_
  12.9 0.6 select_bitcast_fusion.refs_1_
  13.5 0.1 broadcast_in_dim.32
  13.6 0.0 copy-done.1
  13.6 0.1 broadcast_in_dim.31
  13.7 0.0 copy-done
  13.7 1.9 concatenate.3
  15.5 150.7 %p1.2 = (f32[3072,2048]{1,0:T(8,128)}, f32[3072,128]{1,0:T(8,128)}, f32[32,3072]{1,0:T(8,128)}, f32[128,2048]{1,0:T(8,128)}, f32[4,8,256,256]{3,2,1,0:T(8,128)},...) custom-call(bf16[6144,1024]{1,0:T(8,128)(2,1)} %bitcast.20, ...), custom_call_target="tpu_custom_call" | custom-call | flops 215040000000 | bytes 36864000 | tf_op jit(solution)/shard_map/p1/pallas_call | solution.py:587
  166.2 74.3 %p2.2 = (bf16[3072,1024]{1,0:T(8,128)(2,1)}, f32[24,1024]{1,0:T(8,128)}, f32[4,8,256,256]{3,2,1,0:T(8,128)}) custom-call(bf16[6144,1024]{1,0:T(8,128)(2,1)} %bitcast.21, bf16[2,1024]{1,0:T(2,128)(2,1)} %refs_1_.3, f32[4,8,256,256]{3,2,1,0:T(8,128)} %get-tuple-element.23.refs_2_, f32[4,8,256,256]{3,2,1,0:T(8,128)} %get-tuple-element.24.refs_3_, ...), custom_call_target="tpu_custom_call" | custom-call | flops 92160000000 | bytes 36864000 | tf_op jit(solution)/shard_map/p2/pallas_call | solution.py:715
  240.5 1.5 collective-permute-start
  242.0 0.9 collective-permute-done.refs_1_
  243.0 0.0 copy-start.2
  243.0 0.6 copy-done.2
  243.6 119.3 %p1.3 = (f32[3072,2048]{1,0:T(8,128)}, f32[3072,128]{1,0:T(8,128)}, f32[32,3072]{1,0:T(8,128)}, f32[128,2048]{1,0:T(8,128)}, f32[4,8,256,256]{3,2,1,0:T(8,128)}, /*index=5*/f32[4,8,256,256]{3,2,1,0:T(8,128)}) custom-call(bf16[3072,1024]{1,0:T(8,128)(2,1)} %get-tuple-element.30.refs_0_, f32[24,1024]{1,0:T(8,128)} %copy-done.2, bf16[2,1024]{1,0:T(2,128)(2,1)} %refs_1_.3, ...), custom_call_target="tpu_custom_call" | custom-call | flops 215040000000 | bytes 36864000 | tf_op jit(solution)/shard_map/p1/pallas_call | solution.py:587
  362.9 61.8 %p2.3 = (bf16[3072,1024]{1,0:T(8,128)(2,1)}, f32[3072,1024]{1,0:T(8,128)}) custom-call(bf16[3072,1024]{1,0:T(8,128)(2,1)} %get-tuple-element.30.refs_0_, bf16[2,1024]{1,0:T(2,128)(2,1)} %refs_1_.3, f32[4,8,256,256]{3,2,1,0:T(8,128)} %get-tuple-element.33.refs_2_, f32[4,8,256,256]{3,2,1,0:T(8,128)} %get-tuple-element.34.refs_3_, ...), custom_call_target="tpu_custom_call" | custom-call | flops 92160000000 | bytes 36864000 | tf_op jit(solution)/shard_map/p2/pallas_call | solution.py:715
  424.8 12.8 %finish.1 = bf16[6144,1024]{1,0:T(8,128)(2,1)} custom-call(bf16[3072,1024]{1,0:T(8,128)(2,1)} %get-tuple-element.39.own_ref, f32[3072,1024]{1,0:T(8,128)} %get-tuple-element.40.other_ref), custom_call_target="tpu_custom_call" | custom-call | flops 3145728 | bytes 25165824 | tf_op jit(solution)/shard_map/finish/pallas_call | solution.py:751
  (4 shorter events, 0.0 us)
Async XLA Ops:
  0.0 13.7 %copy-start = (bf16[2,4,256]{2,1,0:T(4,128)(2,1)S(1)}, bf16[2,4,256]{2,1,0:T(4,128)(2,1)}, u32[]{:S(2)}) copy-start(bf16[2,4,256]{2,1,0:T(4,128)(2,1)} %param.22) | copy-start | bytes 12292
  0.0 13.6 %copy-start.1 = (f32[2,4]{1,0:T(2,128)S(1)}, f32[2,4]{1,0:T(2,128)}, u32[]{:S(2)}) copy-start(f32[2,4]{1,0:T(2,128)} %param.26) | copy-start | bytes 100
  240.5 2.5 collective-permute-start
  243.0 0.6 copy-start.2

commit v9 on v8

--- a/solution.py
+++ b/solution.py
@@ -101,6 +101,13 @@
     return jnp.asarray(np.tile(one, (3, 1)), BF16)
 
 
+def per_channel(v, t, heads):
+    n, per = v.shape[0], PC // HD
+    low = lax.broadcasted_iota(jnp.int32, (n, LANES), 1) < HD
+    wide = [jnp.broadcast_to(v[:, r:r + 1], (n, LANES)) for r in [head_row(h, heads) for h in range(per * t, per * (t + 1))]]
+    return lanes_cat(*[jnp.where(low, a, b) for a, b in zip(wide[::2], wide[1::2])])
+
+
 def kcat6(parts):
     a, b, c = parts
     return lanes_cat(a, b, c, a), lanes_cat(b, a)
@@ -280,7 +287,7 @@
     row = slice(layer, layer + 1)
     nw, cbc, bbc = nw_ref[row].astype(F32), cbc_ref[...].astype(F32), bbc_ref[row].astype(F32)
     if fetch_x:
-        (ax, asm, az, ao), (y_ref, c_ref, ac_ref, s_in), (gx, gs, gz, go), refs = refs[:4], refs[4:8], refs[8:12], refs[12:]
+        (ax, asm, az, ao), (y_ref, c_ref, ac_ref, s_in), (gx, gs, gy, gz, go), refs = refs[:4], refs[4:8], refs[8:13], refs[13:]
     else:
         (ax, gx, gs, az, ao), (y_ref, c_ref, ac_ref, s_in), (gz, go), refs = refs[:5], refs[5:9], refs[9:11], refs[11:]
     (wf, wb, wsem, sm, wdt, cst, st, hcar, xcar, qcar, aoff, ubuf, h_s, la1_s, la2_s, lb1_s, lb2_s, cc_s, cbd_s, row_s, aw_s,
@@ -306,7 +313,8 @@
     if fetch_x:
         xg = Gather(piece_rows(ax, layer), gx, send, recv, 2 * SEMS, False)
         small = Small(asm, gs, *sems)
-        acts += xg.plan(plans[2])
+        yg = Gather(piece_rows(ax, layer + 1), gy, send, recv, 3 * SEMS)
+        acts += xg.plan(plans[2]) + yg.plan(plans[3])
 
     def load_w(slot, zsrc):
         return pltpu.make_async_copy(gx.at[:, pl.ds(2 * zsrc, sp)], wf.at[slot], wsem.at[slot])
@@ -378,7 +386,7 @@
         low = ci[:heads] < SUB
         wT = dtT * jnp.exp2(jnp.where(low, mid, alast) - acT)
         pad = jnp.zeros((BLK - 3 * heads, BLK), BF16)
-        a3, w3 = rows_cat(*split3(acT), pad).T, rows_cat(*split3(wT), pad).T
+        a3, w3 = (rows_cat(*split3(acT), pad).T, rows_cat(*split3(wT), pad).T) if by_z else (acT.T, wT.T)
         ac_ref[:, here_rows] = acT + aoff[:, :1]
         aoff[...] = aoff[...] + alast
 
@@ -493,8 +501,8 @@
         s1, s2, s3 = split3(st[:, sl])
         inter = dot(c12, rows_cat(s1, s1)) + dot(c12, rows_cat(s2, s2)) + dot(c13, rows_cat(s3, s1))
         n3 = e3_ref.shape[0]
-        acx = dot(a3[:, :n3], e3_ref[:, gl])
-        wx = dot(w3[:, :n3], e3_ref[:, gl])
+        wide = lambda v: dot(v[:, :n3], e3_ref[:, gl]) if by_z else per_channel(v, k, heads)
+        acx, wx = wide(a3), wide(w3)
         proj(hs, k + EARLY + 1)
         return x0[k][b * BLK:(b + 1) * BLK], acx, wx, inter
 
@@ -557,6 +565,7 @@
         og.finish()
         if fetch_x:
             xg.drain()
+            yg.finish()
 
         @pl.when(jnp.logical_not(upper))
         def _():
@@ -581,7 +590,7 @@
     gathered = lambda r: jax.ShapeDtypeStruct((n_dp, n_tp, r, PC), F32)
     outs = [jax.ShapeDtypeStruct((n, width), F32), jax.ShapeDtypeStruct((n, NST), F32),
             jax.ShapeDtypeStruct((heads, n), F32), jax.ShapeDtypeStruct((NST, width), F32)]
-    more = ([gathered(PC), jax.ShapeDtypeStruct((n_tp,) + comm[1].shape, F32)] if fetch_x else []) + [gathered(PC)] * 2
+    more = ([gathered(PC), jax.ShapeDtypeStruct((n_tp,) + comm[1].shape, F32), gathered(PC)] if fetch_x else []) + [gathered(PC)] * 2
     vm = pltpu.VMEM
     dma = lambda k: [pltpu.SemaphoreType.DMA((k,))] * 2
     return pl.pallas_call(
@@ -603,42 +612,32 @@
             vm((nb * (NST + SUB), 4 * SUB), BF16), vm((nb * (NST + SUB), 2 * SUB), BF16),
             vm((n, 4 * SUB), BF16), vm((n, 2 * SUB), BF16), vm((n, 4 * NST), BF16), vm((n, LANES), F32),
             vm((2 * nb, 2 * heads // 2, LANES), F32), vm((n, 2 * BLK), BF16), vm((NST, sp * PC), F32), pltpu.SemaphoreType.DMA((2,))]
-        + dma(3 * SEMS) + (dma(8) if fetch_x else []),
+        + dma(4 * SEMS) + (dma(8) if fetch_x else []),
         compiler_params=pltpu.CompilerParams(dimension_semantics=("arbitrary", "arbitrary"), vmem_limit_bytes=VMEM_CAP,
                                              collective_id=cid, has_side_effects=True),
         cost_estimate=pl.CostEstimate(flops=n * 70 * 10 ** 6, bytes_accessed=n * 12000, transcendentals=0),
     )(u, halo, nw, wbc, cbc, bbc, e3, *comm)
 
 
-def p2_body(*refs, geom, mix_in, layer, fetch_x, plans):
+def p2_body(*refs, geom, layer, last):
     n_dp, n_tp, heads = geom
     (u_ref, nw_ref, wz_ref, wo_ref, sm_ref, y_ref, c_ref, ac_ref, s_ref, e3_ref), refs = refs[:10], refs[10:]
-    if fetch_x:
-        (ax, o_ref, f_ref, gx), refs = refs[:4], refs[4:]
-    else:
-        (o_ref, r_ref), refs = refs[:2], refs[2:]
-    (wzb, wob, s3, ubuf, send, recv), refs = refs[:6], refs[6:]
+    (o_ref, f_ref, wzb, wob, s3, ubuf), refs = refs[:6], refs[6:]
     i = pl.program_id(0)
     width = PC * n_tp
-    if fetch_x:
-        xg = Gather(piece_rows(ax, layer + 1), gx, send, recv, 0)
-
-        @pl.when(i == 0)
-        def _():
-            entry_barrier(xg.peers())
-        at_steps(i, xg.plan(plans))
-    else:
-        fbuf, = refs
-        dp, tp, z, c = here()
+    if last:
+        fbuf, send, recv = refs
+        dp, tp, _, c = here()
+        partner = (dp, tp + 1 - 2 * c)
 
         def swap(k):
             return pltpu.make_async_remote_copy(
-                src_ref=fbuf.at[k % 2], dst_ref=r_ref.at[pl.ds(pl.multiple_of(k * BLK2, BLK2), BLK2)],
-                send_sem=send.at[k % 2], recv_sem=recv.at[0], device_id=(dp, 2 * z + 1 - c), device_id_type=MESH)
+                src_ref=fbuf.at[k % 2], dst_ref=f_ref.at[pl.ds(pl.multiple_of(k * BLK2, BLK2), BLK2)],
+                send_sem=send.at[k % 2], recv_sem=recv, device_id=partner, device_id_type=MESH)
 
         @pl.when(i == 0)
         def _():
-            entry_barrier([(dp, 2 * z + 1 - c)])
+            entry_barrier([partner])
 
         @pl.when(i > 1)
         def _():
@@ -660,7 +659,7 @@
             s3[k] = rows_cat(v, w)
 
     u = u_ref[...].astype(F32)
-    u = u if mix_in else unmix(u, ubuf)
+    u = u if last else unmix(u, ubuf)
     h = rms(u, nw_ref[layer:layer + 1].astype(F32))
     c1, c2, c3 = split3(c_ref[...])
     c12, c13 = lanes_cat(c1, c2), lanes_cat(c1, c3)
@@ -676,7 +675,7 @@
     sc = lax.rsqrt(ss / width + EPS)
     g = lanes_cat(*[(v * sc * sm_ref[t, 5:6, :]).astype(BF16) for t, v in enumerate(vs)])
     un = round_bf16(u + dot(g, wob[...]))
-    if fetch_x:
+    if not last:
         o_ref[...] = un.astype(BF16)
         f_ref[...] = un[BLK2 - CAR:]
     else:
@@ -684,19 +683,15 @@
         fbuf[i % 2] = un
         o_ref[...] = un.astype(BF16)
 
-    @pl.when(i == pl.num_programs(0) - 1)
-    def _():
-        if fetch_x:
-            xg.finish()
-        else:
+        @pl.when(i == pl.num_programs(0) - 1)
+        def _():
             swap(i).start()
             for k in range(2):
                 swap(i - 1 + k).wait_send()
-            whole = pltpu.make_async_copy(r_ref, r_ref, recv.at[0])
-            whole.wait()
-
-
-def p2(u, base, nw, wz, wo, sm, y, c, ac, s, e3, comm, n, n_dp, n_tp, mix_in, layer, fetch_x, plans, cid):
+            pltpu.make_async_copy(f_ref, f_ref, recv).wait()
+
+
+def p2(u, base, nw, wz, wo, sm, y, c, ac, s, e3, n, n_dp, n_tp, layer, last, cid):
     d_model, heads = u.shape[-1], PC // HD * n_tp
     width = PC * n_tp
     fixed = lambda shp: pl.BlockSpec(shp, lambda i: (0,) * len(shp), pipeline_mode=pl.Buffered(1))
@@ -706,29 +701,29 @@
     vm = pltpu.VMEM
     outs = [jax.ShapeDtypeStruct((n, d_model), BF16)]
     specs = [rows(d_model)]
-    if fetch_x:
-        outs += [shape(CAR, d_model), shape(n_dp, n_tp, PC, PC)]
-        specs += [pl.BlockSpec((CAR, d_model), lambda i: (0, 0)), hbm]
-    else:
+    if last:
         outs += [shape(n, d_model)]
         specs += [hbm]
+    else:
+        outs += [shape(CAR, d_model)]
+        specs += [pl.BlockSpec((CAR, d_model), lambda i: (0, 0))]
     return pl.pallas_call(
-        functools.partial(p2_body, geom=(n_dp, n_tp, heads), mix_in=mix_in, layer=layer, fetch_x=fetch_x, plans=plans),
+        functools.partial(p2_body, geom=(n_dp, n_tp, heads), layer=layer, last=last),
         name="p2", grid=(n // BLK2,),
         in_specs=[pl.BlockSpec((BLK2, d_model), lambda i: (base() + i, 0)),
                   fixed((2, d_model)),
                   fixed((n_dp, n_tp, PC, PC)), fixed((n_dp, n_tp, PC, PC)),
                   pl.BlockSpec((n_tp, SMALL, PC), lambda i: (0, layer, 0), pipeline_mode=pl.Buffered(1)),
                   rows(width), rows(NST), pl.BlockSpec((heads, BLK2), lambda i: (0, i)),
-                  fixed((NST, width)), fixed((3 * heads, width))] + [hbm] * len(comm),
+                  fixed((NST, width)), fixed((3 * heads, width))],
         out_specs=specs, out_shape=outs,
         scratch_shapes=[vm((d_model, width), BF16), vm((width, d_model), BF16), vm((3, 2 * NST, width), BF16),
                         vm((d_model // LANES * BLK2, LANES), F32)]
-        + [pltpu.SemaphoreType.DMA((SEMS,))] * 2 + ([] if fetch_x else [vm((2, BLK2, d_model), F32)]),
+        + ([vm((2, BLK2, d_model), F32), pltpu.SemaphoreType.DMA((2,)), pltpu.SemaphoreType.DMA] if last else []),
         compiler_params=pltpu.CompilerParams(dimension_semantics=("arbitrary",), vmem_limit_bytes=VMEM_CAP,
-                                             collective_id=cid, has_side_effects=True),
+                                             collective_id=cid, has_side_effects=last),
         cost_estimate=pl.CostEstimate(flops=n * 30 * 10 ** 6, bytes_accessed=n * 12000, transcendentals=0),
-    )(u, nw, wz, wo, sm, y, c, ac, s, e3, *comm)
+    )(u, nw, wz, wo, sm, y, c, ac, s, e3)
 
 
 def finish_body(own_ref, other_ref, o_ref):
@@ -770,11 +765,11 @@
 
 
 PLAN_X = "00020405030607040809"
-PLAN_Z0 = "04090a0c0b0c0e0d0e10"
-PLAN_O0 = "090d0f110f1113111315"
+PLAN_Z0 = "04080a0b0a0b0d0b0d0f"
+PLAN_O0 = "080c0e100e1012101214"
+PLAN_Y = "0d101113121315141516"
 PLAN_Z1 = "0002040604060906080b"
 PLAN_O1 = "06090b0e0b0e100d1013"
-PLAN_X1 = "0003050705070907090a"
 
 
 def solution(mesh):
@@ -798,12 +793,12 @@
         common = (n, n_dp, n_tp)
         bc = (norm_w, w_bc, conv_bc, bias_bc, e3)
 
-        y, c, ac, s, gx, gs, gz, go = p1(u, half(BLK * NBS), halo, *bc, (ax, small, az, ao), *common, False, 0, True,
-                                         (PLAN_Z0, PLAN_O0, PLAN_X), 1)
-        u, f, gx = p2(u, half(BLK2), norm_w, gz, go, gs, y, c, ac, s, e3, (ax,), *common, False, 0, True, PLAN_X1, 2)
+        y, c, ac, s, _, gs, gx, gz, go = p1(u, half(BLK * NBS), halo, *bc, (ax, small, az, ao), *common, False, 0, True,
+                                         (PLAN_Z0, PLAN_O0, PLAN_X, PLAN_Y), 1)
+        u, f = p2(u, half(BLK2), norm_w, gz, go, gs, y, c, ac, s, e3, *common, 0, False, None)
         halo = lax.ppermute(f, 'tp', up)
-        y, c, ac, s, gz, go = p1(u, none, halo, *bc, (ax, gx, gs, az, ao), *common, True, 1, False, (PLAN_Z1, PLAN_O1), 3)
-        own, other = p2(u, none, norm_w, gz, go, gs, y, c, ac, s, e3, (), *common, True, 1, False, None, 4)
+        y, c, ac, s, gz, go = p1(u, none, halo, *bc, (ax, gx, gs, az, ao), *common, True, 1, False, (PLAN_Z1, PLAN_O1), 2)
+        own, other = p2(u, none, norm_w, gz, go, gs, y, c, ac, s, e3, *common, 1, True, 3)
         return finish(own, other)[None]
 
     return jax.shard_map(device_forward, mesh=mesh, in_specs=in_specs, out_specs=P('dp'), check_vma=False)

time: 440 us -> 447 us (1.016)
    pallas_call x2, Pallas kernels: 270 us -> 289 us  [p1(): pl.pallas_call(functools.partial(p1_body, geom=(n_dp, n_tp, heads, nb, nb...]
    pallas_call x2, Pallas kernels: 136 us -> 120 us  [p2(): pl.pallas_call(functools.partial(p2_body, geom=(n_dp, n_tp, heads), layer...]
where the time goes in v9:
time: 447 us; the launch traced here: 444 us
  Pallas kernels  422 us (94%)
  other arithmetic  11.7 us (3%)
  starting transfers between devices  5.17 us (1%)
  local copies, waits for them, and re-layouts  4.48 us (1%)
    pallas_call x2, Pallas kernels, p1(): pl.pallas_call(functools.partial(p1_body, geom=(n_dp, n_tp, heads, nb, nb...  289 us
    pallas_call x2, Pallas kernels, p2(): pl.pallas_call(functools.partial(p2_body, geom=(n_dp, n_tp, heads), layer...  120 us
    pallas_call x1, Pallas kernels, finish(): pl.pallas_call(finish_body, name='finish', grid=(2, ni), in_specs=[pl.Blo...  12.8 us
  transfers between devices with their start and end apart: 1, of which 1 were waited for; matrix products, arithmetic and copies ran while one was open for 0% of the time, Pallas kernels for 0%

profile of v9, /device:TPU:0, one launch (start us, length us, event | category | flops | bytes accessed | tf_op | source)
XLA Modules:
  0.0 444.3 jit_solution(9213326857900705008)
XLA Ops:
  0.0 0.0 copy-start
  0.0 0.0 copy-start.1
  0.0 0.7 negate_multiply_fusion
  0.7 0.7 bitcast_convert_fusion.1
  1.4 0.7 bitcast_convert_fusion
  2.1 0.7 broadcast_in_dim.15
  2.8 0.1 reshape.41
  2.9 0.7 convert_bitcast_fusion
  3.7 0.9 slice_bitcast_fusion
  4.6 0.1 copy.21
  4.7 2.7 convert_element_type.23.refs_9_.refs_10_
  7.4 2.7 convert_element_type.21.refs_7_
  10.1 2.8 convert_element_type.24.refs_10_.refs_11_
  12.9 0.6 select_bitcast_fusion.refs_1_
  13.6 0.1 broadcast_in_dim.32
  13.6 0.0 copy-done.1
  13.7 0.1 broadcast_in_dim.31
  13.7 0.0 copy-done
  13.7 1.8 concatenate.3
  15.6 165.1 %p1.2 = (f32[3072,2048]{1,0:T(8,128)}, f32[3072,128]{1,0:T(8,128)}, f32[32,3072]{1,0:T(8,128)}, f32[128,2048]{1,0:T(8,128)}, f32[4,8,256,256]{3,2,1,0:T(8,128)},...) custom-call(bf16[6144,1024]{1,0:T(8,128)(2,1)} %bitcast.20, ...), custom_call_target="tpu_custom_call" | custom-call | flops 215040000000 | bytes 36864000 | tf_op jit(solution)/shard_map/p1/pallas_call | solution.py:596
  180.6 58.9 %p2.2 = (bf16[3072,1024]{1,0:T(8,128)(2,1)}, f32[24,1024]{1,0:T(8,128)}) custom-call(bf16[6144,1024]{1,0:T(8,128)(2,1)} %bitcast.21, bf16[2,1024]{1,0:T(2,128)(2,1)} %refs_1_.3, f32[4,8,256,256]{3,2,1,0:T(8,128)} %get-tuple-element.23.refs_2_, f32[4,8,256,256]{3,2,1,0:T(8,128)} %get-tuple-element.24.refs_3_, ...), custom_call_target="tpu_custom_call" | custom-call | flops 92160000000 | bytes 36864000 | tf_op jit(solution)/shard_map/p2/pallas_call | solution.py:710
  239.5 5.2 %collective-permute-start = (f32[24,1024]{1,0:T(8,128)}, f32[24,1024]{1,0:T(8,128)S(1)}, u32[]{:S(2)}, u32[]{:S(2)}) collective-permute-start(f32[24,1024]{1,0:T(8,128)} %get-tuple-element.31), channel_id=1, source_target_pairs={{0,1},{2,3},{4,5},{6,7},{8,9},{10,11},{12,13},{14,15},{16,17},{18,... | collective-permute-start | bytes 294920 | tf_op jit(solution)/shard_map/ppermute | solution.py:799
  244.7 0.9 collective-permute-done.refs_1_
  245.6 0.0 copy-start.2
  245.6 0.6 copy-done.2
  246.2 123.9 %p1.3 = (f32[3072,2048]{1,0:T(8,128)}, f32[3072,128]{1,0:T(8,128)}, f32[32,3072]{1,0:T(8,128)}, f32[128,2048]{1,0:T(8,128)}, f32[4,8,256,256]{3,2,1,0:T(8,128)}, /*index=5*/f32[4,8,256,256]{3,2,1,0:T(8,128)}) custom-call(bf16[3072,1024]{1,0:T(8,128)(2,1)} %get-tuple-element.30.refs_0_, f32[24,1024]{1,0:T(8,128)} %copy-done.2, bf16[2,1024]{1,0:T(2,128)(2,1)} %refs_1_.3, ...), custom_call_target="tpu_custom_call" | custom-call | flops 215040000000 | bytes 36864000 | tf_op jit(solution)/shard_map/p1/pallas_call | solution.py:596
  370.1 61.3 %p2.3 = (bf16[3072,1024]{1,0:T(8,128)(2,1)}, f32[3072,1024]{1,0:T(8,128)}) custom-call(bf16[3072,1024]{1,0:T(8,128)(2,1)} %get-tuple-element.30.refs_0_, bf16[2,1024]{1,0:T(2,128)(2,1)} %refs_1_.3, f32[4,8,256,256]{3,2,1,0:T(8,128)} %get-tuple-element.33.refs_2_, f32[4,8,256,256]{3,2,1,0:T(8,128)} %get-tuple-element.34.refs_3_, ...), custom_call_target="tpu_custom_call" | custom-call | flops 92160000000 | bytes 36864000 | tf_op jit(solution)/shard_map/p2/pallas_call | solution.py:710
  431.5 12.8 %finish.1 = bf16[6144,1024]{1,0:T(8,128)(2,1)} custom-call(bf16[3072,1024]{1,0:T(8,128)(2,1)} %get-tuple-element.39.own_ref, f32[3072,1024]{1,0:T(8,128)} %get-tuple-element.40.other_ref), custom_call_target="tpu_custom_call" | custom-call | flops 3145728 | bytes 25165824 | tf_op jit(solution)/shard_map/finish/pallas_call | solution.py:746
  (4 shorter events, 0.0 us)
Async XLA Ops:
  0.0 13.7 %copy-start = (bf16[2,4,256]{2,1,0:T(4,128)(2,1)S(1)}, bf16[2,4,256]{2,1,0:T(4,128)(2,1)}, u32[]{:S(2)}) copy-start(bf16[2,4,256]{2,1,0:T(4,128)(2,1)} %param.22) | copy-start | bytes 12292
  0.0 13.6 %copy-start.1 = (f32[2,4]{1,0:T(2,128)S(1)}, f32[2,4]{1,0:T(2,128)}, u32[]{:S(2)}) copy-start(f32[2,4]{1,0:T(2,128)} %param.26) | copy-start | bytes 100
  239.5 6.1 %collective-permute-start = (f32[24,1024]{1,0:T(8,128)}, f32[24,1024]{1,0:T(8,128)S(1)}, u32[]{:S(2)}, u32[]{:S(2)}) collective-permute-start(f32[24,1024]{1,0:T(8,128)} %get-tuple-element.31), channel_id=1, source_target_pairs={{0,1},{2,3},{4,5},{6,7},{8,9},{10,11},{12,13},{14,15},{16,17},{18,... | collective-permute-start | bytes 294920 | tf_op jit(solution)/shard_map/ppermute | solution.py:799
  245.6 0.6 copy-start.2

commit v10 on v9

--- a/solution.py
+++ b/solution.py
@@ -101,13 +101,6 @@
     return jnp.asarray(np.tile(one, (3, 1)), BF16)
 
 
-def per_channel(v, t, heads):
-    n, per = v.shape[0], PC // HD
-    low = lax.broadcasted_iota(jnp.int32, (n, LANES), 1) < HD
-    wide = [jnp.broadcast_to(v[:, r:r + 1], (n, LANES)) for r in [head_row(h, heads) for h in range(per * t, per * (t + 1))]]
-    return lanes_cat(*[jnp.where(low, a, b) for a, b in zip(wide[::2], wide[1::2])])
-
-
 def kcat6(parts):
     a, b, c = parts
     return lanes_cat(a, b, c, a), lanes_cat(b, a)
@@ -134,20 +127,17 @@
 
 
 class Gather:
-    def __init__(self, piece, g, send, recv, base, keep=True):
+    def __init__(self, piece, g, send, recv, base):
         self.piece, self.g, self.send, self.recv, self.base = piece, g, send, recv, base
         self.dp, self.tp, self.z, self.c = here()
         x, y = self.dp // 2, self.dp % 2
         self.side = ((1 - x) * 2 + y, x * 2 + 1 - y)
         self.partner = (self.dp, 2 * self.z + 1 - self.c)
-        self.quarters, self.keep = g.shape[0], keep
+        self.quarters = g.shape[0]
 
     def rdma(self, k, src, dst, dev):
         return pltpu.make_async_remote_copy(src_ref=src, dst_ref=dst, send_sem=self.send.at[self.base + k],
                                             recv_sem=self.recv.at[self.base + k], device_id=dev, device_id_type=MESH)
-
-    def local(self, q):
-        return pltpu.make_async_copy(self.piece(q), self.g.at[q, self.tp], self.send.at[self.base + q])
 
     def own(self, q):
         return self.rdma(4 + q, self.piece(q), self.g.at[q, self.tp], self.partner)
@@ -178,9 +168,6 @@
             self.own(q).start()
         for dz in ORDER:
             self.line(dz).start()
-        if self.keep:
-            for q in range(self.quarters):
-                self.local(q).start()
 
     def spread(self, dz):
         self.line(dz).wait_recv()
@@ -200,8 +187,6 @@
     def settle_own(self):
         for q in range(self.quarters):
             self.own(q).wait_recv()
-            if self.keep:
-                self.local(q).wait()
 
     def settle(self, dz):
         self.over(dz).wait_recv()
@@ -283,13 +268,13 @@
 
 def p1_body(*refs, geom, mixed, layer, fetch_x, plans):
     n_dp, n_tp, heads, nb, nbs, sp = geom
-    (u_ref, halo_ref, nw_ref, wbc_ref, cbc_ref, bbc_ref, e3_ref), refs = refs[:7], refs[7:]
+    (u_ref, halo_ref, nw_ref, wbc_ref, cbc_ref, bbc_ref, e3_ref, own_ref), refs = refs[:8], refs[8:]
     row = slice(layer, layer + 1)
     nw, cbc, bbc = nw_ref[row].astype(F32), cbc_ref[...].astype(F32), bbc_ref[row].astype(F32)
     if fetch_x:
         (ax, asm, az, ao), (y_ref, c_ref, ac_ref, s_in), (gx, gs, gy, gz, go), refs = refs[:4], refs[4:8], refs[8:13], refs[13:]
     else:
-        (ax, gx, gs, az, ao), (y_ref, c_ref, ac_ref, s_in), (gz, go), refs = refs[:5], refs[5:9], refs[9:11], refs[11:]
+        (gx, gs, az, ao), (y_ref, c_ref, ac_ref, s_in), (gz, go), refs = refs[:4], refs[4:8], refs[8:10], refs[10:]
     (wf, wb, wsem, sm, wdt, cst, st, hcar, xcar, qcar, aoff, ubuf, h_s, la1_s, la2_s, lb1_s, lb2_s, cc_s, cbd_s, row_s, aw_s,
      sbuf, hsem, send, recv), sems = refs[:25], refs[25:]
     p, i = pl.program_id(0), pl.program_id(1)
@@ -311,7 +296,7 @@
     og = Gather(piece_cols(ao, layer), go, send, recv, SEMS)
     acts = zg.plan(plans[0]) + og.plan(plans[1])
     if fetch_x:
-        xg = Gather(piece_rows(ax, layer), gx, send, recv, 2 * SEMS, False)
+        xg = Gather(piece_rows(ax, layer), gx, send, recv, 2 * SEMS)
         small = Small(asm, gs, *sems)
         yg = Gather(piece_rows(ax, layer + 1), gy, send, recv, 3 * SEMS)
         acts += xg.plan(plans[2]) + yg.plan(plans[3])
@@ -319,10 +304,9 @@
     def load_w(slot, zsrc):
         return pltpu.make_async_copy(gx.at[:, pl.ds(2 * zsrc, sp)], wf.at[slot], wsem.at[slot])
 
-    def load_own():
+    def load_first():
         _, tp, _, c = here()
-        return ([pltpu.make_async_copy(piece_rows(ax, layer)(q), wf.at[0, q, c], wsem.at[0]) for q in range(n_dp)]
-                + [pltpu.make_async_copy(gx.at[q, tp + 1 - 2 * c], wf.at[0, q, 1 - c], wsem.at[0]) for q in range(n_dp)])
+        return pltpu.make_async_copy(gx.at[:, tp + 1 - 2 * c], wf.at[0, :, 1 - c], wsem.at[0]) if by_z else load_w(0, 0)
 
     @pl.when(step == 0)
     def _():
@@ -336,11 +320,7 @@
         if fetch_x:
             small.finish()
             xg.settle_own()
-        if by_z:
-            for v in load_own():
-                v.start()
-        else:
-            load_w(0, 0).start()
+        load_first().start()
         cp = pltpu.make_async_copy(gs.at[:, pl.ds(layer * SMALL, SMALL)], sm, wsem.at[2])
         cp.start()
         cp.wait()
@@ -386,7 +366,7 @@
         low = ci[:heads] < SUB
         wT = dtT * jnp.exp2(jnp.where(low, mid, alast) - acT)
         pad = jnp.zeros((BLK - 3 * heads, BLK), BF16)
-        a3, w3 = (rows_cat(*split3(acT), pad).T, rows_cat(*split3(wT), pad).T) if by_z else (acT.T, wT.T)
+        a3, w3 = rows_cat(*split3(acT), pad).T, rows_cat(*split3(wT), pad).T
         ac_ref[:, here_rows] = acT + aoff[:, :1]
         aoff[...] = aoff[...] + alast
 
@@ -452,8 +432,7 @@
 
         @pl.when(p == 0)
         def _():
-            for v in load_own() if by_z else [load_w(0, 0)]:
-                v.wait()
+            load_first().wait()
 
         @pl.when(p > 0)
         def _():
@@ -461,6 +440,12 @@
         for q in range(n_dp):
             for k in range(sp):
                 wb[q * PC:(q + 1) * PC, k * PC:(k + 1) * PC] = wf[slot, q, k].astype(BF16)
+
+        @pl.when(p == 0)
+        def _():
+            _, tp, _, c = here()
+            wb[:, pl.ds(pl.multiple_of((c if by_z else tp) * PC, PC), PC)] = own_ref[...].astype(BF16)
+
         @pl.when((p > 0) & jnp.logical_not(upper))
         def _():
             state_out(p - 1).start()
@@ -501,7 +486,7 @@
         s1, s2, s3 = split3(st[:, sl])
         inter = dot(c12, rows_cat(s1, s1)) + dot(c12, rows_cat(s2, s2)) + dot(c13, rows_cat(s3, s1))
         n3 = e3_ref.shape[0]
-        wide = lambda v: dot(v[:, :n3], e3_ref[:, gl]) if by_z else per_channel(v, k, heads)
+        wide = lambda v: dot(v[:, :n3], e3_ref[:, gl])
         acx, wx = wide(a3), wide(w3)
         proj(hs, k + EARLY + 1)
         return x0[k][b * BLK:(b + 1) * BLK], acx, wx, inter
@@ -577,7 +562,7 @@
             pltpu.make_async_copy(s_in, s_in, hsem.at[1]).wait()
 
 
-def p1(u, base, halo, nw, wbc, cbc, bbc, e3, comm, n, n_dp, n_tp, mixed, layer, fetch_x, plans, cid):
+def p1(u, base, halo, nw, wbc, cbc, bbc, e3, own, comm, n, n_dp, n_tp, mixed, layer, fetch_x, plans, cid):
     d_model, heads = u.shape[-1], PC // HD * n_tp
     sp, nbs = (2, NBS) if fetch_x else (n_tp, 1)
     width, nb, rows = PC * n_tp, n // BLK, BLK * nbs
@@ -598,7 +583,7 @@
         name="p1", grid=(n_tp // sp, ni),
         in_specs=[pl.BlockSpec((rows, d_model), lambda p, i: (base() + once(p, i), 0)),
                   fixed((CAR, d_model)), fixed((2, d_model)), own_layer(d_model, PC), own_layer(4, PC), fixed((2, PC)),
-                  fixed((3 * heads, width))] + [hbm] * len(comm),
+                  fixed((3 * heads, width)), own_layer(d_model, PC)] + [hbm] * len(comm),
         out_specs=[pl.BlockSpec((rows, sp * PC), lambda p, i: (i, col(p))),
                    pl.BlockSpec((rows, NST), lambda p, i: (once(p, i), 0)),
                    pl.BlockSpec((heads, rows), lambda p, i: (0, once(p, i))),
@@ -616,12 +601,12 @@
         compiler_params=pltpu.CompilerParams(dimension_semantics=("arbitrary", "arbitrary"), vmem_limit_bytes=VMEM_CAP,
                                              collective_id=cid, has_side_effects=True),
         cost_estimate=pl.CostEstimate(flops=n * 70 * 10 ** 6, bytes_accessed=n * 12000, transcendentals=0),
-    )(u, halo, nw, wbc, cbc, bbc, e3, *comm)
+    )(u, halo, nw, wbc, cbc, bbc, e3, own, *comm)
 
 
 def p2_body(*refs, geom, layer, last):
     n_dp, n_tp, heads = geom
-    (u_ref, nw_ref, wz_ref, wo_ref, sm_ref, y_ref, c_ref, ac_ref, s_ref, e3_ref), refs = refs[:10], refs[10:]
+    (u_ref, nw_ref, wz_ref, wo_ref, ownz_ref, owno_ref, sm_ref, y_ref, c_ref, ac_ref, s_ref, e3_ref), refs = refs[:12], refs[12:]
     (o_ref, f_ref, wzb, wob, s3, ubuf), refs = refs[:6], refs[6:]
     i = pl.program_id(0)
     width = PC * n_tp
@@ -654,6 +639,9 @@
                 a, b = slice(d * PC, (d + 1) * PC), slice(t * PC, (t + 1) * PC)
                 wzb[a, b] = wz_ref[d, t].astype(BF16)
                 wob[b, a] = wo_ref[d, t].astype(BF16)
+        mine = pl.ds(pl.multiple_of(here()[1] * PC, PC), PC)
+        wzb[:, mine] = ownz_ref[...].astype(BF16)
+        wob[mine, :] = owno_ref[...].astype(BF16)
         a, b, c_ = split3(jnp.where(here()[3] == 1, s_ref[...], 0.0))
         for k, (v, w) in enumerate(((a, a), (b, b), (c_, a))):
             s3[k] = rows_cat(v, w)
@@ -691,10 +679,11 @@
             pltpu.make_async_copy(f_ref, f_ref, recv).wait()
 
 
-def p2(u, base, nw, wz, wo, sm, y, c, ac, s, e3, n, n_dp, n_tp, layer, last, cid):
+def p2(u, base, nw, wz, wo, az, ao, sm, y, c, ac, s, e3, n, n_dp, n_tp, layer, last, cid):
     d_model, heads = u.shape[-1], PC // HD * n_tp
     width = PC * n_tp
     fixed = lambda shp: pl.BlockSpec(shp, lambda i: (0,) * len(shp), pipeline_mode=pl.Buffered(1))
+    own_layer = lambda *shp: pl.BlockSpec((None,) + shp, lambda i: (layer, 0, 0), pipeline_mode=pl.Buffered(1))
     hbm = pl.BlockSpec(memory_space=pl.ANY)
     rows = lambda w: pl.BlockSpec((BLK2, w), lambda i: (i, 0))
     shape = lambda *s: jax.ShapeDtypeStruct(s, F32)
@@ -712,7 +701,7 @@
         name="p2", grid=(n // BLK2,),
         in_specs=[pl.BlockSpec((BLK2, d_model), lambda i: (base() + i, 0)),
                   fixed((2, d_model)),
-                  fixed((n_dp, n_tp, PC, PC)), fixed((n_dp, n_tp, PC, PC)),
+                  fixed((n_dp, n_tp, PC, PC)), fixed((n_dp, n_tp, PC, PC)), own_layer(d_model, PC), own_layer(PC, d_model),
                   pl.BlockSpec((n_tp, SMALL, PC), lambda i: (0, layer, 0), pipeline_mode=pl.Buffered(1)),
                   rows(width), rows(NST), pl.BlockSpec((heads, BLK2), lambda i: (0, i)),
                   fixed((NST, width)), fixed((3 * heads, width))],
@@ -723,7 +712,7 @@
         compiler_params=pltpu.CompilerParams(dimension_semantics=("arbitrary",), vmem_limit_bytes=VMEM_CAP,
                                              collective_id=cid, has_side_effects=last),
         cost_estimate=pl.CostEstimate(flops=n * 30 * 10 ** 6, bytes_accessed=n * 12000, transcendentals=0),
-    )(u, nw, wz, wo, sm, y, c, ac, s, e3)
+    )(u, nw, wz, wo, az, ao, sm, y, c, ac, s, e3)
 
 
 def finish_body(own_ref, other_ref, o_ref):
@@ -791,14 +780,14 @@
         half = lambda blk: (lambda: lax.axis_index('tp') % 2 * (n // blk))
         none = lambda: 0
         common = (n, n_dp, n_tp)
-        bc = (norm_w, w_bc, conv_bc, bias_bc, e3)
+        bc = (norm_w, w_bc, conv_bc, bias_bc, e3, ax)
 
         y, c, ac, s, _, gs, gx, gz, go = p1(u, half(BLK * NBS), halo, *bc, (ax, small, az, ao), *common, False, 0, True,
                                          (PLAN_Z0, PLAN_O0, PLAN_X, PLAN_Y), 1)
-        u, f = p2(u, half(BLK2), norm_w, gz, go, gs, y, c, ac, s, e3, *common, 0, False, None)
+        u, f = p2(u, half(BLK2), norm_w, gz, go, az, ao, gs, y, c, ac, s, e3, *common, 0, False, None)
         halo = lax.ppermute(f, 'tp', up)
-        y, c, ac, s, gz, go = p1(u, none, halo, *bc, (ax, gx, gs, az, ao), *common, True, 1, False, (PLAN_Z1, PLAN_O1), 2)
-        own, other = p2(u, none, norm_w, gz, go, gs, y, c, ac, s, e3, *common, 1, True, 3)
+        y, c, ac, s, gz, go = p1(u, none, halo, *bc, (gx, gs, az, ao), *common, True, 1, False, (PLAN_Z1, PLAN_O1), 2)
+        own, other = p2(u, none, norm_w, gz, go, az, ao, gs, y, c, ac, s, e3, *common, 1, True, 3)
         return finish(own, other)[None]
 
     return jax.shard_map(device_forward, mesh=mesh, in_specs=in_specs, out_specs=P('dp'), check_vma=False)

time: 447 us -> 449 us (level)
  no operation moved by 1% of the time
where the time goes in v10:
time: 449 us; the launch traced here: 447 us
  Pallas kernels  424 us (94%)
  other arithmetic  11.7 us (3%)
  starting transfers between devices  5.16 us (1%)
    pallas_call x2, Pallas kernels, p1(): pl.pallas_call(functools.partial(p1_body, geom=(n_dp, n_tp, heads, nb, nb...  290 us
    pallas_call x2, Pallas kernels, p2(): pl.pallas_call(functools.partial(p2_body, geom=(n_dp, n_tp, heads), layer...  122 us
    pallas_call x1, Pallas kernels, finish(): pl.pallas_call(finish_body, name='finish', grid=(2, ni), in_specs=[pl.Blo...  12.8 us
  transfers between devices with their start and end apart: 1, of which 1 were waited for; matrix products, arithmetic and copies ran while one was open for 0% of the time, Pallas kernels for 0%

profile of v10, /device:TPU:0, one launch (start us, length us, event | category | flops | bytes accessed | tf_op | source)
XLA Modules:
  0.0 446.7 jit_solution(352829888820976048)
XLA Ops:
  0.0 0.0 copy-start
  0.0 0.0 copy-start.1
  0.0 0.7 negate_multiply_fusion
  0.7 0.7 bitcast_convert_fusion.1
  1.4 0.7 bitcast_convert_fusion
  2.1 0.7 broadcast_in_dim.15
  2.8 0.1 reshape.41
  2.9 0.7 convert_bitcast_fusion
  3.7 0.9 slice_bitcast_fusion
  4.6 0.1 copy.21
  4.7 2.7 convert_element_type.23.refs_10_.refs_4_
  7.4 2.8 convert_element_type.24.refs_11_.refs_5_
  10.2 2.7 convert_element_type.21.refs_7_.refs_8_
  12.9 0.6 select_bitcast_fusion.refs_1_
  13.6 0.1 broadcast_in_dim.32
  13.6 0.0 copy-done.1
  13.7 0.1 broadcast_in_dim.31
  13.7 0.0 copy-done
  13.7 1.8 concatenate.3
  15.6 165.1 %p1.2 = (f32[3072,2048]{1,0:T(8,128)}, f32[3072,128]{1,0:T(8,128)}, f32[32,3072]{1,0:T(8,128)}, f32[128,2048]{1,0:T(8,128)}, f32[4,8,256,256]{3,2,1,0:T(8,128)},...) custom-call(bf16[6144,1024]{1,0:T(8,128)(2,1)} %bitcast.20, ...), custom_call_target="tpu_custom_call" | custom-call | flops 215040000000 | bytes 36864000 | tf_op jit(solution)/shard_map/p1/pallas_call | solution.py:581
  180.7 59.8 %p2.2 = (bf16[3072,1024]{1,0:T(8,128)(2,1)}, f32[24,1024]{1,0:T(8,128)}) custom-call(bf16[6144,1024]{1,0:T(8,128)(2,1)} %bitcast.21, bf16[2,1024]{1,0:T(2,128)(2,1)} %refs_1_.3, f32[4,8,256,256]{3,2,1,0:T(8,128)} %get-tuple-element.23.refs_2_, f32[4,8,256,256]{3,2,1,0:T(8,128)} %get-tuple-element.24.refs_3_, ...), custom_call_target="tpu_custom_call" | custom-call | flops 92160000000 | bytes 36864000 | tf_op jit(solution)/shard_map/p2/pallas_call | solution.py:699
  240.4 5.2 %collective-permute-start = (f32[24,1024]{1,0:T(8,128)}, f32[24,1024]{1,0:T(8,128)S(1)}, u32[]{:S(2)}, u32[]{:S(2)}) collective-permute-start(f32[24,1024]{1,0:T(8,128)} %get-tuple-element.31), channel_id=1, source_target_pairs={{0,1},{2,3},{4,5},{6,7},{8,9},{10,11},{12,13},{14,15},{16,17},{18,... | collective-permute-start | bytes 294920 | tf_op jit(solution)/shard_map/ppermute | solution.py:788
  245.6 0.9 collective-permute-done.refs_1_
  246.5 0.0 copy-start.2
  246.5 0.6 copy-done.2
  247.2 124.5 %p1.3 = (f32[3072,2048]{1,0:T(8,128)}, f32[3072,128]{1,0:T(8,128)}, f32[32,3072]{1,0:T(8,128)}, f32[128,2048]{1,0:T(8,128)}, f32[4,8,256,256]{3,2,1,0:T(8,128)}, /*index=5*/f32[4,8,256,256]{3,2,1,0:T(8,128)}) custom-call(bf16[3072,1024]{1,0:T(8,128)(2,1)} %get-tuple-element.30.refs_0_, f32[24,1024]{1,0:T(8,128)} %copy-done.2, bf16[2,1024]{1,0:T(2,128)(2,1)} %refs_1_.3, ...), custom_call_target="tpu_custom_call" | custom-call | flops 215040000000 | bytes 36864000 | tf_op jit(solution)/shard_map/p1/pallas_call | solution.py:581
  371.6 62.2 %p2.3 = (bf16[3072,1024]{1,0:T(8,128)(2,1)}, f32[3072,1024]{1,0:T(8,128)}) custom-call(bf16[3072,1024]{1,0:T(8,128)(2,1)} %get-tuple-element.30.refs_0_, bf16[2,1024]{1,0:T(2,128)(2,1)} %refs_1_.3, f32[4,8,256,256]{3,2,1,0:T(8,128)} %get-tuple-element.33.refs_2_, f32[4,8,256,256]{3,2,1,0:T(8,128)} %get-tuple-element.34.refs_3_, ...), custom_call_target="tpu_custom_call" | custom-call | flops 92160000000 | bytes 36864000 | tf_op jit(solution)/shard_map/p2/pallas_call | solution.py:699
  433.8 12.8 %finish.1 = bf16[6144,1024]{1,0:T(8,128)(2,1)} custom-call(bf16[3072,1024]{1,0:T(8,128)(2,1)} %get-tuple-element.39.own_ref, f32[3072,1024]{1,0:T(8,128)} %get-tuple-element.40.other_ref), custom_call_target="tpu_custom_call" | custom-call | flops 3145728 | bytes 25165824 | tf_op jit(solution)/shard_map/finish/pallas_call | solution.py:735
  (4 shorter events, 0.0 us)
Async XLA Ops:
  0.0 13.7 %copy-start = (bf16[2,4,256]{2,1,0:T(4,128)(2,1)S(1)}, bf16[2,4,256]{2,1,0:T(4,128)(2,1)}, u32[]{:S(2)}) copy-start(bf16[2,4,256]{2,1,0:T(4,128)(2,1)} %param.22) | copy-start | bytes 12292
  0.0 13.6 %copy-start.1 = (f32[2,4]{1,0:T(2,128)S(1)}, f32[2,4]{1,0:T(2,128)}, u32[]{:S(2)}) copy-start(f32[2,4]{1,0:T(2,128)} %param.26) | copy-start | bytes 100
  240.4 6.1 %collective-permute-start = (f32[24,1024]{1,0:T(8,128)}, f32[24,1024]{1,0:T(8,128)S(1)}, u32[]{:S(2)}, u32[]{:S(2)}) collective-permute-start(f32[24,1024]{1,0:T(8,128)} %get-tuple-element.31), channel_id=1, source_target_pairs={{0,1},{2,3},{4,5},{6,7},{8,9},{10,11},{12,13},{14,15},{16,17},{18,... | collective-permute-start | bytes 294920 | tf_op jit(solution)/shard_map/ppermute | solution.py:788
  246.5 0.6 copy-start.2

commit v11 on v8

--- a/solution.py
+++ b/solution.py
@@ -769,12 +769,12 @@
     return jnp.concatenate(v, axis=1).reshape(-1, PC)
 
 
-PLAN_X = "00020405030607040809"
-PLAN_Z0 = "04090a0c0b0c0e0d0e10"
-PLAN_O0 = "090d0f110f1113111315"
-PLAN_Z1 = "0002040604060906080b"
-PLAN_O1 = "06090b0e0b0e100d1013"
-PLAN_X1 = "0003050705070907090a"
+PLAN_X = "00010305030507040709"
+PLAN_Z0 = "0407080b0a0b0e0d0e11"
+PLAN_O0 = "080c0e110f1113121315"
+PLAN_Z1 = "0003050806080b090b0e"
+PLAN_O1 = "000a0c0f0d0f12101214"
+PLAN_X1 = "0003050806080a080a0b"
 
 
 def solution(mesh):

time: 440 us -> 435 us (0.989)
    pallas_call x2, Pallas kernels: 270 us -> 265 us  [p1(): pl.pallas_call(functools.partial(p1_body, geom=(n_dp, n_tp, heads, nb, nb...]
where the time goes in v11:
time: 435 us
  Pallas kernels  416 us (96%)
  other arithmetic  11.7 us (3%)
  local copies, waits for them, and re-layouts  4.49 us (1%)
    pallas_call x2, Pallas kernels, p1(): pl.pallas_call(functools.partial(p1_body, geom=(n_dp, n_tp, heads, nb, nb...  265 us
    pallas_call x2, Pallas kernels, p2(): pl.pallas_call(functools.partial(p2_body, geom=(n_dp, n_tp, heads), mix_i...  138 us
    pallas_call x1, Pallas kernels, finish(): pl.pallas_call(finish_body, name='finish', grid=(2, ni), in_specs=[pl.Blo...  12.8 us
  transfers between devices with their start and end apart: 1, of which 1 were waited for; matrix products, arithmetic and copies ran while one was open for 0% of the time, Pallas kernels for 0%

profile of v11, /device:TPU:0, one launch (start us, length us, event | category | flops | bytes accessed | tf_op | source)
XLA Modules:
  0.0 434.7 jit_solution(11947665143899241503)
XLA Ops:
  0.0 0.0 copy-start
  0.0 0.0 copy-start.1
  0.0 0.7 negate_multiply_fusion
  0.7 0.7 bitcast_convert_fusion.1
  1.4 0.7 bitcast_convert_fusion
  2.1 0.7 broadcast_in_dim.15
  2.8 0.1 reshape.41
  2.9 0.7 convert_bitcast_fusion
  3.7 0.9 slice_bitcast_fusion
  4.6 0.1 copy.21
  4.7 2.7 convert_element_type.21.refs_7_.refs_10_
  7.4 2.7 convert_element_type.23.refs_9_.refs_10_
  10.1 2.8 convert_element_type.24.refs_10_.refs_11_
  12.9 0.6 select_bitcast_fusion.refs_1_
  13.5 0.1 broadcast_in_dim.32
  13.6 0.0 copy-done.1
  13.6 0.1 broadcast_in_dim.31
  13.7 0.0 copy-done
  13.7 1.9 concatenate.3
  15.5 150.6 %p1.2 = (f32[3072,2048]{1,0:T(8,128)}, f32[3072,128]{1,0:T(8,128)}, f32[32,3072]{1,0:T(8,128)}, f32[128,2048]{1,0:T(8,128)}, f32[4,8,256,256]{3,2,1,0:T(8,128)},...) custom-call(bf16[6144,1024]{1,0:T(8,128)(2,1)} %bitcast.20, ...), custom_call_target="tpu_custom_call" | custom-call | flops 215040000000 | bytes 36864000 | tf_op jit(solution)/shard_map/p1/pallas_call | solution.py:587
  166.1 76.0 %p2.2 = (bf16[3072,1024]{1,0:T(8,128)(2,1)}, f32[24,1024]{1,0:T(8,128)}, f32[4,8,256,256]{3,2,1,0:T(8,128)}) custom-call(bf16[6144,1024]{1,0:T(8,128)(2,1)} %bitcast.21, bf16[2,1024]{1,0:T(2,128)(2,1)} %refs_1_.3, f32[4,8,256,256]{3,2,1,0:T(8,128)} %get-tuple-element.23.refs_2_, f32[4,8,256,256]{3,2,1,0:T(8,128)} %get-tuple-element.24.refs_3_, ...), custom_call_target="tpu_custom_call" | custom-call | flops 92160000000 | bytes 36864000 | tf_op jit(solution)/shard_map/p2/pallas_call | solution.py:715
  242.1 1.5 collective-permute-start
  243.7 0.9 collective-permute-done.refs_1_
  244.6 0.0 copy-start.2
  244.6 0.6 copy-done.2
  245.2 114.8 %p1.3 = (f32[3072,2048]{1,0:T(8,128)}, f32[3072,128]{1,0:T(8,128)}, f32[32,3072]{1,0:T(8,128)}, f32[128,2048]{1,0:T(8,128)}, f32[4,8,256,256]{3,2,1,0:T(8,128)}, /*index=5*/f32[4,8,256,256]{3,2,1,0:T(8,128)}) custom-call(bf16[3072,1024]{1,0:T(8,128)(2,1)} %get-tuple-element.30.refs_0_, f32[24,1024]{1,0:T(8,128)} %copy-done.2, bf16[2,1024]{1,0:T(2,128)(2,1)} %refs_1_.3, ...), custom_call_target="tpu_custom_call" | custom-call | flops 215040000000 | bytes 36864000 | tf_op jit(solution)/shard_map/p1/pallas_call | solution.py:587
  360.0 61.8 %p2.3 = (bf16[3072,1024]{1,0:T(8,128)(2,1)}, f32[3072,1024]{1,0:T(8,128)}) custom-call(bf16[3072,1024]{1,0:T(8,128)(2,1)} %get-tuple-element.30.refs_0_, bf16[2,1024]{1,0:T(2,128)(2,1)} %refs_1_.3, f32[4,8,256,256]{3,2,1,0:T(8,128)} %get-tuple-element.33.refs_2_, f32[4,8,256,256]{3,2,1,0:T(8,128)} %get-tuple-element.34.refs_3_, ...), custom_call_target="tpu_custom_call" | custom-call | flops 92160000000 | bytes 36864000 | tf_op jit(solution)/shard_map/p2/pallas_call | solution.py:715
  421.9 12.8 %finish.1 = bf16[6144,1024]{1,0:T(8,128)(2,1)} custom-call(bf16[3072,1024]{1,0:T(8,128)(2,1)} %get-tuple-element.39.own_ref, f32[3072,1024]{1,0:T(8,128)} %get-tuple-element.40.other_ref), custom_call_target="tpu_custom_call" | custom-call | flops 3145728 | bytes 25165824 | tf_op jit(solution)/shard_map/finish/pallas_call | solution.py:751
  (4 shorter events, 0.0 us)
Async XLA Ops:
  0.0 13.7 %copy-start = (bf16[2,4,256]{2,1,0:T(4,128)(2,1)S(1)}, bf16[2,4,256]{2,1,0:T(4,128)(2,1)}, u32[]{:S(2)}) copy-start(bf16[2,4,256]{2,1,0:T(4,128)(2,1)} %param.22) | copy-start | bytes 12292
  0.0 13.6 %copy-start.1 = (f32[2,4]{1,0:T(2,128)S(1)}, f32[2,4]{1,0:T(2,128)}, u32[]{:S(2)}) copy-start(f32[2,4]{1,0:T(2,128)} %param.26) | copy-start | bytes 100
  242.1 2.5 collective-permute-start
  244.6 0.6 copy-start.2

commit v12 on v11

--- a/solution.py
+++ b/solution.py
@@ -318,6 +318,8 @@
 
     @pl.when(step == 0)
     def _():
+        if not by_z:
+            load_w(0, 0).start()
         entry_barrier((small.peers() + [(s, here()[1]) for s in zg.side]) if fetch_x else zg.peers())
         if fetch_x:
             small.start()
@@ -331,8 +333,6 @@
         if by_z:
             for v in load_own():
                 v.start()
-        else:
-            load_w(0, 0).start()
         cp = pltpu.make_async_copy(gs.at[:, pl.ds(layer * SMALL, SMALL)], sm, wsem.at[2])
         cp.start()
         cp.wait()
@@ -617,7 +617,7 @@
         (ax, o_ref, f_ref, gx), refs = refs[:4], refs[4:]
     else:
         (o_ref, r_ref), refs = refs[:2], refs[2:]
-    (wzb, wob, s3, ubuf, send, recv), refs = refs[:6], refs[6:]
+    (wzb, wob, wof, wsem, s3, ubuf, send, recv), refs = refs[:8], refs[8:]
     i = pl.program_id(0)
     width = PC * n_tp
     if fetch_x:
@@ -650,11 +650,10 @@
 
     @pl.when(i == 0)
     def _():
+        pltpu.make_async_copy(wo_ref, wof, wsem).start()
         for d in range(n_dp):
             for t in range(n_tp):
-                a, b = slice(d * PC, (d + 1) * PC), slice(t * PC, (t + 1) * PC)
-                wzb[a, b] = wz_ref[d, t].astype(BF16)
-                wob[b, a] = wo_ref[d, t].astype(BF16)
+                wzb[d * PC:(d + 1) * PC, t * PC:(t + 1) * PC] = wz_ref[d, t].astype(BF16)
         a, b, c_ = split3(jnp.where(here()[3] == 1, s_ref[...], 0.0))
         for k, (v, w) in enumerate(((a, a), (b, b), (c_, a))):
             s3[k] = rows_cat(v, w)
@@ -675,6 +674,14 @@
         vs.append(v)
     sc = lax.rsqrt(ss / width + EPS)
     g = lanes_cat(*[(v * sc * sm_ref[t, 5:6, :]).astype(BF16) for t, v in enumerate(vs)])
+
+    @pl.when(i == 0)
+    def _():
+        pltpu.make_async_copy(wo_ref, wof, wsem).wait()
+        for d in range(n_dp):
+            for t in range(n_tp):
+                wob[t * PC:(t + 1) * PC, d * PC:(d + 1) * PC] = wof[d, t].astype(BF16)
+
     un = round_bf16(u + dot(g, wob[...]))
     if fetch_x:
         o_ref[...] = un.astype(BF16)
@@ -717,12 +724,13 @@
         name="p2", grid=(n // BLK2,),
         in_specs=[pl.BlockSpec((BLK2, d_model), lambda i: (base() + i, 0)),
                   fixed((2, d_model)),
-                  fixed((n_dp, n_tp, PC, PC)), fixed((n_dp, n_tp, PC, PC)),
+                  fixed((n_dp, n_tp, PC, PC)), hbm,
                   pl.BlockSpec((n_tp, SMALL, PC), lambda i: (0, layer, 0), pipeline_mode=pl.Buffered(1)),
                   rows(width), rows(NST), pl.BlockSpec((heads, BLK2), lambda i: (0, i)),
                   fixed((NST, width)), fixed((3 * heads, width))] + [hbm] * len(comm),
         out_specs=specs, out_shape=outs,
-        scratch_shapes=[vm((d_model, width), BF16), vm((width, d_model), BF16), vm((3, 2 * NST, width), BF16),
+        scratch_shapes=[vm((d_model, width), BF16), vm((width, d_model), BF16), vm((n_dp, n_tp, PC, PC), F32),
+                        pltpu.SemaphoreType.DMA, vm((3, 2 * NST, width), BF16),
                         vm((d_model // LANES * BLK2, LANES), F32)]
         + [pltpu.SemaphoreType.DMA((SEMS,))] * 2 + ([] if fetch_x else [vm((2, BLK2, d_model), F32)]),
         compiler_params=pltpu.CompilerParams(dimension_semantics=("arbitrary",), vmem_limit_bytes=VMEM_CAP,

time: 435 us -> 434 us (level)
  no operation moved by 1% of the time
where the time goes in v12:
time: 434 us; the launch traced here: 433 us
  Pallas kernels  415 us (96%)
  other arithmetic  11.7 us (3%)
  local copies, waits for them, and re-layouts  4.49 us (1%)
    pallas_call x2, Pallas kernels, p1(): pl.pallas_call(functools.partial(p1_body, geom=(n_dp, n_tp, heads, nb, nb...  264 us
    pallas_call x2, Pallas kernels, p2(): pl.pallas_call(functools.partial(p2_body, geom=(n_dp, n_tp, heads), mix_i...  138 us
    pallas_call x1, Pallas kernels, finish(): pl.pallas_call(finish_body, name='finish', grid=(2, ni), in_specs=[pl.Blo...  12.8 us
  transfers between devices with their start and end apart: 1, of which 1 were waited for; matrix products, arithmetic and copies ran while one was open for 0% of the time, Pallas kernels for 0%

profile of v12, /device:TPU:0, one launch (start us, length us, event | category | flops | bytes accessed | tf_op | source)
XLA Modules:
  0.0 433.5 jit_solution(9417416385030927600)
XLA Ops:
  0.0 0.0 copy-start
  0.0 0.0 copy-start.1
  0.0 0.7 negate_multiply_fusion
  0.7 0.7 bitcast_convert_fusion.1
  1.4 0.7 bitcast_convert_fusion
  2.1 0.7 broadcast_in_dim.15
  2.8 0.1 reshape.41
  2.9 0.7 convert_bitcast_fusion
  3.7 0.9 slice_bitcast_fusion
  4.6 0.1 copy.21
  4.7 2.7 convert_element_type.21.refs_7_.refs_10_
  7.4 2.7 convert_element_type.23.refs_9_.refs_10_
  10.1 2.8 convert_element_type.24.refs_10_.refs_11_
  12.9 0.6 select_bitcast_fusion.refs_1_
  13.5 0.1 broadcast_in_dim.32
  13.6 0.0 copy-done.1
  13.6 0.1 broadcast_in_dim.31
  13.7 0.0 copy-done
  13.7 1.9 concatenate.3
  15.5 150.6 %p1.2 = (f32[3072,2048]{1,0:T(8,128)}, f32[3072,128]{1,0:T(8,128)}, f32[32,3072]{1,0:T(8,128)}, f32[128,2048]{1,0:T(8,128)}, f32[4,8,256,256]{3,2,1,0:T(8,128)},...) custom-call(bf16[6144,1024]{1,0:T(8,128)(2,1)} %bitcast.20, ...), custom_call_target="tpu_custom_call" | custom-call | flops 215040000000 | bytes 36864000 | tf_op jit(solution)/shard_map/p1/pallas_call | solution.py:587
  166.1 75.9 %p2.2 = (bf16[3072,1024]{1,0:T(8,128)(2,1)}, f32[24,1024]{1,0:T(8,128)}, f32[4,8,256,256]{3,2,1,0:T(8,128)}) custom-call(bf16[6144,1024]{1,0:T(8,128)(2,1)} %bitcast.21, bf16[2,1024]{1,0:T(2,128)(2,1)} %refs_1_.3, f32[4,8,256,256]{3,2,1,0:T(8,128)} %get-tuple-element.23.refs_2_, f32[4,8,256,256]{3,2,1,0:T(8,128)} %get-tuple-element.24.refs_3_, ...), custom_call_target="tpu_custom_call" | custom-call | flops 92160000000 | bytes 36864000 | tf_op jit(solution)/shard_map/p2/pallas_call | solution.py:722
  242.1 1.5 collective-permute-start
  243.6 0.9 collective-permute-done.refs_1_
  244.5 0.0 copy-start.2
  244.5 0.6 copy-done.2
  245.1 113.1 %p1.3 = (f32[3072,2048]{1,0:T(8,128)}, f32[3072,128]{1,0:T(8,128)}, f32[32,3072]{1,0:T(8,128)}, f32[128,2048]{1,0:T(8,128)}, f32[4,8,256,256]{3,2,1,0:T(8,128)}, /*index=5*/f32[4,8,256,256]{3,2,1,0:T(8,128)}) custom-call(bf16[3072,1024]{1,0:T(8,128)(2,1)} %get-tuple-element.30.refs_0_, f32[24,1024]{1,0:T(8,128)} %copy-done.2, bf16[2,1024]{1,0:T(2,128)(2,1)} %refs_1_.3, ...), custom_call_target="tpu_custom_call" | custom-call | flops 215040000000 | bytes 36864000 | tf_op jit(solution)/shard_map/p1/pallas_call | solution.py:587
  358.2 62.4 %p2.3 = (bf16[3072,1024]{1,0:T(8,128)(2,1)}, f32[3072,1024]{1,0:T(8,128)}) custom-call(bf16[3072,1024]{1,0:T(8,128)(2,1)} %get-tuple-element.30.refs_0_, bf16[2,1024]{1,0:T(2,128)(2,1)} %refs_1_.3, f32[4,8,256,256]{3,2,1,0:T(8,128)} %get-tuple-element.33.refs_2_, f32[4,8,256,256]{3,2,1,0:T(8,128)} %get-tuple-element.34.refs_3_, ...), custom_call_target="tpu_custom_call" | custom-call | flops 92160000000 | bytes 36864000 | tf_op jit(solution)/shard_map/p2/pallas_call | solution.py:722
  420.7 12.8 %finish.1 = bf16[6144,1024]{1,0:T(8,128)(2,1)} custom-call(bf16[3072,1024]{1,0:T(8,128)(2,1)} %get-tuple-element.39.own_ref, f32[3072,1024]{1,0:T(8,128)} %get-tuple-element.40.other_ref), custom_call_target="tpu_custom_call" | custom-call | flops 3145728 | bytes 25165824 | tf_op jit(solution)/shard_map/finish/pallas_call | solution.py:759
  (4 shorter events, 0.0 us)
Async XLA Ops:
  0.0 13.7 %copy-start = (bf16[2,4,256]{2,1,0:T(4,128)(2,1)S(1)}, bf16[2,4,256]{2,1,0:T(4,128)(2,1)}, u32[]{:S(2)}) copy-start(bf16[2,4,256]{2,1,0:T(4,128)(2,1)} %param.22) | copy-start | bytes 12292
  0.0 13.6 %copy-start.1 = (f32[2,4]{1,0:T(2,128)S(1)}, f32[2,4]{1,0:T(2,128)}, u32[]{:S(2)}) copy-start(f32[2,4]{1,0:T(2,128)} %param.26) | copy-start | bytes 100
  242.1 2.4 collective-permute-start
  244.5 0.6 copy-start.2
